TPU v7x, 32 devices: a whole 2x2x4 slice. The times are simulated.
32 devices in a mesh: sx: 8 (over y, x, core), sy: 4 (over z).
Axes of the slice: x: 2, y: 2, z: 4, core: 2. Of those that a mesh axis runs over, the one named last changes fastest.
Arguments:
- vectors: bfloat16 [64, 64, 128, 128], P(None, 'sx', 'sy'), may hold values from -0.4453125 to 0.4453125
- root_stiff: float32 [64, 128, 128], P('sx', 'sy'), may hold values from 0.5 to 2
- diag_coef: float32 [64, 128, 128], P('sx', 'sy'), may hold values from -3 to 3
- counts: int32 [8, 4], P('sx', 'sy'), may hold values from 8 to 64, as said below
Outputs:
- own_block: float32 [8, 4, 64, 64], P('sx', 'sy')
- face_blocks: float32 [8, 4, 64, 256], P('sx', 'sy')
- corner_blocks: float32 [8, 4, 64, 256], P('sx', 'sy')
- offsets: int32 [8, 4], P('sx', 'sy')
Inputs may be any that keep to these rules, and one draw needn't show every extreme that they name: Some subdomain has exactly 64 eigenvectors in every draw; small counts are more common than large ones.
All inputs are finite; a program needn't handle non-finite values.
Results may differ from a plain program's by a relative error of at most 0.007.
Values may be sent and summed in bfloat16 or wider, within the bound.
No kernel may reach another device: no remote copies, remote signals or barrier semaphores. Data moves between devices by JAX's collectives and lax.ppermute only.
A program may use at most 128 MiB of HBM per device.

v0:
```python
import jax
import jax.numpy as jnp
from jax import lax
from jax.sharding import PartitionSpec as P


def extended(cells, sides, width):
    for axis, dim in sides:
        count = lax.axis_size(axis)
        ends = count - 1
        head = lax.slice_in_dim(cells, 0, width, axis=dim)
        tail = lax.slice_in_dim(cells, cells.shape[dim] - width, cells.shape[dim], axis=dim)
        cells = jnp.concatenate(
            [
                lax.ppermute(tail, axis, [(i, (i + 1) % count) for i in range(ends)]),
                cells,
                lax.ppermute(head, axis, [((i + 1) % count, i) for i in range(ends)]),
            ],
            axis=dim,
        )
    return cells


def smooth_along(values, dim_index):
    length = values.shape[dim_index]
    zero_slab = jnp.zeros_like(lax.slice_in_dim(values, 0, 1, axis=dim_index))
    below_side = jnp.concatenate(
        [zero_slab, lax.slice_in_dim(values, 0, length - 1, axis=dim_index)], axis=dim_index
    )
    above_side = jnp.concatenate(
        [lax.slice_in_dim(values, 1, length, axis=dim_index), zero_slab], axis=dim_index
    )
    return values + 0.5 * (below_side + above_side)


def own_term(masked, scaled, stiff_here, diag_here):
    scaled_wide = scaled.astype(jnp.float32)
    smoothed = smooth_along(smooth_along(smooth_along(scaled_wide, 1), 2), 3)
    beside = smoothed - scaled_wide
    applied = (diag_here[None] * masked.astype(jnp.float32) - stiff_here[None] * beside).astype(
        jnp.bfloat16
    )
    vec_rows = masked.shape[0]
    return lax.dot_general(
        masked.reshape(vec_rows, -1),
        applied.reshape(vec_rows, -1),
        (((1,), (1,)), ((), ())),
        preferred_element_type=jnp.float32,
    )


def face_term(own_layer, near_layer):
    weighted = 0.5 * smooth_along(smooth_along(near_layer.astype(jnp.float32), 1), 2)
    vec_rows = own_layer.shape[0]
    return -lax.dot_general(
        own_layer.astype(jnp.float32).reshape(vec_rows, -1),
        weighted.reshape(vec_rows, -1),
        (((1,), (1,)), ((), ())),
        precision=lax.Precision.HIGHEST,
        preferred_element_type=jnp.float32,
    )


def corner_term(own_column, near_column):
    weighted = 0.25 * smooth_along(near_column.astype(jnp.float32), 1)
    return -lax.dot_general(
        own_column.astype(jnp.float32),
        weighted,
        (((1,), (1,)), ((), ())),
        precision=lax.Precision.HIGHEST,
        preferred_element_type=jnp.float32,
    )


def on_device(vectors, root_stiff, diag_coef, counts):
    vec_rows = vectors.shape[0]
    live_count = counts[0, 0]
    row_index = lax.broadcasted_iota(jnp.int32, (vec_rows, 1, 1, 1), 0)
    masked = jnp.where(row_index < live_count, vectors, jnp.zeros_like(vectors))
    scaled = (root_stiff[None] * masked.astype(jnp.float32)).astype(jnp.bfloat16)
    padded = extended(scaled, (("sx", 1), ("sy", 2)), 1)
    own_block = own_term(masked, scaled, root_stiff, diag_coef)
    faces = [
        face_term(scaled[:, 0], padded[:, 0, 1:-1]),
        face_term(scaled[:, -1], padded[:, -1, 1:-1]),
        face_term(scaled[:, :, 0], padded[:, 1:-1, 0]),
        face_term(scaled[:, :, -1], padded[:, 1:-1, -1]),
    ]
    corners = [
        corner_term(scaled[:, 0, 0], padded[:, 0, 0]),
        corner_term(scaled[:, 0, -1], padded[:, 0, -1]),
        corner_term(scaled[:, -1, 0], padded[:, -1, 0]),
        corner_term(scaled[:, -1, -1], padded[:, -1, -1]),
    ]
    every_count = lax.all_gather(counts, "sy", axis=1, tiled=True)
    my_place = lax.axis_index("sy")
    order = lax.broadcasted_iota(jnp.int32, every_count.shape, 1)
    offsets = jnp.sum(
        jnp.where(order < my_place, every_count, jnp.zeros_like(every_count))
    ).reshape(1, 1)
    return (
        own_block[None, None],
        jnp.concatenate(faces, axis=1)[None, None],
        jnp.concatenate(corners, axis=1)[None, None],
        offsets,
    )


def solution(mesh):
    return jax.shard_map(
        on_device,
        mesh=mesh,
        in_specs=(
            P(None, "sx", "sy", None),
            P("sx", "sy", None),
            P("sx", "sy", None),
            P("sx", "sy"),
        ),
        out_specs=(
            P("sx", "sy", None, None),
            P("sx", "sy", None, None),
            P("sx", "sy", None, None),
            P("sx", "sy"),
        ),
        check_vma=False,
    )
```

profile of v0, /device:TPU:12, one launch (start us, length us, event | category | flops | bytes accessed | tf_op | source)
XLA Modules:
  0.0 110.7 jit_solution(2636912736025117690)
XLA Ops:
  1.3 8.9 %fusion.2 = (bf16[64,8,32,128]{3,0,2,1:T(8,128)(2,1)S(1)}, f32[64,8,32,128]{3,0,2,1:T(8,128)}) fusion(f32[8,32,128]{2,1,0:T(8,128)} %param.5, bf16[64,8,32,128]{3,2,1,0:T(8,128)(2,1)} %param.4, pred[64]{0:T(512)(128)(4,1)S(1)} %iota_compare_fusion), kind=kLoop, calls=%fused_computation.4 | loop fusion | flops 10485760 | bytes 16908352 | tf_op jit(solution)/shard_map/convert_element_type | solution.py:80
  10.2 2.0 %copy-done.1 = bf16[64,8,32,128]{3,0,2,1:T(8,128)(2,1)} copy-done((bf16[64,8,32,128]{3,0,2,1:T(8,128)(2,1)}, bf16[64,8,32,128]{3,0,2,1:T(8,128)(2,1)S(1)}, u32[]{:S(2)}) %copy-start.1) | copy-done | bytes 4194328
  12.2 0.1 fusion.92
  12.2 1.9 %collective-permute-start = (bf16[64,1,32,128]{3,0,2,1:T(8,128)(2,1)S(1)}, bf16[64,1,32,128]{3,0,2,1:T(8,128)(2,1)S(1)}, u32[]{:S(2)}, u32[]{:S(2)}) collective-permute-start(bf16[64,1,32,128]{3,0,2,1:T(8,128)(2,1)S(1)} %get-tuple-element.16), channel_id=1, source_target_pairs={{0,4},{4,8},{8,12},{12,16},{16,20},{20,24},{24,28},{1,5},{5,9},{9,... | collective-permute-start | bytes 1572872 | tf_op jit(solution)/shard_map/ppermute | solution.py:15
  14.2 4.5 %collective-permute-start.1 = (bf16[64,1,32,128]{3,0,2,1:T(8,128)(2,1)S(1)}, bf16[64,1,32,128]{3,0,2,1:T(8,128)(2,1)S(1)}, u32[]{:S(2)}, u32[]{:S(2)}) collective-permute-start(bf16[64,1,32,128]{3,0,2,1:T(8,128)(2,1)S(1)} %get-tuple-element.17), channel_id=1, source_target_pairs={{4,0},{8,4},{12,8},{16,12},{20,16},{24,20},{28,24},{5,1},{9,5},{13... | collective-permute-start | bytes 1572872 | tf_op jit(solution)/shard_map/ppermute | solution.py:17
  18.7 0.0 copy-start.2
  18.7 13.6 %fusion.90 = (f32[64,7,32,128]{3,0,2,1:T(8,128)}, f32[64,7,32,128]{3,0,2,1:T(8,128)}) fusion(f32[64,8,32,128]{3,0,2,1:T(8,128)} %get-tuple-element.13), kind=kLoop, calls=%fused_computation.123 | loop fusion | bytes 29360128 | tf_op jit(solution)/shard_map/slice | solution.py:28
  32.4 8.5 %multiply_add_fusion.1 = f32[64,8,32,128]{3,0,2,1:T(8,128)S(1)} fusion(f32[64,7,32,128]{3,0,2,1:T(8,128)} %get-tuple-element.9, f32[64,7,32,128]{3,0,2,1:T(8,128)} %get-tuple-element.8, bf16[64,8,32,128]{3,2,1,0:T(8,128)(2,1)} %param.4, pred[64]{0:T(512)(128)(4,1)S(1)} %iota_compare_fusion, f32[8,32,128]{2,1,0:T(8,128)S(1)} %copy-done.2), kind=kLoop, calls=%fused_computation.6 | loop fusion | flops 16777216 | bytes 27394112 | tf_op jit(solution)/shard_map/add | solution.py:33
  40.9 6.6 %fusion.89 = (f32[64,8,31,128]{3,0,2,1:T(8,128)}, f32[64,8,31,128]{3,0,2,1:T(8,128)}) fusion(f32[64,8,32,128]{3,0,2,1:T(8,128)S(1)} %multiply_add_fusion.1), kind=kLoop, calls=%fused_computation.122 | loop fusion | bytes 32505856 | tf_op jit(solution)/shard_map/slice | solution.py:28
  47.5 7.2 %multiply_add_fusion = f32[64,8,32,128]{3,0,2,1:T(8,128)S(1)} fusion(f32[64,8,32,128]{3,0,2,1:T(8,128)S(1)} %multiply_add_fusion.1, f32[64,8,31,128]{3,0,2,1:T(8,128)} %get-tuple-element.7, f32[64,8,31,128]{3,0,2,1:T(8,128)} %get-tuple-element.6), kind=kLoop, calls=%fused_computation.5 | loop fusion | flops 6291456 | bytes 33030144 | tf_op jit(solution)/shard_map/add | solution.py:33
  54.7 3.2 %copy-done = f32[64,8,32,128]{3,0,2,1:T(8,128)} copy-done((f32[64,8,32,128]{3,0,2,1:T(8,128)}, f32[64,8,32,128]{3,0,2,1:T(8,128)S(1)}, u32[]{:S(2)}) %copy-start) | copy-done | bytes 8388632
  58.0 7.3 %fusion.88 = (f32[64,8,32,127]{3,0,2,1:T(8,128)}, f32[64,8,32,127]{3,0,2,1:T(8,128)}) fusion(f32[64,8,32,128]{3,0,2,1:T(8,128)S(1)} %multiply_add_fusion), kind=kLoop, calls=%fused_computation.121 | loop fusion | bytes 33292288 | tf_op jit(solution)/shard_map/slice | solution.py:28
  65.3 0.6 dynamic-slice
  65.9 0.9 bitcast_dynamic-update-slice_fusion
  66.7 15.0 %fusion.9 = f32[1,1,64,64]{3,2,1,0:T(8,128)} fusion(f32[64,8,32,128]{3,0,2,1:T(8,128)} %copy-done, f32[64,8,32,127]{3,0,2,1:T(8,128)} %get-tuple-element.5, f32[64,8,32,127]{3,0,2,1:T(8,128)} %get-tuple-element.4, f32[8,32,128]{2,1,0:T(8,128)S(1)} %copy-done.2, f32[8,32,128]{2,1,0:T(8,128)S(1)} %copy-done.3, bf16[64,8,32,128]{3,2,1,0:T(8,128)(2,1)} %param.4, ...), kind=kOutput, calls=%fused_computation.15 | convolution fusion | flops 297795584 | bytes 29507648 | tf_op jit(solution)/shard_map/dot_general | solution.py:44
  81.8 8.5 %all-reduce.30 = s32[4]{0:T(128)S(1)} all-reduce(s32[4]{0:T(128)S(1)} %bitcast_dynamic-update-slice_fusion), channel_id=1, replica_groups=mesh['sx'=8,'sy'=4] {'sy'}, use_global_device_ids=true, to_apply=%add.30 | all-reduce | flops 4 | bytes 32
  90.2 0.3 copy.24
  90.6 0.3 copy.22
  90.9 1.0 fusion.91
  91.9 0.1 copy.26
  92.0 0.1 copy.28
  92.1 0.6 fusion.70
  92.8 0.0 collective-permute-done
  92.8 1.0 pad_maximum_fusion.2
  93.8 1.9 %collective-permute-start.2 = (bf16[64,10,1,128]{3,0,2,1:T(8,128)(2,1)S(1)}, bf16[64,10,1,128]{3,0,2,1:T(8,128)(2,1)S(1)}, u32[]{:S(2)}, u32[]{:S(2)}) collective-permute-start(bf16[64,10,1,128]{3,0,2,1:T(8,128)(2,1)S(1)} %get-tuple-element.10), channel_id=1, source_target_pairs={{0,1},{1,2},{2,3},{4,5},{5,6},{6,7},{8,9},{9,10},{10,11},{12,13},{... | collective-permute-start | bytes 491528 | tf_op jit(solution)/shard_map/ppermute | solution.py:15
  95.7 3.9 %collective-permute-start.3 = (bf16[64,10,1,128]{3,0,2,1:T(8,128)(2,1)S(1)}, bf16[64,10,1,128]{3,0,2,1:T(8,128)(2,1)S(1)}, u32[]{:S(2)}, u32[]{:S(2)}) collective-permute-start(bf16[64,10,1,128]{3,0,2,1:T(8,128)(2,1)S(1)} %get-tuple-element.11), channel_id=1, source_target_pairs={{1,0},{2,1},{3,2},{5,4},{6,5},{7,6},{9,8},{10,9},{11,10},{13,12},{... | collective-permute-start | bytes 491528 | tf_op jit(solution)/shard_map/ppermute | solution.py:17
  99.6 0.1 bitcast_convert_fusion
  99.8 0.2 fusion.96
  100.0 0.1 bitcast_convert_fusion.1
  100.1 0.2 fusion.94
  100.4 0.3 multiply_add_fusion.3
  100.7 0.4 fusion.93
  101.1 0.3 multiply_add_fusion.2
  101.4 0.4 fusion.95
  101.8 1.0 convolution_negate_fusion.1
  102.8 1.0 convolution_negate_fusion
  104.1 0.1 fusion.97
  104.3 0.1 fusion.99
  104.4 0.1 fusion.101
  104.5 0.1 fusion.102
  104.6 0.4 convolution_negate_fusion.7
  105.0 0.4 convolution_negate_fusion.6
  105.4 1.0 convolution_negate_fusion.5
  106.4 1.0 convolution_negate_fusion.3
  107.3 1.0 convolution_negate_fusion.4
  108.3 1.0 convolution_negate_fusion.2
  109.3 0.7 maximum_bitcast_fusion.1
  110.0 0.7 maximum_bitcast_fusion
  (20 shorter events, 0.3 us)
Async XLA Ops:
  10.2 2.0 %copy-start.1 = (bf16[64,8,32,128]{3,0,2,1:T(8,128)(2,1)}, bf16[64,8,32,128]{3,0,2,1:T(8,128)(2,1)S(1)}, u32[]{:S(2)}) copy-start(bf16[64,8,32,128]{3,0,2,1:T(8,128)(2,1)S(1)} %get-tuple-element.12) | copy-start | bytes 12582916
  12.2 80.5 %collective-permute-start = (bf16[64,1,32,128]{3,0,2,1:T(8,128)(2,1)S(1)}, bf16[64,1,32,128]{3,0,2,1:T(8,128)(2,1)S(1)}, u32[]{:S(2)}, u32[]{:S(2)}) collective-permute-start(bf16[64,1,32,128]{3,0,2,1:T(8,128)(2,1)S(1)} %get-tuple-element.16), channel_id=1, source_target_pairs={{0,4},{4,8},{8,12},{12,16},{16,20},{20,24},{24,28},{1,5},{5,9},{9,... | collective-permute-start | bytes 1572872 | tf_op jit(solution)/shard_map/ppermute | solution.py:15
  14.2 78.6 %collective-permute-start.1 = (bf16[64,1,32,128]{3,0,2,1:T(8,128)(2,1)S(1)}, bf16[64,1,32,128]{3,0,2,1:T(8,128)(2,1)S(1)}, u32[]{:S(2)}, u32[]{:S(2)}) collective-permute-start(bf16[64,1,32,128]{3,0,2,1:T(8,128)(2,1)S(1)} %get-tuple-element.17), channel_id=1, source_target_pairs={{4,0},{8,4},{12,8},{16,12},{20,16},{24,20},{28,24},{5,1},{9,5},{13... | collective-permute-start | bytes 1572872 | tf_op jit(solution)/shard_map/ppermute | solution.py:17
  18.7 13.7 %copy-start.2 = (f32[8,32,128]{2,1,0:T(8,128)S(1)}, f32[8,32,128]{2,1,0:T(8,128)}, u32[]{:S(2)}) copy-start(f32[8,32,128]{2,1,0:T(8,128)} %param.5) | copy-start | bytes 393220
  54.7 3.3 %copy-start = (f32[64,8,32,128]{3,0,2,1:T(8,128)}, f32[64,8,32,128]{3,0,2,1:T(8,128)S(1)}, u32[]{:S(2)}) copy-start(f32[64,8,32,128]{3,0,2,1:T(8,128)S(1)} %multiply_add_fusion) | copy-start | bytes 25165828
  58.0 7.3 %copy-start.4 = (u32[32]{0:T(128)S(1)}, u32[32]{0:T(128)}, u32[]{:S(2)}) copy-start(u32[32]{0:T(128)} %constant.87) | copy-start | bytes 388
  58.0 8.8 %copy-start.3 = (f32[8,32,128]{2,1,0:T(8,128)S(1)}, f32[8,32,128]{2,1,0:T(8,128)}, u32[]{:S(2)}) copy-start(f32[8,32,128]{2,1,0:T(8,128)} %param.6) | copy-start | bytes 393220
  93.8 10.2 %collective-permute-start.2 = (bf16[64,10,1,128]{3,0,2,1:T(8,128)(2,1)S(1)}, bf16[64,10,1,128]{3,0,2,1:T(8,128)(2,1)S(1)}, u32[]{:S(2)}, u32[]{:S(2)}) collective-permute-start(bf16[64,10,1,128]{3,0,2,1:T(8,128)(2,1)S(1)} %get-tuple-element.10), channel_id=1, source_target_pairs={{0,1},{1,2},{2,3},{4,5},{5,6},{6,7},{8,9},{9,10},{10,11},{12,13},{... | collective-permute-start | bytes 491528 | tf_op jit(solution)/shard_map/ppermute | solution.py:15
  95.7 8.2 %collective-permute-start.3 = (bf16[64,10,1,128]{3,0,2,1:T(8,128)(2,1)S(1)}, bf16[64,10,1,128]{3,0,2,1:T(8,128)(2,1)S(1)}, u32[]{:S(2)}, u32[]{:S(2)}) collective-permute-start(bf16[64,10,1,128]{3,0,2,1:T(8,128)(2,1)S(1)} %get-tuple-element.11), channel_id=1, source_target_pairs={{1,0},{2,1},{3,2},{5,4},{6,5},{7,6},{9,8},{10,9},{11,10},{13,12},{... | collective-permute-start | bytes 491528 | tf_op jit(solution)/shard_map/ppermute | solution.py:17
where the time goes:
time: 112 us; the launch traced here: 111 us
  local copies, waits for them, and re-layouts  37.9 us (34%)
  other arithmetic  28.7 us (26%)
  matrix products  21.7 us (19%)
  starting transfers between devices  12.3 us (11%)
  blocking collectives  8.45 us (8%)
  between operations  1.63 us (1%)
    slice x13, local copies, waits for them, and re-layouts, smooth_along(): lax.slice_in_dim(values, 0, length - 1, axis=dim_index)  29.3 us
    add x6, other arithmetic, smooth_along(): return values + 0.5 * (below_side + above_side)  16.4 us
    dot_general x1, matrix products, own_term(): lax.dot_general(masked.reshape(vec_rows, -1), applied.reshape(vec_rows, -...  15 us
    convert_element_type x1, other arithmetic, on_device(): (root_stiff[None] * masked.astype(jnp.float32)).astype(jnp.bfloat16)  8.91 us
    ppermute x2, starting transfers between devices, extended(): lax.ppermute(head, axis, [((i + 1) % count, i) for i in range(ends)])  8.47 us
    unnamed x1, blocking collectives  8.45 us
    unnamed x13, local copies, waits for them, and re-layouts  6.67 us
    dot_general x4, matrix products, corner_term(): lax.dot_general(own_column.astype(jnp.float32), weighted, (((1,), (1,)),...  3.84 us
  transfers between devices with their start and end apart: 4, of which 0 were waited for; matrix products, arithmetic and copies ran while one was open for 60% of the time, Pallas kernels for 0%

commit v1 on v0

v1 whole, which is shorter than its diff:
```python
import jax
import jax.numpy as jnp
from jax import lax
from jax.experimental import pallas as pl
from jax.experimental.pallas import tpu as pltpu
from jax.sharding import PartitionSpec as P

F32 = jnp.float32
BF = jnp.bfloat16
NT = (((1,), (1,)), ((), ()))
NN = (((1,), (0,)), ((), ()))
PAD = 4
VM = pl.BlockSpec(memory_space=pltpu.VMEM)
SM = pl.BlockSpec(memory_space=pltpu.SMEM)
ANY = pl.BlockSpec(memory_space=pl.ANY)


def cost(flops, bytes_accessed):
    return pl.CostEstimate(flops=flops, bytes_accessed=bytes_accessed, transcendentals=0)


def tri(n, reps, scale):
    size = n * reps
    i = lax.broadcasted_iota(jnp.int32, (size, size), 0)
    j = lax.broadcasted_iota(jnp.int32, (size, size), 1)
    near = ((i // n) == (j // n)) & (jnp.abs(i - j) == 1)
    return (jnp.where(i == j, 1.0, jnp.where(near, 0.5, 0.0)) * scale).astype(BF)


def even(axis):
    return lax.rem(lax.axis_index(axis), 2) == 0


def pairs(count, first):
    steps = []
    for i in range(first, count - 1, 2):
        steps += [(i, i + 1), (i + 1, i)]
    return steps


def edge_kernel(cnt, v, s, fxa, fxb, fxc, fya, fyb, xbuf, ybuf, rx, ry, xsem, ysem):
    _, rows, ny, nz = xbuf.shape
    nx, band = ybuf.shape[2], ybuf.shape[3]
    stx, sty = ny + PAD, band + PAD
    x_even, y_even = even("sx"), even("sy")
    xa = jnp.where(x_even, nx - 1, 0)
    xb = nx - 1 - xa
    ya = jnp.where(y_even, ny - band, 0)
    yb = ny - band - ya
    xcopies = [pltpu.make_async_copy(v.at[:, x], xbuf.at[i], xsem.at[i]) for i, x in enumerate((xb, xa))]
    ycopies = [
        pltpu.make_async_copy(v.at[:, :, pl.ds(pl.multiple_of(y, band), band)], ybuf.at[i], ysem.at[i])
        for i, y in enumerate((ya, yb))
    ]
    for c in xcopies + ycopies:
        c.start()
    live = lax.broadcasted_iota(jnp.int32, (rows, nz), 0) < cnt[0, 0]

    def scaled(m, stiff):
        return jnp.where(live, m * jnp.broadcast_to(stiff, (rows, nz)), 0.0).astype(BF)

    for i, (x, out) in enumerate(((xb, fxb), (xa, fxa))):
        xcopies[i].wait()
        for a in range(rows):
            rx[a * stx : a * stx + ny, :] = xbuf[i, a].astype(F32)
        for y in range(ny):
            out[y] = scaled(rx[pl.ds(y, rows, stride=stx), :], s[x, pl.ds(y, 1), :])
        if i == 0:
            fxc[0] = fxb[jnp.where(y_even, ny - 1, 0)]
            fxc[1] = fxb[jnp.where(y_even, 0, ny - 1)]
    for i, (y0, out) in enumerate(((ya, fya), (yb, fyb))):
        ycopies[i].wait()
        inner = jnp.where(y0 == 0, 0, band - 1)
        for x in range(nx):
            for a in range(rows):
                ry[x, a * sty : a * sty + band, :] = ybuf[i, a, x].astype(F32)
            out[x] = scaled(ry[x, pl.ds(inner, rows, stride=sty), :], s[x, pl.ds(y0 + inner, 1), :])


def edges(counts, vectors, stiff):
    rows, nx, ny, nz = vectors.shape
    band = 16
    face = lambda *dims: jax.ShapeDtypeStruct((*dims, rows, nz), BF)
    return pl.pallas_call(
        edge_kernel,
        out_shape=(face(ny), face(ny), face(2), face(nx), face(nx)),
        in_specs=[SM, ANY, VM],
        out_specs=(VM,) * 5,
        scratch_shapes=[
            pltpu.VMEM((2, rows, ny, nz), BF),
            pltpu.VMEM((2, rows, nx, band, nz), BF),
            pltpu.VMEM((rows * (ny + PAD), nz), F32),
            pltpu.VMEM((nx, rows * (band + PAD), nz), F32),
            pltpu.SemaphoreType.DMA((2,)),
            pltpu.SemaphoreType.DMA((2,)),
        ],
        cost_estimate=cost(10**6, 4 * 10**6),
        name="edges",
    )(counts, vectors, stiff)


def pack_kernel(known, fya, fyb, rxa, rxc, mya, myb, sem):
    nx, rows, nz = fya.shape
    ny = rxa.shape[0]
    y_even = even("sy")
    hi = jnp.where(y_even, ny - 1, 0)
    copies = [
        pltpu.make_async_copy(rxa.at[y], out.at[nx], sem.at[i])
        for i, (y, out) in enumerate(((hi, mya), (ny - 1 - hi, myb)))
    ]
    for c in copies:
        c.start()
    lane = lax.broadcasted_iota(jnp.int32, (rows, nz), 1)
    counts = jnp.zeros((rows, nz), F32)
    for i in range(known.shape[1]):
        counts = jnp.where(lane == i, known[0, i].astype(F32), counts)
    for i, (src, out) in enumerate(((fya, mya), (fyb, myb))):
        out[0:nx] = src[...]
        out[nx + 1] = rxc[i]
        out[nx + 2] = counts.astype(BF)
    for c in copies:
        c.wait()


def pack(known, fya, fyb, rxa, rxc):
    nx, rows, nz = fya.shape
    out = jax.ShapeDtypeStruct((nx + 3, rows, nz), BF)
    return pl.pallas_call(
        pack_kernel,
        out_shape=(out, out),
        in_specs=[SM, VM, VM, ANY, VM],
        out_specs=(VM, VM),
        scratch_shapes=[pltpu.SemaphoreType.DMA((2,))],
        cost_estimate=cost(10**5, 10**6),
        name="pack",
    )(known, fya, fyb, rxa, rxc)


def own_kernel(cnt, v, s, d, fxa, fxb, fya, fyb, own, wxa, wxb, wya, wyb, wc, vbuf, r, er, ubuf, pbuf, szr, acc, sem):
    nx, rows, ny, nz = vbuf.shape
    st = ny + PAD

    def copy(x):
        return pltpu.make_async_copy(v.at[:, x], vbuf.at[x], sem.at[x])

    for x in range(nx):
        copy(x).start()
    er[...] = d[...] + s[...] * s[...]
    ubuf[...] = jnp.zeros_like(ubuf)
    acc[...] = jnp.zeros_like(acc)
    szr[...] = tri(nz, 2, -0.25)

    def along_z(stack, n):
        wide = jnp.concatenate([jnp.concatenate([stack(2 * c), stack(2 * c + 1)], 1) for c in range(n // 2)], 0)
        z = lax.dot_general(wide, szr[...], NN, preferred_element_type=F32)
        return [z[(i // 2) * rows : (i // 2 + 1) * rows, (i % 2) * nz : (i % 2 + 1) * nz] for i in range(n)]

    def smooth_part(total):
        zs = along_z(lambda y: pbuf[y], ny)
        for c in range(ny // 2):
            left = jnp.concatenate([zs[2 * c].astype(BF), zs[2 * c + 1].astype(BF)], 1)
            right = jnp.concatenate([pbuf[2 * c], pbuf[2 * c + 1]], 1)
            total += lax.dot_general(left, right, NT, preferred_element_type=F32)
        last = lax.dot_general(pbuf[ny], szr[0:nz, 0:nz], NN, preferred_element_type=F32).astype(BF)
        return total + lax.dot_general(last, pbuf[ny], NT, preferred_element_type=F32)

    @pl.loop(0, nx)
    def _(x):
        copy(x).wait()
        for a in range(rows):
            r[a * st : a * st + ny, :] = vbuf[x, a].astype(F32)
        total = acc[...]
        last = None
        left, right = [], []
        for y in range(ny):
            m = r[pl.ds(y, rows, stride=st), :]
            stiff = jnp.broadcast_to(s[x, pl.ds(y, 1), :], (rows, nz))
            centre = jnp.broadcast_to(er[x, pl.ds(y, 1), :], (rows, nz))
            u = (m * stiff).astype(BF)
            left.append((m * centre).astype(BF))
            right.append(m.astype(BF))
            both = u + ubuf[y]
            ubuf[y] = u
            pbuf[y] = both if last is None else both + last
            last = both
            if y % 2:
                total += lax.dot_general(
                    jnp.concatenate(left, 1), jnp.concatenate(right, 1), NT, preferred_element_type=F32
                )
                left, right = [], []
        pbuf[ny] = last
        acc[...] = smooth_part(total)

    last = None
    for y in range(ny):
        both = ubuf[y]
        pbuf[y] = both if last is None else both + last
        last = both
    pbuf[ny] = last
    total = smooth_part(acc[...])
    live = cnt[0, 0]
    keep = (lax.broadcasted_iota(jnp.int32, (rows, rows), 0) < live) & (
        lax.broadcasted_iota(jnp.int32, (rows, rows), 1) < live
    )
    own[...] = jnp.where(keep, total, 0.0)

    for src, out in ((fxa, wxa), (fxb, wxb), (fya, wya), (fyb, wyb)):
        n = src.shape[0]
        zs = along_z(lambda i: src[i], n)
        for i in range(n):
            t = zs[i] + zs[i]
            if i > 0:
                t = t + zs[i - 1]
            if i < n - 1:
                t = t + zs[i + 1]
            out[i] = t.astype(BF)
    y_even = even("sy")
    rows_y = (jnp.where(y_even, ny - 1, 0), jnp.where(y_even, 0, ny - 1))
    for i, src in enumerate((fxa, fxb)):
        zs = along_z(lambda k: src[rows_y[k]], 2)
        for k in range(2):
            wc[2 * i + k] = zs[k].astype(BF)


def own(counts, vectors, stiff, diag, fxa, fxb, fya, fyb):
    rows, nx, ny, nz = vectors.shape
    face = lambda n: jax.ShapeDtypeStruct((n, rows, nz), BF)
    return pl.pallas_call(
        own_kernel,
        out_shape=(jax.ShapeDtypeStruct((rows, rows), F32), face(ny), face(ny), face(nx), face(nx), face(4)),
        in_specs=[SM, ANY, VM, VM, VM, VM, VM, VM],
        out_specs=(VM,) * 6,
        scratch_shapes=[
            pltpu.VMEM((nx, rows, ny, nz), BF),
            pltpu.VMEM((rows * (ny + PAD), nz), F32),
            pltpu.VMEM((nx, ny, nz), F32),
            pltpu.VMEM((ny, rows, nz), BF),
            pltpu.VMEM((ny + 1, rows, nz), BF),
            pltpu.VMEM((2 * nz, 2 * nz), BF),
            pltpu.VMEM((rows, rows), F32),
            pltpu.SemaphoreType.DMA((nx,)),
        ],
        cost_estimate=cost(2 * 10**9, 8 * 10**6),
        name="own",
    )(counts, vectors, stiff, diag, fxa, fxb, fya, fyb)


def couple_kernel(masks, cnt, wxa, wxb, wya, wyb, wc, rxa, rxb, rya, ryb, known, faces, corners, offsets):
    nx, rows, nz = wya.shape
    x_even, y_even = even("sx"), even("sy")

    def gram(left, right, n):
        total = jnp.zeros((rows, rows), F32)
        for i in range(0, n, 2):
            total += lax.dot_general(
                jnp.concatenate([left[i], left[i + 1]], 1),
                jnp.concatenate([right[i], right[i + 1]], 1),
                NT,
                preferred_element_type=F32,
            )
        return total

    ya, yb = gram(wya, rya, nx), gram(wyb, ryb, nx)
    around = [
        [lax.dot_general(wc[2 * i + k], ry[nx + i], NT, preferred_element_type=F32) for k, ry in enumerate((rya, ryb))]
        for i in range(2)
    ]
    n = wxa.shape[0]
    xa, xb = gram(wxa, rxa, n), gram(wxb, rxb, n)
    parts = (
        jnp.where(x_even, xb, xa),
        jnp.where(x_even, xa, xb),
        jnp.where(y_even, yb, ya),
        jnp.where(y_even, ya, yb),
    )
    for i, part in enumerate(parts):
        faces[:, i * rows : (i + 1) * rows] = part
    for ix in range(2):
        for iy in range(2):
            options = [
                jnp.where(y_even == (iy == 1), around[k][0], around[k][1]) for k in range(2)
            ]
            i = 2 * ix + iy
            corners[:, i * rows : (i + 1) * rows] = jnp.where(x_even == (ix == 1), options[0], options[1])

    me = lax.axis_index("sy")
    total = jnp.int32(0)
    for i, mask in enumerate(masks):
        total += jnp.where((me ^ mask) < me, known[0, i], 0)
    lane = lax.broadcasted_iota(jnp.int32, (8, nz), 1)
    theirs = rya[nx + 2, 0:16].astype(F32)[0:8]
    picked = jnp.zeros((8, nz), F32)
    for i, mask in enumerate(masks):
        picked = jnp.where((lane == i) & ((me ^ (mask ^ 1)) < me), theirs, picked)
    offsets[...] = jnp.sum(picked[0:1], axis=1, keepdims=True).astype(jnp.int32) + total


def couple(masks, counts, ws, received, known):
    wxa = ws[0]
    rows, nz = wxa.shape[1:]
    block = jax.ShapeDtypeStruct((rows, 4 * rows), F32)
    return pl.pallas_call(
        lambda *refs: couple_kernel(masks, *refs),
        out_shape=(block, block, jax.ShapeDtypeStruct((1, 1), jnp.int32)),
        in_specs=[SM] + [VM] * 9 + [SM],
        out_specs=(VM, VM, VM),
        cost_estimate=cost(10**8, 3 * 10**6),
        name="couple",
    )(counts, *ws, *received, known)


def on_device(vectors, root_stiff, diag_coef, counts):
    n_x, n_y = lax.axis_size("sx"), lax.axis_size("sy")
    fxa, fxb, fxc, fya, fyb = edges(counts, vectors, root_stiff)
    rxc = lax.ppermute(fxc, "sx", pairs(n_x, 1))
    rxb = lax.ppermute(fxb, "sx", pairs(n_x, 1))
    rxa = lax.ppermute(fxa, "sx", pairs(n_x, 0))
    known, masks, bit = counts, [0], n_y // 2
    while bit >= 2:
        other = lax.ppermute(known, "sy", [(i, i ^ bit) for i in range(n_y)])
        known = jnp.concatenate([known, other], axis=1)
        masks += [m ^ bit for m in masks]
        bit //= 2
    mya, myb = pack(known, fya, fyb, rxa, rxc)
    rya = lax.ppermute(mya, "sy", pairs(n_y, 0))
    ryb = lax.ppermute(myb, "sy", pairs(n_y, 1))
    own_block, *ws = own(counts, vectors, root_stiff, diag_coef, fxa, fxb, fya, fyb)
    faces, corners, offsets = couple(tuple(masks), counts, ws, (rxa, rxb, rya, ryb), known)
    return own_block[None, None], faces[None, None], corners[None, None], offsets


def solution(mesh):
    assert mesh.shape["sy"] & (mesh.shape["sy"] - 1) == 0
    return jax.shard_map(
        on_device,
        mesh=mesh,
        in_specs=(
            P(None, "sx", "sy", None),
            P("sx", "sy", None),
            P("sx", "sy", None),
            P("sx", "sy"),
        ),
        out_specs=(
            P("sx", "sy", None, None),
            P("sx", "sy", None, None),
            P("sx", "sy", None, None),
            P("sx", "sy"),
        ),
        check_vma=False,
    )
```

time: 112 us -> 46.7 us (0.42)
  local copies, waits for them, and re-layouts: 37.9 us -> 1.66 us
  other arithmetic: 28.7 us -> 1.28 us
  matrix products: 21.7 us -> 0 us
  Pallas kernels: 0 us -> 20.5 us
  blocking collectives: 8.45 us -> 0 us
  waiting for transfers between devices: 0.01 us -> 7.52 us
  starting transfers between devices: 12.3 us -> 14 us
    slice x19 -> x0, local copies, waits for them, and re-layouts: 31.2 us -> none  [the longest x13 29.3 us: smooth_along(): lax.slice_in_dim(values, 0, length - 1, axis=dim_index)]
    dot_general x9 -> x0, matrix products: 21.7 us -> none  [the longest x1 15 us: own_term(): lax.dot_general(masked.reshape(vec_rows, -1), applied.reshape(vec_rows, -...]
    pallas_call x0 -> x4, Pallas kernels: none -> 20.5 us  [the longest x1 10.5 us: own(): pl.pallas_call(own_kernel, out_shape=(jax.ShapeDtypeStruct((rows, rows),...]
    add x6 -> x0, other arithmetic: 16.4 us -> none  [smooth_along(): return values + 0.5 * (below_side + above_side)]
    convert_element_type x7 -> x0, other arithmetic: 9.18 us -> none  [the longest x1 8.91 us: on_device(): (root_stiff[None] * masked.astype(jnp.float32)).astype(jnp.bfloat16)]
    unnamed x1 -> x0, blocking collectives: 8.45 us -> none
    ppermute x4 -> x6, waiting for transfers between devices: 0.01 us -> 7.52 us  [the longest x1 7.51 us: on_device(): rxc = lax.ppermute(fxc, 'sx', pairs(n_x, 1))]
    unnamed x13 -> x10, local copies, waits for them, and re-layouts: 6.67 us -> 1.66 us
  transfers between devices with their start and end apart: 4 -> 6, of which waited for: 0 -> 1; matrix products, arithmetic and copies ran while one was open for 60% -> 3% of each run, Pallas kernels for 0% -> 28%
where the time goes in v1:
time: 46.7 us; the launch traced here: 46.3 us
  Pallas kernels  20.5 us (44%)
  starting transfers between devices  14 us (30%)
  waiting for transfers between devices  7.52 us (16%)
  local copies, waits for them, and re-layouts  1.66 us (4%)
  between operations  1.4 us (3%)
  other arithmetic  1.28 us (3%)
    pallas_call x1, Pallas kernels, own(): pl.pallas_call(own_kernel, out_shape=(jax.ShapeDtypeStruct((rows, rows),...  10.5 us
    ppermute x1, waiting for transfers between devices, on_device(): rxc = lax.ppermute(fxc, 'sx', pairs(n_x, 1))  7.51 us
    ppermute x1, starting transfers between devices, on_device(): ryb = lax.ppermute(myb, 'sy', pairs(n_y, 1))  5.04 us
    pallas_call x1, Pallas kernels, edges(): pl.pallas_call(edge_kernel, out_shape=(face(ny), face(ny), face(2), face(...  4.56 us
    ppermute x1, starting transfers between devices, on_device(): rxb = lax.ppermute(fxb, 'sx', pairs(n_x, 1))  3.43 us
    pallas_call x1, Pallas kernels, couple(): pl.pallas_call(lambda *refs: couple_kernel(masks, *refs), out_shape=(bloc...  2.95 us
    ppermute x1, starting transfers between devices, on_device(): rxc = lax.ppermute(fxc, 'sx', pairs(n_x, 1))  2.74 us
    ppermute x1, starting transfers between devices, on_device(): other = lax.ppermute(known, 'sy', [(i, i ^ bit) for i in range(n_y)])  2.65 us
  transfers between devices with their start and end apart: 6, of which 1 were waited for; matrix products, arithmetic and copies ran while one was open for 3% of the time, Pallas kernels for 28%

profile of v1, /device:TPU:12, one launch (start us, length us, event | category | flops | bytes accessed | tf_op | source)
XLA Modules:
  0.0 46.3 jit_solution(12710773387051592763)
XLA Ops:
  1.3 4.6 %edges.1 = (bf16[32,64,128]{2,1,0:T(8,128)(2,1)}, bf16[32,64,128]{2,1,0:T(8,128)(2,1)}, bf16[2,64,128]{2,1,0:T(8,128)(2,1)}, bf16[8,64,128]{2,1,0:T(8,128)(2,1)}, bf16[8,64,128]{2,1,0:T(8,128)(2,1)}) custom-call(s32[1,1]{1,0:T(1,128)S(6)} %copy.8.cnt.refs_0_, bf16[64,8,32,128]{3,2,1,0:T(8,128)(2,1)} %v.3, f32[8,32,128]{2,1,0:T(8,128)} %s.3), custom_call_target="tpu_custom_call" | custom-call | flops 1000000 | bytes 4000000 | tf_op jit(solution)/shard_map/edges/pallas_call | solution.py:84
  5.8 0.1 collective-permute-start
  5.9 3.4 %collective-permute-start.1 = (bf16[32,64,128]{2,1,0:T(8,128)(2,1)}, bf16[32,64,128]{2,1,0:T(8,128)(2,1)S(1)}, u32[]{:S(2)}, u32[]{:S(2)}) collective-permute-start(bf16[32,64,128]{2,1,0:T(8,128)(2,1)} %get-tuple-element.21.fxb), channel_id=1, source_target_pairs={{4,8},{8,4},{12,16},{16,12},{20,24},{24,20},{5,9},{9,5},{13,17},{1... | collective-permute-start | bytes 1572872 | tf_op jit(solution)/shard_map/ppermute | solution.py:316
  9.4 2.7 %collective-permute-start.2 = (s32[1,1]{1,0:T(1,128)}, s32[1,1]{1,0:T(1,128)}, u32[]{:S(2)}, u32[]{:S(2)}) collective-permute-start(s32[1,1]{1,0:T(1,128)} %param.7), channel_id=1, source_target_pairs={{0,2},{1,3},{2,0},{3,1},{4,6},{5,7},{6,4},{7,5},{8,10},{9,11},{10,... | collective-permute-start | bytes 20 | tf_op jit(solution)/shard_map/ppermute | solution.py:320
  12.0 2.7 %collective-permute-start.3 = (bf16[2,64,128]{2,1,0:T(8,128)(2,1)}, bf16[2,64,128]{2,1,0:T(8,128)(2,1)S(1)}, u32[]{:S(2)}, u32[]{:S(2)}) collective-permute-start(bf16[2,64,128]{2,1,0:T(8,128)(2,1)} %get-tuple-element.30), channel_id=1, source_target_pairs={{4,8},{8,4},{12,16},{16,12},{20,24},{24,20},{5,9},{9,5},{13,17},{1... | collective-permute-start | bytes 98312 | tf_op jit(solution)/shard_map/ppermute | solution.py:315
  14.8 0.0 collective-permute-done.2
  14.8 1.3 %pad_add_fusion.known.refs_10_ = s32[1,2]{1,0:T(1,128)} fusion(s32[1,1]{1,0:T(1,128)} %collective-permute-done.2, s32[1,1]{1,0:T(1,128)S(6)} %copy.8.cnt.refs_0_), kind=kLoop, calls=%fused_computation | loop fusion | flops 2 | bytes 16 | tf_op jit(solution)/shard_map/concatenate | solution.py:321
  16.0 7.5 %collective-permute-done.3.rxc = bf16[2,64,128]{2,1,0:T(8,128)(2,1)S(1)} collective-permute-done((bf16[2,64,128]{2,1,0:T(8,128)(2,1)}, bf16[2,64,128]{2,1,0:T(8,128)(2,1)S(1)}, u32[]{:S(2)}, u32[]{:S(2)}) %collective-permute-start.3) | collective-permute-done | bytes 32800 | tf_op jit(solution)/shard_map/ppermute | solution.py:315
  23.6 0.0 copy-start.4
  23.6 0.0 collective-permute-done.rxa.refs_6_
  23.6 0.0 copy-start
  23.6 0.6 %copy-done.4 = bf16[2,64,128]{2,1,0:T(8,128)(2,1)} copy-done((bf16[2,64,128]{2,1,0:T(8,128)(2,1)}, bf16[2,64,128]{2,1,0:T(8,128)(2,1)S(1)}, u32[]{:S(2)}) %copy-start.4) | copy-done | bytes 32792
  24.2 0.2 copy-done
  24.4 2.5 %pack.1 = (bf16[11,64,128]{2,1,0:T(8,128)(2,1)}, bf16[11,64,128]{2,1,0:T(8,128)(2,1)}) custom-call(s32[1,2]{1,0:T(1,128)} %pad_add_fusion.known.refs_10_, bf16[8,64,128]{2,1,0:T(8,128)(2,1)} %get-tuple-element.22.fya, bf16[8,64,128]{2,1,0:T(8,128)(2,1)} %get-tuple-element.23.fyb, bf16[32,64,128]{2,1,0:T(8,128)(2,1)} %copy-done, bf16[2,64,128]{2,1,0:T(8,128)(2,1)} %copy-done.4), custom_call_target="tpu_custom_call" | custom-call | flops 100000 | bytes 1000000 | tf_op jit(solution)/shard_map/pack/pallas_call | solution.py:128
  26.9 0.1 collective-permute-start.4
  26.9 5.0 %collective-permute-start.5 = (bf16[11,64,128]{2,1,0:T(8,128)(2,1)}, bf16[11,64,128]{2,1,0:T(8,128)(2,1)S(1)}, u32[]{:S(2)}, u32[]{:S(2)}) collective-permute-start(bf16[11,64,128]{2,1,0:T(8,128)(2,1)} %get-tuple-element.32), channel_id=1, source_target_pairs={{1,2},{2,1},{5,6},{6,5},{9,10},{10,9},{13,14},{14,13},{17,18},{18,... | collective-permute-start | bytes 540680 | tf_op jit(solution)/shard_map/ppermute | solution.py:326
  32.0 10.5 %own.1 = (f32[64,64]{1,0:T(8,128)}, bf16[32,64,128]{2,1,0:T(8,128)(2,1)}, bf16[32,64,128]{2,1,0:T(8,128)(2,1)}, bf16[8,64,128]{2,1,0:T(8,128)(2,1)}, bf16[8,64,1...) custom-call(s32[1,1]{1,0:T(1,128)S(6)} %copy.8.cnt.refs_0_, bf16[64,8,32,128]{3,2,1,0:T(8,128)(2,1)} %v.3, f32[8,32,128]{2,1,0:T(8,128)} %s.3, ...), custom_call_target="tpu_custom_call" | custom-call | flops 2000000000 | bytes 8000000 | tf_op jit(solution)/shard_map/own/pallas_call | solution.py:228
  42.5 0.0 collective-permute-done.1.refs_7_
  42.5 0.0 copy-start.1
  42.5 0.0 collective-permute-done.4.refs_8_
  42.5 0.0 copy-start.2
  42.5 0.0 collective-permute-done.5.refs_9_
  42.5 0.0 copy-start.3
  42.5 0.7 %copy-done.1 = bf16[32,64,128]{2,1,0:T(8,128)(2,1)} copy-done((bf16[32,64,128]{2,1,0:T(8,128)(2,1)}, bf16[32,64,128]{2,1,0:T(8,128)(2,1)S(1)}, u32[]{:S(2)}) %copy-start.1) | copy-done | bytes 524312
  43.3 0.1 copy-done.2
  43.3 0.1 copy-done.3
  43.4 2.9 %couple.1 = (f32[64,256]{1,0:T(8,128)}, f32[64,256]{1,0:T(8,128)}, s32[1,1]{1,0:T(1,128)}) custom-call(s32[1,1]{1,0:T(1,128)S(6)} %copy.8.cnt.refs_0_, bf16[32,64,128]{2,1,0:T(8,128)(2,1)} %get-tuple-element.25.refs_1_, bf16[32,64,128]{2,1,0:T(8,128)(2,1)} %get-tuple-element.26.refs_2_, bf16[8,64,128]{2,1,0:T(8,128)(2,1)} %get-tuple-element.27.refs_3_, ...), custom_call_target="tpu_custom_call" | custom-call | flops 100000000 | bytes 3000000 | tf_op jit(solution)/shard_map/couple/pallas_call | solution.py:302
Async XLA Ops:
  5.8 17.7 %collective-permute-start = (bf16[32,64,128]{2,1,0:T(8,128)(2,1)}, bf16[32,64,128]{2,1,0:T(8,128)(2,1)S(1)}, u32[]{:S(2)}, u32[]{:S(2)}) collective-permute-start(bf16[32,64,128]{2,1,0:T(8,128)(2,1)} %get-tuple-element.20.fxa), channel_id=1, source_target_pairs={{0,4},{4,0},{8,12},{12,8},{16,20},{20,16},{24,28},{28,24},{1,5},{5... | collective-permute-start | bytes 1572872 | tf_op jit(solution)/shard_map/ppermute | solution.py:317
  5.9 36.6 %collective-permute-start.1 = (bf16[32,64,128]{2,1,0:T(8,128)(2,1)}, bf16[32,64,128]{2,1,0:T(8,128)(2,1)S(1)}, u32[]{:S(2)}, u32[]{:S(2)}) collective-permute-start(bf16[32,64,128]{2,1,0:T(8,128)(2,1)} %get-tuple-element.21.fxb), channel_id=1, source_target_pairs={{4,8},{8,4},{12,16},{16,12},{20,24},{24,20},{5,9},{9,5},{13,17},{1... | collective-permute-start | bytes 1572872 | tf_op jit(solution)/shard_map/ppermute | solution.py:316
  9.4 5.4 %collective-permute-start.2 = (s32[1,1]{1,0:T(1,128)}, s32[1,1]{1,0:T(1,128)}, u32[]{:S(2)}, u32[]{:S(2)}) collective-permute-start(s32[1,1]{1,0:T(1,128)} %param.7), channel_id=1, source_target_pairs={{0,2},{1,3},{2,0},{3,1},{4,6},{5,7},{6,4},{7,5},{8,10},{9,11},{10,... | collective-permute-start | bytes 20 | tf_op jit(solution)/shard_map/ppermute | solution.py:320
  12.0 11.5 %collective-permute-start.3 = (bf16[2,64,128]{2,1,0:T(8,128)(2,1)}, bf16[2,64,128]{2,1,0:T(8,128)(2,1)S(1)}, u32[]{:S(2)}, u32[]{:S(2)}) collective-permute-start(bf16[2,64,128]{2,1,0:T(8,128)(2,1)} %get-tuple-element.30), channel_id=1, source_target_pairs={{4,8},{8,4},{12,16},{16,12},{20,24},{24,20},{5,9},{9,5},{13,17},{1... | collective-permute-start | bytes 98312 | tf_op jit(solution)/shard_map/ppermute | solution.py:315
  23.6 0.6 %copy-start.4 = (bf16[2,64,128]{2,1,0:T(8,128)(2,1)}, bf16[2,64,128]{2,1,0:T(8,128)(2,1)S(1)}, u32[]{:S(2)}) copy-start(bf16[2,64,128]{2,1,0:T(8,128)(2,1)S(1)} %collective-permute-done.3.rxc) | copy-start | bytes 98308
  23.6 0.8 %copy-start = (bf16[32,64,128]{2,1,0:T(8,128)(2,1)}, bf16[32,64,128]{2,1,0:T(8,128)(2,1)S(1)}, u32[]{:S(2)}) copy-start(bf16[32,64,128]{2,1,0:T(8,128)(2,1)S(1)} %collective-permute-done.rxa.refs_6_) | copy-start | bytes 1572868
  26.9 15.6 %collective-permute-start.4 = (bf16[11,64,128]{2,1,0:T(8,128)(2,1)}, bf16[11,64,128]{2,1,0:T(8,128)(2,1)S(1)}, u32[]{:S(2)}, u32[]{:S(2)}) collective-permute-start(bf16[11,64,128]{2,1,0:T(8,128)(2,1)} %get-tuple-element.31), channel_id=1, source_target_pairs={{0,1},{1,0},{2,3},{3,2},{4,5},{5,4},{6,7},{7,6},{8,9},{9,8},{10,11... | collective-permute-start | bytes 540680 | tf_op jit(solution)/shard_map/ppermute | solution.py:325
  26.9 15.6 %collective-permute-start.5 = (bf16[11,64,128]{2,1,0:T(8,128)(2,1)}, bf16[11,64,128]{2,1,0:T(8,128)(2,1)S(1)}, u32[]{:S(2)}, u32[]{:S(2)}) collective-permute-start(bf16[11,64,128]{2,1,0:T(8,128)(2,1)} %get-tuple-element.32), channel_id=1, source_target_pairs={{1,2},{2,1},{5,6},{6,5},{9,10},{10,9},{13,14},{14,13},{17,18},{18,... | collective-permute-start | bytes 540680 | tf_op jit(solution)/shard_map/ppermute | solution.py:326
  42.5 0.8 %copy-start.1 = (bf16[32,64,128]{2,1,0:T(8,128)(2,1)}, bf16[32,64,128]{2,1,0:T(8,128)(2,1)S(1)}, u32[]{:S(2)}) copy-start(bf16[32,64,128]{2,1,0:T(8,128)(2,1)S(1)} %collective-permute-done.1.refs_7_) | copy-start | bytes 1572868
  42.5 0.8 %copy-start.2 = (bf16[11,64,128]{2,1,0:T(8,128)(2,1)}, bf16[11,64,128]{2,1,0:T(8,128)(2,1)S(1)}, u32[]{:S(2)}) copy-start(bf16[11,64,128]{2,1,0:T(8,128)(2,1)S(1)} %collective-permute-done.4.refs_8_) | copy-start | bytes 540676
  42.5 0.9 %copy-start.3 = (bf16[11,64,128]{2,1,0:T(8,128)(2,1)}, bf16[11,64,128]{2,1,0:T(8,128)(2,1)S(1)}, u32[]{:S(2)}) copy-start(bf16[11,64,128]{2,1,0:T(8,128)(2,1)S(1)} %collective-permute-done.5.refs_9_) | copy-start | bytes 540676

commit v2 on v1

--- a/solution.py
+++ b/solution.py
@@ -13,6 +13,7 @@
 VM = pl.BlockSpec(memory_space=pltpu.VMEM)
 SM = pl.BlockSpec(memory_space=pltpu.SMEM)
 ANY = pl.BlockSpec(memory_space=pl.ANY)
+HBM = pl.BlockSpec(memory_space=pltpu.HBM)
 
 
 def cost(flops, bytes_accessed):
@@ -38,7 +39,12 @@
     return steps
 
 
-def edge_kernel(cnt, v, s, fxa, fxb, fxc, fya, fyb, xbuf, ybuf, rx, ry, xsem, ysem):
+def edge_kernel(cnt_any, v, s_any, fxa, fxb, fxc, fya, fyb, cnt, s, xbuf, ybuf, rx, ry, xsem, ysem, sem):
+    small = [
+        pltpu.make_async_copy(src, dst, sem.at[i]) for i, (src, dst) in enumerate(((cnt_any, cnt), (s_any, s)))
+    ]
+    for c in small:
+        c.start()
     _, rows, ny, nz = xbuf.shape
     nx, band = ybuf.shape[2], ybuf.shape[3]
     stx, sty = ny + PAD, band + PAD
@@ -54,6 +60,8 @@
     ]
     for c in xcopies + ycopies:
         c.start()
+    for c in small:
+        c.wait()
     live = lax.broadcasted_iota(jnp.int32, (rows, nz), 0) < cnt[0, 0]
 
     def scaled(m, stiff):
@@ -84,42 +92,40 @@
     return pl.pallas_call(
         edge_kernel,
         out_shape=(face(ny), face(ny), face(2), face(nx), face(nx)),
-        in_specs=[SM, ANY, VM],
+        in_specs=[HBM, HBM, HBM],
         out_specs=(VM,) * 5,
         scratch_shapes=[
+            pltpu.SMEM((1, 1), jnp.int32),
+            pltpu.VMEM(stiff.shape, F32),
             pltpu.VMEM((2, rows, ny, nz), BF),
             pltpu.VMEM((2, rows, nx, band, nz), BF),
             pltpu.VMEM((rows * (ny + PAD), nz), F32),
             pltpu.VMEM((nx, rows * (band + PAD), nz), F32),
             pltpu.SemaphoreType.DMA((2,)),
             pltpu.SemaphoreType.DMA((2,)),
+            pltpu.SemaphoreType.DMA((2,)),
         ],
         cost_estimate=cost(10**6, 4 * 10**6),
+        compiler_params=pltpu.CompilerParams(vmem_limit_bytes=57 * 2**20),
         name="edges",
     )(counts, vectors, stiff)
 
 
-def pack_kernel(known, fya, fyb, rxa, rxc, mya, myb, sem):
+def pack_kernel(fya, fyb, rxa, rxc, *rest):
+    *known, mya, myb = rest
     nx, rows, nz = fya.shape
     ny = rxa.shape[0]
     y_even = even("sy")
     hi = jnp.where(y_even, ny - 1, 0)
-    copies = [
-        pltpu.make_async_copy(rxa.at[y], out.at[nx], sem.at[i])
-        for i, (y, out) in enumerate(((hi, mya), (ny - 1 - hi, myb)))
-    ]
-    for c in copies:
-        c.start()
     lane = lax.broadcasted_iota(jnp.int32, (rows, nz), 1)
     counts = jnp.zeros((rows, nz), F32)
-    for i in range(known.shape[1]):
-        counts = jnp.where(lane == i, known[0, i].astype(F32), counts)
-    for i, (src, out) in enumerate(((fya, mya), (fyb, myb))):
+    for i, one in enumerate(known):
+        counts = jnp.where(lane == i, one[0, 0].astype(F32), counts)
+    for i, (src, y, out) in enumerate(((fya, hi, mya), (fyb, ny - 1 - hi, myb))):
         out[0:nx] = src[...]
+        out[nx] = rxa[y]
         out[nx + 1] = rxc[i]
         out[nx + 2] = counts.astype(BF)
-    for c in copies:
-        c.wait()
 
 
 def pack(known, fya, fyb, rxa, rxc):
@@ -128,23 +134,22 @@
     return pl.pallas_call(
         pack_kernel,
         out_shape=(out, out),
-        in_specs=[SM, VM, VM, ANY, VM],
+        in_specs=[VM] * 4 + [SM] * len(known),
         out_specs=(VM, VM),
-        scratch_shapes=[pltpu.SemaphoreType.DMA((2,))],
         cost_estimate=cost(10**5, 10**6),
+        compiler_params=pltpu.CompilerParams(vmem_limit_bytes=8 * 2**20),
         name="pack",
-    )(known, fya, fyb, rxa, rxc)
-
-
-def own_kernel(cnt, v, s, d, fxa, fxb, fya, fyb, own, wxa, wxb, wya, wyb, wc, vbuf, r, er, ubuf, pbuf, szr, acc, sem):
-    nx, rows, ny, nz = vbuf.shape
+    )(fya, fyb, rxa, rxc, *known)
+
+
+def own_kernel(
+    cnt_any, v, s, d, fxa, fxb, fya, fyb, own, wxa, wxb, wya, wyb, wc,
+    cnt, r, er, ubuf, pbuf, szr, acc, small_sem,
+):
+    rows, nx, ny, nz = v.shape
     st = ny + PAD
-
-    def copy(x):
-        return pltpu.make_async_copy(v.at[:, x], vbuf.at[x], sem.at[x])
-
-    for x in range(nx):
-        copy(x).start()
+    small = pltpu.make_async_copy(cnt_any, cnt, small_sem)
+    small.start()
     er[...] = d[...] + s[...] * s[...]
     ubuf[...] = jnp.zeros_like(ubuf)
     acc[...] = jnp.zeros_like(acc)
@@ -166,9 +171,8 @@
 
     @pl.loop(0, nx)
     def _(x):
-        copy(x).wait()
         for a in range(rows):
-            r[a * st : a * st + ny, :] = vbuf[x, a].astype(F32)
+            r[a * st : a * st + ny, :] = v[a, x].astype(F32)
         total = acc[...]
         last = None
         left, right = [], []
@@ -198,6 +202,7 @@
         last = both
     pbuf[ny] = last
     total = smooth_part(acc[...])
+    small.wait()
     live = cnt[0, 0]
     keep = (lax.broadcasted_iota(jnp.int32, (rows, rows), 0) < live) & (
         lax.broadcasted_iota(jnp.int32, (rows, rows), 1) < live
@@ -228,65 +233,80 @@
     return pl.pallas_call(
         own_kernel,
         out_shape=(jax.ShapeDtypeStruct((rows, rows), F32), face(ny), face(ny), face(nx), face(nx), face(4)),
-        in_specs=[SM, ANY, VM, VM, VM, VM, VM, VM],
+        in_specs=[HBM] + [VM] * 7,
         out_specs=(VM,) * 6,
         scratch_shapes=[
-            pltpu.VMEM((nx, rows, ny, nz), BF),
+            pltpu.SMEM((1, 1), jnp.int32),
             pltpu.VMEM((rows * (ny + PAD), nz), F32),
             pltpu.VMEM((nx, ny, nz), F32),
             pltpu.VMEM((ny, rows, nz), BF),
             pltpu.VMEM((ny + 1, rows, nz), BF),
             pltpu.VMEM((2 * nz, 2 * nz), BF),
             pltpu.VMEM((rows, rows), F32),
-            pltpu.SemaphoreType.DMA((nx,)),
+            pltpu.SemaphoreType.DMA(()),
         ],
+        compiler_params=pltpu.CompilerParams(vmem_limit_bytes=16 * 2**20),
         cost_estimate=cost(2 * 10**9, 8 * 10**6),
         name="own",
     )(counts, vectors, stiff, diag, fxa, fxb, fya, fyb)
 
 
-def couple_kernel(masks, cnt, wxa, wxb, wya, wyb, wc, rxa, rxb, rya, ryb, known, faces, corners, offsets):
+def gram(left, right, n, total):
+    for i in range(0, n, 2):
+        total += lax.dot_general(
+            jnp.concatenate([left[i], left[i + 1]], 1),
+            jnp.concatenate([right[i], right[i + 1]], 1),
+            NT,
+            preferred_element_type=F32,
+        )
+    return total
+
+
+def across_x_kernel(wxa, wxb, rxa, rxb, out):
+    n, rows, _ = wxa.shape
+    zero = jnp.zeros((rows, rows), F32)
+    xa, xb = gram(wxa, rxa, n, zero), gram(wxb, rxb, n, zero)
+    x_even = even("sx")
+    out[:, 0:rows] = jnp.where(x_even, xb, xa)
+    out[:, rows : 2 * rows] = jnp.where(x_even, xa, xb)
+
+
+def across_x(wxa, wxb, rxa, rxb):
+    _, rows, _ = wxa.shape
+    return pl.pallas_call(
+        across_x_kernel,
+        out_shape=jax.ShapeDtypeStruct((rows, 2 * rows), F32),
+        in_specs=[VM] * 4,
+        out_specs=VM,
+        cost_estimate=cost(10**8, 2 * 10**6),
+        compiler_params=pltpu.CompilerParams(vmem_limit_bytes=8 * 2**20),
+        name="across_x",
+    )(wxa, wxb, rxa, rxb)
+
+
+def across_y_kernel(masks, fx, wya, wyb, wc, rya, ryb, *rest):
+    *known, faces, corners, offsets = rest
     nx, rows, nz = wya.shape
     x_even, y_even = even("sx"), even("sy")
-
-    def gram(left, right, n):
-        total = jnp.zeros((rows, rows), F32)
-        for i in range(0, n, 2):
-            total += lax.dot_general(
-                jnp.concatenate([left[i], left[i + 1]], 1),
-                jnp.concatenate([right[i], right[i + 1]], 1),
-                NT,
-                preferred_element_type=F32,
-            )
-        return total
-
-    ya, yb = gram(wya, rya, nx), gram(wyb, ryb, nx)
+    zero = jnp.zeros((rows, rows), F32)
     around = [
         [lax.dot_general(wc[2 * i + k], ry[nx + i], NT, preferred_element_type=F32) for k, ry in enumerate((rya, ryb))]
         for i in range(2)
     ]
-    n = wxa.shape[0]
-    xa, xb = gram(wxa, rxa, n), gram(wxb, rxb, n)
-    parts = (
-        jnp.where(x_even, xb, xa),
-        jnp.where(x_even, xa, xb),
-        jnp.where(y_even, yb, ya),
-        jnp.where(y_even, ya, yb),
-    )
-    for i, part in enumerate(parts):
-        faces[:, i * rows : (i + 1) * rows] = part
+    ya, yb = gram(wya, rya, nx, zero), gram(wyb, ryb, nx, zero)
+    faces[:, 0 : 2 * rows] = fx[...]
+    faces[:, 2 * rows : 3 * rows] = jnp.where(y_even, yb, ya)
+    faces[:, 3 * rows : 4 * rows] = jnp.where(y_even, ya, yb)
     for ix in range(2):
         for iy in range(2):
-            options = [
-                jnp.where(y_even == (iy == 1), around[k][0], around[k][1]) for k in range(2)
-            ]
+            options = [jnp.where(y_even == (iy == 1), around[k][0], around[k][1]) for k in range(2)]
             i = 2 * ix + iy
             corners[:, i * rows : (i + 1) * rows] = jnp.where(x_even == (ix == 1), options[0], options[1])
 
     me = lax.axis_index("sy")
     total = jnp.int32(0)
-    for i, mask in enumerate(masks):
-        total += jnp.where((me ^ mask) < me, known[0, i], 0)
+    for one, mask in zip(known, masks):
+        total += jnp.where((me ^ mask) < me, one[0, 0], 0)
     lane = lax.broadcasted_iota(jnp.int32, (8, nz), 1)
     theirs = rya[nx + 2, 0:16].astype(F32)[0:8]
     picked = jnp.zeros((8, nz), F32)
@@ -295,37 +315,41 @@
     offsets[...] = jnp.sum(picked[0:1], axis=1, keepdims=True).astype(jnp.int32) + total
 
 
-def couple(masks, counts, ws, received, known):
-    wxa = ws[0]
-    rows, nz = wxa.shape[1:]
+def across_y(masks, fx, wya, wyb, wc, rya, ryb, known):
+    rows = wya.shape[1]
     block = jax.ShapeDtypeStruct((rows, 4 * rows), F32)
     return pl.pallas_call(
-        lambda *refs: couple_kernel(masks, *refs),
+        lambda *refs: across_y_kernel(masks, *refs),
         out_shape=(block, block, jax.ShapeDtypeStruct((1, 1), jnp.int32)),
-        in_specs=[SM] + [VM] * 9 + [SM],
+        in_specs=[VM] * 6 + [SM] * len(known),
         out_specs=(VM, VM, VM),
-        cost_estimate=cost(10**8, 3 * 10**6),
-        name="couple",
-    )(counts, *ws, *received, known)
+        cost_estimate=cost(10**8, 10**6),
+        compiler_params=pltpu.CompilerParams(vmem_limit_bytes=8 * 2**20),
+        name="across_y",
+    )(fx, wya, wyb, wc, rya, ryb, *known)
+
+
+def swap(values, axis, first):
+    return lax.ppermute(values, axis, pairs(lax.axis_size(axis), first))
 
 
 def on_device(vectors, root_stiff, diag_coef, counts):
-    n_x, n_y = lax.axis_size("sx"), lax.axis_size("sy")
-    fxa, fxb, fxc, fya, fyb = edges(counts, vectors, root_stiff)
-    rxc = lax.ppermute(fxc, "sx", pairs(n_x, 1))
-    rxb = lax.ppermute(fxb, "sx", pairs(n_x, 1))
-    rxa = lax.ppermute(fxa, "sx", pairs(n_x, 0))
-    known, masks, bit = counts, [0], n_y // 2
+    n_y = lax.axis_size("sy")
+    known, masks, bit = [counts], [0], n_y // 2
     while bit >= 2:
-        other = lax.ppermute(known, "sy", [(i, i ^ bit) for i in range(n_y)])
-        known = jnp.concatenate([known, other], axis=1)
+        known += [lax.ppermute(one, "sy", [(i, i ^ bit) for i in range(n_y)]) for one in known]
         masks += [m ^ bit for m in masks]
         bit //= 2
+    fxa, fxb, fxc, fya, fyb = edges(counts, vectors, root_stiff)
+    rxc = swap(fxc, "sx", 1)
+    rxb = swap(fxb, "sx", 1)
+    rxa = swap(fxa, "sx", 0)
+    own_block, wxa, wxb, wya, wyb, wc = own(counts, vectors, root_stiff, diag_coef, fxa, fxb, fya, fyb)
     mya, myb = pack(known, fya, fyb, rxa, rxc)
-    rya = lax.ppermute(mya, "sy", pairs(n_y, 0))
-    ryb = lax.ppermute(myb, "sy", pairs(n_y, 1))
-    own_block, *ws = own(counts, vectors, root_stiff, diag_coef, fxa, fxb, fya, fyb)
-    faces, corners, offsets = couple(tuple(masks), counts, ws, (rxa, rxb, rya, ryb), known)
+    rya = swap(mya, "sy", 0)
+    ryb = swap(myb, "sy", 1)
+    fx = across_x(wxa, wxb, rxa, rxb)
+    faces, corners, offsets = across_y(tuple(masks), fx, wya, wyb, wc, rya, ryb, known)
     return own_block[None, None], faces[None, None], corners[None, None], offsets
 
 

time: 46.7 us -> 46.4 us (level)
  Pallas kernels: 20.5 us -> 15.1 us
  local copies, waits for them, and re-layouts: 1.66 us -> 6.6 us
  other arithmetic: 1.28 us -> 0 us
  waiting for transfers between devices: 7.52 us -> 8.52 us
    unnamed x10 -> x18, local copies, waits for them, and re-layouts: 1.66 us -> 6.6 us
    pallas_call x2 -> x3, Pallas kernels: 5.44 us -> 2.71 us  [the longest x1 1.58 us: across_y(): pl.pallas_call(lambda *refs: across_y_kernel(masks, *refs), out_shape=(bl...]
    pallas_call x1, Pallas kernels: 10.5 us -> 8.26 us  [own(): pl.pallas_call(own_kernel, out_shape=(jax.ShapeDtypeStruct((rows, rows),...]
    concatenate x1 -> x0, other arithmetic: 1.28 us -> none  [on_device(): known = jnp.concatenate([known, other], axis=1)]
    ppermute x6, waiting for transfers between devices: 7.52 us -> 8.52 us  [the longest x5 6.55 us: swap(): return lax.ppermute(values, axis, pairs(lax.axis_size(axis), first))]
  transfers between devices with their start and end apart: 6 -> 6, of which waited for: 1 -> 2; matrix products, arithmetic and copies ran while one was open for 3% -> 0% of each run, Pallas kernels for 28% -> 20%
where the time goes in v2:
time: 46.4 us; the launch traced here: 46.1 us
  Pallas kernels  15.1 us (33%)
  starting transfers between devices  14.3 us (31%)
  waiting for transfers between devices  8.52 us (18%)
  local copies, waits for them, and re-layouts  6.6 us (14%)
  between operations  1.56 us (3%)
    ppermute x5, starting transfers between devices, swap(): return lax.ppermute(values, axis, pairs(lax.axis_size(axis), first))  11.6 us
    pallas_call x1, Pallas kernels, own(): pl.pallas_call(own_kernel, out_shape=(jax.ShapeDtypeStruct((rows, rows),...  8.26 us
    unnamed x18, local copies, waits for them, and re-layouts  6.6 us
    ppermute x5, waiting for transfers between devices, swap(): return lax.ppermute(values, axis, pairs(lax.axis_size(axis), first))  6.55 us
    pallas_call x1, Pallas kernels, edges(): pl.pallas_call(edge_kernel, out_shape=(face(ny), face(ny), face(2), face(...  4.12 us
    ppermute x1, starting transfers between devices, on_device(): lax.ppermute(one, 'sy', [(i, i ^ bit) for i in range(n_y)])  2.65 us
    ppermute x1, waiting for transfers between devices, on_device(): lax.ppermute(one, 'sy', [(i, i ^ bit) for i in range(n_y)])  1.97 us
    pallas_call x1, Pallas kernels, across_y(): pl.pallas_call(lambda *refs: across_y_kernel(masks, *refs), out_shape=(bl...  1.58 us
  transfers between devices with their start and end apart: 6, of which 2 were waited for; matrix products, arithmetic and copies ran while one was open for 0% of the time, Pallas kernels for 20%

profile of v2, /device:TPU:12, one launch (start us, length us, event | category | flops | bytes accessed | tf_op | source)
XLA Modules:
  0.0 46.1 jit_solution(4116977064921196158)
XLA Ops:
  0.6 0.0 copy-start
  0.6 0.0 copy-start.1
  1.4 4.1 %edges.1 = (bf16[32,64,128]{2,1,0:T(8,128)(2,1)}, bf16[32,64,128]{2,1,0:T(8,128)(2,1)}, bf16[2,64,128]{2,1,0:T(8,128)(2,1)}, bf16[8,64,128]{2,1,0:T(8,128)(2,1)}, bf16[8,64,128]{2,1,0:T(8,128)(2,1)}) custom-call(s32[1,1]{1,0:T(1,128)S(6)} %copy.8.cnt_any.rest_0_.refs_6_, bf16[64,8,32,128]{3,2,1,0:T(8,128)(2,1)} %v.3, f32[8,32,128]{2,1,0:T(8,128)} %s.1), custom_call_target="tpu_custom_call" | custom-call | flops 1000000 | bytes 4000000 | tf_op jit(solution)/shard_map/edges/pallas_call | solution.py:92
  5.6 0.1 collective-permute-start
  5.7 3.4 %collective-permute-start.1 = (bf16[32,64,128]{2,1,0:T(8,128)(2,1)}, bf16[32,64,128]{2,1,0:T(8,128)(2,1)S(1)}, u32[]{:S(2)}, u32[]{:S(2)}) collective-permute-start(bf16[32,64,128]{2,1,0:T(8,128)(2,1)} %get-tuple-element.21.fxb), channel_id=1, source_target_pairs={{4,8},{8,4},{12,16},{16,12},{20,24},{24,20},{5,9},{9,5},{13,17},{1... | collective-permute-start | bytes 1572872 | tf_op jit(solution)/shard_map/ppermute | solution.py:333
  9.1 3.0 %collective-permute-start.2 = (bf16[2,64,128]{2,1,0:T(8,128)(2,1)}, bf16[2,64,128]{2,1,0:T(8,128)(2,1)S(1)}, u32[]{:S(2)}, u32[]{:S(2)}) collective-permute-start(bf16[2,64,128]{2,1,0:T(8,128)(2,1)} %get-tuple-element.30), channel_id=1, source_target_pairs={{4,8},{8,4},{12,16},{16,12},{20,24},{24,20},{5,9},{9,5},{13,17},{1... | collective-permute-start | bytes 98312 | tf_op jit(solution)/shard_map/ppermute | solution.py:333
  12.1 2.7 %collective-permute-start.3 = (s32[1,1]{1,0:T(1,128)}, s32[1,1]{1,0:T(1,128)}, u32[]{:S(2)}, u32[]{:S(2)}) collective-permute-start(s32[1,1]{1,0:T(1,128)} %param.7), channel_id=1, source_target_pairs={{0,2},{1,3},{2,0},{3,1},{4,6},{5,7},{6,4},{7,5},{8,10},{9,11},{10,... | collective-permute-start | bytes 20 | tf_op jit(solution)/shard_map/ppermute | solution.py:340
  14.8 2.0 %collective-permute-done.3.rest_1_.refs_7_ = s32[1,1]{1,0:T(1,128)} collective-permute-done((s32[1,1]{1,0:T(1,128)}, s32[1,1]{1,0:T(1,128)}, u32[]{:S(2)}, u32[]{:S(2)}) %collective-permute-start.3) | collective-permute-done | bytes 36 | tf_op jit(solution)/shard_map/ppermute | solution.py:340
  16.7 6.5 %collective-permute-done.2.rxc = bf16[2,64,128]{2,1,0:T(8,128)(2,1)S(1)} collective-permute-done((bf16[2,64,128]{2,1,0:T(8,128)(2,1)}, bf16[2,64,128]{2,1,0:T(8,128)(2,1)S(1)}, u32[]{:S(2)}, u32[]{:S(2)}) %collective-permute-start.2) | collective-permute-done | bytes 32800 | tf_op jit(solution)/shard_map/ppermute | solution.py:333
  23.3 0.0 collective-permute-done.rxa
  23.3 0.0 copy-start.2
  23.3 0.9 %copy-done.2 = bf16[8,64,128]{2,1,0:T(8,128)(2,1)S(1)} copy-done((bf16[8,64,128]{2,1,0:T(8,128)(2,1)S(1)}, bf16[8,64,128]{2,1,0:T(8,128)(2,1)}, u32[]{:S(2)}) %copy-start.2) | copy-done | bytes 131096
  24.2 0.0 copy-start.4
  24.2 0.9 %copy-done.4 = bf16[8,64,128]{2,1,0:T(8,128)(2,1)S(1)} copy-done((bf16[8,64,128]{2,1,0:T(8,128)(2,1)S(1)}, bf16[8,64,128]{2,1,0:T(8,128)(2,1)}, u32[]{:S(2)}) %copy-start.4) | copy-done | bytes 131096
  25.1 0.7 %pack.1 = (bf16[11,64,128]{2,1,0:T(8,128)(2,1)S(1)}, bf16[11,64,128]{2,1,0:T(8,128)(2,1)S(1)}) custom-call(bf16[8,64,128]{2,1,0:T(8,128)(2,1)S(1)} %copy-done.2, bf16[8,64,128]{2,1,0:T(8,128)(2,1)S(1)} %copy-done.4, bf16[32,64,128]{2,1,0:T(8,128)(2,1)S(1)} %collective-permute-done.rxa, bf16[2,64,128]{2,1,0:T(8,128)(2,1)S(1)} %collective-permute-done.2.rxc, ...), custom_call_target="tpu_custom_call" | custom-call | flops 100000 | bytes 1000000 | tf_op jit(solution)/shard_map/pack/pallas_call | solution.py:134
  25.8 0.1 collective-permute-start.4
  25.8 5.0 %collective-permute-start.5 = (bf16[11,64,128]{2,1,0:T(8,128)(2,1)S(1)}, bf16[11,64,128]{2,1,0:T(8,128)(2,1)S(1)}, u32[]{:S(2)}, u32[]{:S(2)}) collective-permute-start(bf16[11,64,128]{2,1,0:T(8,128)(2,1)S(1)} %get-tuple-element.32), channel_id=1, source_target_pairs={{1,2},{2,1},{5,6},{6,5},{9,10},{10,9},{13,14},{14,13},{17,18},{18,... | collective-permute-start | bytes 540680 | tf_op jit(solution)/shard_map/ppermute | solution.py:333
  30.9 0.0 copy-done
  30.9 0.0 copy-done.1
  30.9 0.0 copy-start.3
  30.9 0.9 %copy-done.3 = bf16[8,64,128]{2,1,0:T(8,128)(2,1)S(1)} copy-done((bf16[8,64,128]{2,1,0:T(8,128)(2,1)S(1)}, bf16[8,64,128]{2,1,0:T(8,128)(2,1)}, u32[]{:S(2)}) %copy-start.3) | copy-done | bytes 131096
  31.8 0.0 copy-start.5
  31.8 0.9 %copy-done.5 = bf16[8,64,128]{2,1,0:T(8,128)(2,1)S(1)} copy-done((bf16[8,64,128]{2,1,0:T(8,128)(2,1)S(1)}, bf16[8,64,128]{2,1,0:T(8,128)(2,1)}, u32[]{:S(2)}) %copy-start.5) | copy-done | bytes 131096
  32.7 0.0 copy-start.6
  32.7 1.0 %copy-done.6 = bf16[32,64,128]{2,1,0:T(8,128)(2,1)S(1)} copy-done((bf16[32,64,128]{2,1,0:T(8,128)(2,1)S(1)}, bf16[32,64,128]{2,1,0:T(8,128)(2,1)}, u32[]{:S(2)}) %copy-start.6) | copy-done | bytes 524312
  33.8 0.0 copy-start.7
  33.8 1.0 %copy-done.7 = bf16[32,64,128]{2,1,0:T(8,128)(2,1)S(1)} copy-done((bf16[32,64,128]{2,1,0:T(8,128)(2,1)S(1)}, bf16[32,64,128]{2,1,0:T(8,128)(2,1)}, u32[]{:S(2)}) %copy-start.7) | copy-done | bytes 524312
  34.8 0.0 copy-start.8
  34.8 0.9 %copy-done.8 = f32[8,32,128]{2,1,0:T(8,128)S(1)} copy-done((f32[8,32,128]{2,1,0:T(8,128)S(1)}, f32[8,32,128]{2,1,0:T(8,128)}, u32[]{:S(2)}) %copy-start.8) | copy-done | bytes 131096
  35.7 8.3 %own.1 = (f32[64,64]{1,0:T(8,128)}, bf16[32,64,128]{2,1,0:T(8,128)(2,1)S(1)}, bf16[32,64,128]{2,1,0:T(8,128)(2,1)S(1)}, bf16[8,64,128]{2,1,0:T(8,128)(2,1)S(1)},...) custom-call(s32[1,1]{1,0:T(1,128)S(6)} %copy.8.cnt_any.rest_0_.refs_6_, ...), custom_call_target="tpu_custom_call" | custom-call | flops 2000000000 | bytes 8000000 | tf_op jit(solution)/shard_map/own/pallas_call | solution.py:233
  44.0 0.0 collective-permute-done.1.rxb
  44.0 0.5 %across_x.1.refs_0_ = f32[64,128]{1,0:T(8,128)S(1)} custom-call(bf16[32,64,128]{2,1,0:T(8,128)(2,1)S(1)} %get-tuple-element.25.wxa, bf16[32,64,128]{2,1,0:T(8,128)(2,1)S(1)} %get-tuple-element.26.wxb, bf16[32,64,128]{2,1,0:T(8,128)(2,1)S(1)} %collective-permute-done.rxa, bf16[32,64,128]{2,1,0:T(8,128)(2,1)S(1)} %collective-permute-done.1.rxb), custom_call_target="tpu_custom_call" | custom-call | flops 100000000 | bytes 2000000 | tf_op jit(solution)/shard_map/across_x/pallas_call | solution.py:276
  44.5 0.0 collective-permute-done.4.refs_4_
  44.5 0.0 collective-permute-done.5.refs_5_
  44.5 1.6 %across_y.1 = (f32[64,256]{1,0:T(8,128)}, f32[64,256]{1,0:T(8,128)}, s32[1,1]{1,0:T(1,128)}) custom-call(f32[64,128]{1,0:T(8,128)S(1)} %across_x.1.refs_0_, bf16[8,64,128]{2,1,0:T(8,128)(2,1)S(1)} %get-tuple-element.27.refs_1_, bf16[8,64,128]{2,1,0:T(8,128)(2,1)S(1)} %get-tuple-element.28.refs_2_, bf16[4,64,128]{2,1,0:T(8,128)(2,1)S(1)} %get-tuple-element.29.refs_3_, ...), custom_call_target="tpu_custom_call" | custom-call | flops 100000000 | bytes 1000000 | tf_op jit(solution)/shard_map/across_y/pallas_call | solution.py:321
Async XLA Ops:
  0.6 30.3 %copy-start = (bf16[64,8,32,128]{3,2,1,0:T(8,128)(2,1)S(1)}, bf16[64,8,32,128]{3,2,1,0:T(8,128)(2,1)}, u32[]{:S(2)}) copy-start(bf16[64,8,32,128]{3,2,1,0:T(8,128)(2,1)} %v.3) | copy-start | bytes 12582916
  0.6 30.3 %copy-start.1 = (f32[8,32,128]{2,1,0:T(8,128)S(1)}, f32[8,32,128]{2,1,0:T(8,128)}, u32[]{:S(2)}) copy-start(f32[8,32,128]{2,1,0:T(8,128)} %s.1) | copy-start | bytes 393220
  5.6 17.7 %collective-permute-start = (bf16[32,64,128]{2,1,0:T(8,128)(2,1)}, bf16[32,64,128]{2,1,0:T(8,128)(2,1)S(1)}, u32[]{:S(2)}, u32[]{:S(2)}) collective-permute-start(bf16[32,64,128]{2,1,0:T(8,128)(2,1)} %get-tuple-element.20.fxa), channel_id=1, source_target_pairs={{0,4},{4,0},{8,12},{12,8},{16,20},{20,16},{24,28},{28,24},{1,5},{5... | collective-permute-start | bytes 1572872 | tf_op jit(solution)/shard_map/ppermute | solution.py:333
  5.7 38.3 %collective-permute-start.1 = (bf16[32,64,128]{2,1,0:T(8,128)(2,1)}, bf16[32,64,128]{2,1,0:T(8,128)(2,1)S(1)}, u32[]{:S(2)}, u32[]{:S(2)}) collective-permute-start(bf16[32,64,128]{2,1,0:T(8,128)(2,1)} %get-tuple-element.21.fxb), channel_id=1, source_target_pairs={{4,8},{8,4},{12,16},{16,12},{20,24},{24,20},{5,9},{9,5},{13,17},{1... | collective-permute-start | bytes 1572872 | tf_op jit(solution)/shard_map/ppermute | solution.py:333
  9.1 14.2 %collective-permute-start.2 = (bf16[2,64,128]{2,1,0:T(8,128)(2,1)}, bf16[2,64,128]{2,1,0:T(8,128)(2,1)S(1)}, u32[]{:S(2)}, u32[]{:S(2)}) collective-permute-start(bf16[2,64,128]{2,1,0:T(8,128)(2,1)} %get-tuple-element.30), channel_id=1, source_target_pairs={{4,8},{8,4},{12,16},{16,12},{20,24},{24,20},{5,9},{9,5},{13,17},{1... | collective-permute-start | bytes 98312 | tf_op jit(solution)/shard_map/ppermute | solution.py:333
  12.1 4.6 %collective-permute-start.3 = (s32[1,1]{1,0:T(1,128)}, s32[1,1]{1,0:T(1,128)}, u32[]{:S(2)}, u32[]{:S(2)}) collective-permute-start(s32[1,1]{1,0:T(1,128)} %param.7), channel_id=1, source_target_pairs={{0,2},{1,3},{2,0},{3,1},{4,6},{5,7},{6,4},{7,5},{8,10},{9,11},{10,... | collective-permute-start | bytes 20 | tf_op jit(solution)/shard_map/ppermute | solution.py:340
  23.3 0.9 %copy-start.2 = (bf16[8,64,128]{2,1,0:T(8,128)(2,1)S(1)}, bf16[8,64,128]{2,1,0:T(8,128)(2,1)}, u32[]{:S(2)}) copy-start(bf16[8,64,128]{2,1,0:T(8,128)(2,1)} %get-tuple-element.22.fya) | copy-start | bytes 393220
  24.2 0.9 %copy-start.4 = (bf16[8,64,128]{2,1,0:T(8,128)(2,1)S(1)}, bf16[8,64,128]{2,1,0:T(8,128)(2,1)}, u32[]{:S(2)}) copy-start(bf16[8,64,128]{2,1,0:T(8,128)(2,1)} %get-tuple-element.23.fyb) | copy-start | bytes 393220
  25.8 18.7 %collective-permute-start.4 = (bf16[11,64,128]{2,1,0:T(8,128)(2,1)S(1)}, bf16[11,64,128]{2,1,0:T(8,128)(2,1)S(1)}, u32[]{:S(2)}, u32[]{:S(2)}) collective-permute-start(bf16[11,64,128]{2,1,0:T(8,128)(2,1)S(1)} %get-tuple-element.31), channel_id=1, source_target_pairs={{0,1},{1,0},{2,3},{3,2},{4,5},{5,4},{6,7},{7,6},{8,9},{9,8},{10,11... | collective-permute-start | bytes 540680 | tf_op jit(solution)/shard_map/ppermute | solution.py:333
  25.8 18.6 %collective-permute-start.5 = (bf16[11,64,128]{2,1,0:T(8,128)(2,1)S(1)}, bf16[11,64,128]{2,1,0:T(8,128)(2,1)S(1)}, u32[]{:S(2)}, u32[]{:S(2)}) collective-permute-start(bf16[11,64,128]{2,1,0:T(8,128)(2,1)S(1)} %get-tuple-element.32), channel_id=1, source_target_pairs={{1,2},{2,1},{5,6},{6,5},{9,10},{10,9},{13,14},{14,13},{17,18},{18,... | collective-permute-start | bytes 540680 | tf_op jit(solution)/shard_map/ppermute | solution.py:333
  30.9 0.9 %copy-start.3 = (bf16[8,64,128]{2,1,0:T(8,128)(2,1)S(1)}, bf16[8,64,128]{2,1,0:T(8,128)(2,1)}, u32[]{:S(2)}) copy-start(bf16[8,64,128]{2,1,0:T(8,128)(2,1)} %get-tuple-element.22.fya) | copy-start | bytes 393220
  31.8 0.9 %copy-start.5 = (bf16[8,64,128]{2,1,0:T(8,128)(2,1)S(1)}, bf16[8,64,128]{2,1,0:T(8,128)(2,1)}, u32[]{:S(2)}) copy-start(bf16[8,64,128]{2,1,0:T(8,128)(2,1)} %get-tuple-element.23.fyb) | copy-start | bytes 393220
  32.7 1.0 %copy-start.6 = (bf16[32,64,128]{2,1,0:T(8,128)(2,1)S(1)}, bf16[32,64,128]{2,1,0:T(8,128)(2,1)}, u32[]{:S(2)}) copy-start(bf16[32,64,128]{2,1,0:T(8,128)(2,1)} %get-tuple-element.20.fxa) | copy-start | bytes 1572868
  33.8 1.0 %copy-start.7 = (bf16[32,64,128]{2,1,0:T(8,128)(2,1)S(1)}, bf16[32,64,128]{2,1,0:T(8,128)(2,1)}, u32[]{:S(2)}) copy-start(bf16[32,64,128]{2,1,0:T(8,128)(2,1)} %get-tuple-element.21.fxb) | copy-start | bytes 1572868
  34.8 0.9 %copy-start.8 = (f32[8,32,128]{2,1,0:T(8,128)S(1)}, f32[8,32,128]{2,1,0:T(8,128)}, u32[]{:S(2)}) copy-start(f32[8,32,128]{2,1,0:T(8,128)} %d.1) | copy-start | bytes 393220

commit v3 on v2

--- a/solution.py
+++ b/solution.py
@@ -10,6 +10,7 @@
 NT = (((1,), (1,)), ((), ()))
 NN = (((1,), (0,)), ((), ()))
 PAD = 4
+BAND = 8
 VM = pl.BlockSpec(memory_space=pltpu.VMEM)
 SM = pl.BlockSpec(memory_space=pltpu.SMEM)
 ANY = pl.BlockSpec(memory_space=pl.ANY)
@@ -39,74 +40,53 @@
     return steps
 
 
-def edge_kernel(cnt_any, v, s_any, fxa, fxb, fxc, fya, fyb, cnt, s, xbuf, ybuf, rx, ry, xsem, ysem, sem):
-    small = [
-        pltpu.make_async_copy(src, dst, sem.at[i]) for i, (src, dst) in enumerate(((cnt_any, cnt), (s_any, s)))
-    ]
-    for c in small:
-        c.start()
-    _, rows, ny, nz = xbuf.shape
-    nx, band = ybuf.shape[2], ybuf.shape[3]
-    stx, sty = ny + PAD, band + PAD
+def edge_kernel(cnt_any, v, s, fxa, fxb, fxc, fya, fyb, cnt, rx, ry, sem):
+    small = pltpu.make_async_copy(cnt_any, cnt, sem)
+    small.start()
+    rows, nx, ny, nz = v.shape
+    stx, sty = ny + PAD, BAND + PAD
     x_even, y_even = even("sx"), even("sy")
     xa = jnp.where(x_even, nx - 1, 0)
-    xb = nx - 1 - xa
-    ya = jnp.where(y_even, ny - band, 0)
-    yb = ny - band - ya
-    xcopies = [pltpu.make_async_copy(v.at[:, x], xbuf.at[i], xsem.at[i]) for i, x in enumerate((xb, xa))]
-    ycopies = [
-        pltpu.make_async_copy(v.at[:, :, pl.ds(pl.multiple_of(y, band), band)], ybuf.at[i], ysem.at[i])
-        for i, y in enumerate((ya, yb))
-    ]
-    for c in xcopies + ycopies:
-        c.start()
-    for c in small:
-        c.wait()
+    ya = jnp.where(y_even, ny - 1, 0)
+    xb, yb = nx - 1 - xa, ny - 1 - ya
+    small.wait()
     live = lax.broadcasted_iota(jnp.int32, (rows, nz), 0) < cnt[0, 0]
 
     def scaled(m, stiff):
         return jnp.where(live, m * jnp.broadcast_to(stiff, (rows, nz)), 0.0).astype(BF)
 
-    for i, (x, out) in enumerate(((xb, fxb), (xa, fxa))):
-        xcopies[i].wait()
+    for x, out in ((xb, fxb), (xa, fxa)):
         for a in range(rows):
-            rx[a * stx : a * stx + ny, :] = xbuf[i, a].astype(F32)
+            rx[a * stx : a * stx + ny, :] = v[a, x].astype(F32)
         for y in range(ny):
             out[y] = scaled(rx[pl.ds(y, rows, stride=stx), :], s[x, pl.ds(y, 1), :])
-        if i == 0:
-            fxc[0] = fxb[jnp.where(y_even, ny - 1, 0)]
-            fxc[1] = fxb[jnp.where(y_even, 0, ny - 1)]
-    for i, (y0, out) in enumerate(((ya, fya), (yb, fyb))):
-        ycopies[i].wait()
-        inner = jnp.where(y0 == 0, 0, band - 1)
+    fxc[0] = fxb[ya]
+    fxc[1] = fxb[yb]
+    for y, out in ((ya, fya), (yb, fyb)):
+        band = pl.multiple_of((y // BAND) * BAND, BAND)
+        inner = y - band
         for x in range(nx):
             for a in range(rows):
-                ry[x, a * sty : a * sty + band, :] = ybuf[i, a, x].astype(F32)
-            out[x] = scaled(ry[x, pl.ds(inner, rows, stride=sty), :], s[x, pl.ds(y0 + inner, 1), :])
+                ry[x, a * sty : a * sty + BAND, :] = v[a, x, pl.ds(band, BAND), :].astype(F32)
+            out[x] = scaled(ry[x, pl.ds(inner, rows, stride=sty), :], s[x, pl.ds(y, 1), :])
 
 
 def edges(counts, vectors, stiff):
     rows, nx, ny, nz = vectors.shape
-    band = 16
-    face = lambda *dims: jax.ShapeDtypeStruct((*dims, rows, nz), BF)
+    face = lambda n: jax.ShapeDtypeStruct((n, rows, nz), BF)
     return pl.pallas_call(
         edge_kernel,
         out_shape=(face(ny), face(ny), face(2), face(nx), face(nx)),
-        in_specs=[HBM, HBM, HBM],
+        in_specs=[HBM, VM, VM],
         out_specs=(VM,) * 5,
         scratch_shapes=[
             pltpu.SMEM((1, 1), jnp.int32),
-            pltpu.VMEM(stiff.shape, F32),
-            pltpu.VMEM((2, rows, ny, nz), BF),
-            pltpu.VMEM((2, rows, nx, band, nz), BF),
             pltpu.VMEM((rows * (ny + PAD), nz), F32),
-            pltpu.VMEM((nx, rows * (band + PAD), nz), F32),
-            pltpu.SemaphoreType.DMA((2,)),
-            pltpu.SemaphoreType.DMA((2,)),
-            pltpu.SemaphoreType.DMA((2,)),
+            pltpu.VMEM((nx, rows * (BAND + PAD), nz), F32),
+            pltpu.SemaphoreType.DMA(()),
         ],
         cost_estimate=cost(10**6, 4 * 10**6),
-        compiler_params=pltpu.CompilerParams(vmem_limit_bytes=57 * 2**20),
+        compiler_params=pltpu.CompilerParams(vmem_limit_bytes=12 * 2**20),
         name="edges",
     )(counts, vectors, stiff)
 
@@ -142,8 +122,51 @@
     )(fya, fyb, rxa, rxc, *known)
 
 
+def along_z(stack, n, stencil):
+    rows, nz = stack(0).shape
+    wide = jnp.concatenate([jnp.concatenate([stack(2 * c), stack(2 * c + 1)], 1) for c in range(n // 2)], 0)
+    z = lax.dot_general(wide, stencil, NN, preferred_element_type=F32)
+    return [z[(i // 2) * rows : (i // 2 + 1) * rows, (i % 2) * nz : (i % 2 + 1) * nz] for i in range(n)]
+
+
+def smooth_kernel(fxa, fxb, fya, fyb, wxa, wxb, wya, wyb, wc):
+    ny, _, nz = fxa.shape
+    stencil = tri(nz, 2, -0.25)
+    for src, out in ((fxa, wxa), (fxb, wxb), (fya, wya), (fyb, wyb)):
+        n = src.shape[0]
+        zs = along_z(lambda i: src[i], n, stencil)
+        for i in range(n):
+            t = zs[i] + zs[i]
+            if i > 0:
+                t = t + zs[i - 1]
+            if i < n - 1:
+                t = t + zs[i + 1]
+            out[i] = t.astype(BF)
+    y_even = even("sy")
+    rows_y = (jnp.where(y_even, ny - 1, 0), jnp.where(y_even, 0, ny - 1))
+    for i, src in enumerate((fxa, fxb)):
+        zs = along_z(lambda k: src[rows_y[k]], 2, stencil)
+        for k in range(2):
+            wc[2 * i + k] = zs[k].astype(BF)
+
+
+def smooth(fxa, fxb, fya, fyb):
+    ny, rows, nz = fxa.shape
+    nx = fya.shape[0]
+    face = lambda n: jax.ShapeDtypeStruct((n, rows, nz), BF)
+    return pl.pallas_call(
+        smooth_kernel,
+        out_shape=(face(ny), face(ny), face(nx), face(nx), face(4)),
+        in_specs=[VM] * 4,
+        out_specs=(VM,) * 5,
+        cost_estimate=cost(10**8, 2 * 10**6),
+        compiler_params=pltpu.CompilerParams(vmem_limit_bytes=12 * 2**20),
+        name="smooth",
+    )(fxa, fxb, fya, fyb)
+
+
 def own_kernel(
-    cnt_any, v, s, d, fxa, fxb, fya, fyb, own, wxa, wxb, wya, wyb, wc,
+    cnt_any, v, s, d, own,
     cnt, r, er, ubuf, pbuf, szr, acc, small_sem,
 ):
     rows, nx, ny, nz = v.shape
@@ -155,13 +178,8 @@
     acc[...] = jnp.zeros_like(acc)
     szr[...] = tri(nz, 2, -0.25)
 
-    def along_z(stack, n):
-        wide = jnp.concatenate([jnp.concatenate([stack(2 * c), stack(2 * c + 1)], 1) for c in range(n // 2)], 0)
-        z = lax.dot_general(wide, szr[...], NN, preferred_element_type=F32)
-        return [z[(i // 2) * rows : (i // 2 + 1) * rows, (i % 2) * nz : (i % 2 + 1) * nz] for i in range(n)]
-
     def smooth_part(total):
-        zs = along_z(lambda y: pbuf[y], ny)
+        zs = along_z(lambda y: pbuf[y], ny, szr[...])
         for c in range(ny // 2):
             left = jnp.concatenate([zs[2 * c].astype(BF), zs[2 * c + 1].astype(BF)], 1)
             right = jnp.concatenate([pbuf[2 * c], pbuf[2 * c + 1]], 1)
@@ -209,32 +227,14 @@
     )
     own[...] = jnp.where(keep, total, 0.0)
 
-    for src, out in ((fxa, wxa), (fxb, wxb), (fya, wya), (fyb, wyb)):
-        n = src.shape[0]
-        zs = along_z(lambda i: src[i], n)
-        for i in range(n):
-            t = zs[i] + zs[i]
-            if i > 0:
-                t = t + zs[i - 1]
-            if i < n - 1:
-                t = t + zs[i + 1]
-            out[i] = t.astype(BF)
-    y_even = even("sy")
-    rows_y = (jnp.where(y_even, ny - 1, 0), jnp.where(y_even, 0, ny - 1))
-    for i, src in enumerate((fxa, fxb)):
-        zs = along_z(lambda k: src[rows_y[k]], 2)
-        for k in range(2):
-            wc[2 * i + k] = zs[k].astype(BF)
-
-
-def own(counts, vectors, stiff, diag, fxa, fxb, fya, fyb):
+
+def own(counts, vectors, stiff, diag):
     rows, nx, ny, nz = vectors.shape
-    face = lambda n: jax.ShapeDtypeStruct((n, rows, nz), BF)
     return pl.pallas_call(
         own_kernel,
-        out_shape=(jax.ShapeDtypeStruct((rows, rows), F32), face(ny), face(ny), face(nx), face(nx), face(4)),
-        in_specs=[HBM] + [VM] * 7,
-        out_specs=(VM,) * 6,
+        out_shape=jax.ShapeDtypeStruct((rows, rows), F32),
+        in_specs=[HBM] + [VM] * 3,
+        out_specs=VM,
         scratch_shapes=[
             pltpu.SMEM((1, 1), jnp.int32),
             pltpu.VMEM((rows * (ny + PAD), nz), F32),
@@ -248,7 +248,7 @@
         compiler_params=pltpu.CompilerParams(vmem_limit_bytes=16 * 2**20),
         cost_estimate=cost(2 * 10**9, 8 * 10**6),
         name="own",
-    )(counts, vectors, stiff, diag, fxa, fxb, fya, fyb)
+    )(counts, vectors, stiff, diag)
 
 
 def gram(left, right, n, total):
@@ -262,29 +262,7 @@
     return total
 
 
-def across_x_kernel(wxa, wxb, rxa, rxb, out):
-    n, rows, _ = wxa.shape
-    zero = jnp.zeros((rows, rows), F32)
-    xa, xb = gram(wxa, rxa, n, zero), gram(wxb, rxb, n, zero)
-    x_even = even("sx")
-    out[:, 0:rows] = jnp.where(x_even, xb, xa)
-    out[:, rows : 2 * rows] = jnp.where(x_even, xa, xb)
-
-
-def across_x(wxa, wxb, rxa, rxb):
-    _, rows, _ = wxa.shape
-    return pl.pallas_call(
-        across_x_kernel,
-        out_shape=jax.ShapeDtypeStruct((rows, 2 * rows), F32),
-        in_specs=[VM] * 4,
-        out_specs=VM,
-        cost_estimate=cost(10**8, 2 * 10**6),
-        compiler_params=pltpu.CompilerParams(vmem_limit_bytes=8 * 2**20),
-        name="across_x",
-    )(wxa, wxb, rxa, rxb)
-
-
-def across_y_kernel(masks, fx, wya, wyb, wc, rya, ryb, *rest):
+def couple_kernel(masks, wxa, wxb, wya, wyb, wc, rxa, rxb, rya, ryb, *rest):
     *known, faces, corners, offsets = rest
     nx, rows, nz = wya.shape
     x_even, y_even = even("sx"), even("sy")
@@ -294,7 +272,9 @@
         for i in range(2)
     ]
     ya, yb = gram(wya, rya, nx, zero), gram(wyb, ryb, nx, zero)
-    faces[:, 0 : 2 * rows] = fx[...]
+    xa, xb = gram(wxa, rxa, wxa.shape[0], zero), gram(wxb, rxb, wxa.shape[0], zero)
+    faces[:, 0:rows] = jnp.where(x_even, xb, xa)
+    faces[:, rows : 2 * rows] = jnp.where(x_even, xa, xb)
     faces[:, 2 * rows : 3 * rows] = jnp.where(y_even, yb, ya)
     faces[:, 3 * rows : 4 * rows] = jnp.where(y_even, ya, yb)
     for ix in range(2):
@@ -315,18 +295,18 @@
     offsets[...] = jnp.sum(picked[0:1], axis=1, keepdims=True).astype(jnp.int32) + total
 
 
-def across_y(masks, fx, wya, wyb, wc, rya, ryb, known):
-    rows = wya.shape[1]
+def couple(masks, ws, received, known):
+    rows = ws[0].shape[1]
     block = jax.ShapeDtypeStruct((rows, 4 * rows), F32)
     return pl.pallas_call(
-        lambda *refs: across_y_kernel(masks, *refs),
+        lambda *refs: couple_kernel(masks, *refs),
         out_shape=(block, block, jax.ShapeDtypeStruct((1, 1), jnp.int32)),
-        in_specs=[VM] * 6 + [SM] * len(known),
+        in_specs=[VM] * 9 + [SM] * len(known),
         out_specs=(VM, VM, VM),
         cost_estimate=cost(10**8, 10**6),
         compiler_params=pltpu.CompilerParams(vmem_limit_bytes=8 * 2**20),
-        name="across_y",
-    )(fx, wya, wyb, wc, rya, ryb, *known)
+        name="couple",
+    )(*ws, *received, *known)
 
 
 def swap(values, axis, first):
@@ -344,12 +324,12 @@
     rxc = swap(fxc, "sx", 1)
     rxb = swap(fxb, "sx", 1)
     rxa = swap(fxa, "sx", 0)
-    own_block, wxa, wxb, wya, wyb, wc = own(counts, vectors, root_stiff, diag_coef, fxa, fxb, fya, fyb)
+    ws = smooth(fxa, fxb, fya, fyb)
     mya, myb = pack(known, fya, fyb, rxa, rxc)
     rya = swap(mya, "sy", 0)
     ryb = swap(myb, "sy", 1)
-    fx = across_x(wxa, wxb, rxa, rxb)
-    faces, corners, offsets = across_y(tuple(masks), fx, wya, wyb, wc, rya, ryb, known)
+    own_block = own(counts, vectors, root_stiff, diag_coef)
+    faces, corners, offsets = couple(tuple(masks), ws, (rxa, rxb, rya, ryb), known)
     return own_block[None, None], faces[None, None], corners[None, None], offsets
 
 

time: 46.4 us -> 39 us (0.84)
  local copies, waits for them, and re-layouts: 6.6 us -> 3.1 us
  Pallas kernels: 15.1 us -> 12.2 us
  waiting for transfers between devices: 8.52 us -> 7.75 us
    unnamed x18 -> x10, local copies, waits for them, and re-layouts: 6.6 us -> 3.1 us
    pallas_call x1, Pallas kernels: 4.12 us -> 1.39 us  [edges(): pl.pallas_call(edge_kernel, out_shape=(face(ny), face(ny), face(2), face(...]
    ppermute x1, waiting for transfers between devices: 1.97 us -> 1.41 us  [on_device(): lax.ppermute(one, 'sy', [(i, i ^ bit) for i in range(n_y)])]
  transfers between devices with their start and end apart: 6 -> 6, of which waited for: 2 -> 2; matrix products, arithmetic and copies ran while one was open for 0% -> 0% of each run, Pallas kernels for 20% -> 23%
where the time goes in v3:
time: 39 us; the launch traced here: 38.8 us
  starting transfers between devices  14.3 us (37%)
  Pallas kernels  12.2 us (31%)
  waiting for transfers between devices  7.75 us (20%)
  local copies, waits for them, and re-layouts  3.1 us (8%)
  between operations  1.41 us (4%)
    ppermute x5, starting transfers between devices, swap(): return lax.ppermute(values, axis, pairs(lax.axis_size(axis), first))  11.6 us
    pallas_call x1, Pallas kernels, own(): pl.pallas_call(own_kernel, out_shape=jax.ShapeDtypeStruct((rows, rows), F...  7.78 us
    ppermute x5, waiting for transfers between devices, swap(): return lax.ppermute(values, axis, pairs(lax.axis_size(axis), first))  6.34 us
    unnamed x10, local copies, waits for them, and re-layouts  3.1 us
    ppermute x1, starting transfers between devices, on_device(): lax.ppermute(one, 'sy', [(i, i ^ bit) for i in range(n_y)])  2.65 us
    pallas_call x1, Pallas kernels, couple(): pl.pallas_call(lambda *refs: couple_kernel(masks, *refs), out_shape=(bloc...  1.85 us
    ppermute x1, waiting for transfers between devices, on_device(): lax.ppermute(one, 'sy', [(i, i ^ bit) for i in range(n_y)])  1.41 us
    pallas_call x1, Pallas kernels, edges(): pl.pallas_call(edge_kernel, out_shape=(face(ny), face(ny), face(2), face(...  1.39 us
  transfers between devices with their start and end apart: 6, of which 2 were waited for; matrix products, arithmetic and copies ran while one was open for 0% of the time, Pallas kernels for 23%

profile of v3, /device:TPU:12, one launch (start us, length us, event | category | flops | bytes accessed | tf_op | source)
XLA Modules:
  0.0 38.8 jit_solution(2770438510373373153)
XLA Ops:
  1.3 0.0 copy-start
  1.3 2.2 %copy-done = bf16[64,8,32,128]{3,2,1,0:T(8,128)(2,1)S(1)} copy-done((bf16[64,8,32,128]{3,2,1,0:T(8,128)(2,1)S(1)}, bf16[64,8,32,128]{3,2,1,0:T(8,128)(2,1)}, u32[]{:S(2)}) %copy-start) | copy-done | bytes 4194328
  3.5 0.0 copy-start.2
  3.5 0.9 %copy-done.2 = f32[8,32,128]{2,1,0:T(8,128)S(1)} copy-done((f32[8,32,128]{2,1,0:T(8,128)S(1)}, f32[8,32,128]{2,1,0:T(8,128)}, u32[]{:S(2)}) %copy-start.2) | copy-done | bytes 131096
  4.4 0.0 copy-start.1
  4.4 0.0 copy-start.3
  4.4 0.0 copy-start.4
  4.4 1.4 %edges.1 = (bf16[32,64,128]{2,1,0:T(8,128)(2,1)S(1)}, bf16[32,64,128]{2,1,0:T(8,128)(2,1)S(1)}, bf16[2,64,128]{2,1,0:T(8,128)(2,1)S(1)}, bf16[8,64,128]{2,1,0:T(8,128)(2,1)S(1)}, bf16[8,64,128]{2,1,0:T(8,128)(2,1)S(1)}) custom-call(s32[1,1]{1,0:T(1,128)S(6)} %copy.8.cnt_any.rest_0_.refs_9_, bf16[64,8,32,128]{3,2,1,0:T(8,128)(2,1)S(1)} %copy-done, ...), custom_call_target="tpu_custom_call" | custom-call | flops 1000000 | bytes 4000000 | tf_op jit(solution)/shard_map/edges/pallas_call | solution.py:77
  5.8 0.1 collective-permute-start
  5.9 3.4 %collective-permute-start.1 = (bf16[32,64,128]{2,1,0:T(8,128)(2,1)S(1)}, bf16[32,64,128]{2,1,0:T(8,128)(2,1)S(1)}, u32[]{:S(2)}, u32[]{:S(2)}) collective-permute-start(bf16[32,64,128]{2,1,0:T(8,128)(2,1)S(1)} %get-tuple-element.20.fxb), channel_id=1, source_target_pairs={{4,8},{8,4},{12,16},{16,12},{20,24},{24,20},{5,9},{9,5},{13,17},{1... | collective-permute-start | bytes 1572872 | tf_op jit(solution)/shard_map/ppermute | solution.py:313
  9.3 3.0 %collective-permute-start.2 = (bf16[2,64,128]{2,1,0:T(8,128)(2,1)S(1)}, bf16[2,64,128]{2,1,0:T(8,128)(2,1)S(1)}, u32[]{:S(2)}, u32[]{:S(2)}) collective-permute-start(bf16[2,64,128]{2,1,0:T(8,128)(2,1)S(1)} %get-tuple-element.28), channel_id=1, source_target_pairs={{4,8},{8,4},{12,16},{16,12},{20,24},{24,20},{5,9},{9,5},{13,17},{1... | collective-permute-start | bytes 98312 | tf_op jit(solution)/shard_map/ppermute | solution.py:313
  12.3 2.7 %collective-permute-start.3 = (s32[1,1]{1,0:T(1,128)}, s32[1,1]{1,0:T(1,128)}, u32[]{:S(2)}, u32[]{:S(2)}) collective-permute-start(s32[1,1]{1,0:T(1,128)} %param.7), channel_id=1, source_target_pairs={{0,2},{1,3},{2,0},{3,1},{4,6},{5,7},{6,4},{7,5},{8,10},{9,11},{10,... | collective-permute-start | bytes 20 | tf_op jit(solution)/shard_map/ppermute | solution.py:320
  15.0 0.5 %smooth.1 = (bf16[32,64,128]{2,1,0:T(8,128)(2,1)S(1)}, bf16[32,64,128]{2,1,0:T(8,128)(2,1)S(1)}, bf16[8,64,128]{2,1,0:T(8,128)(2,1)S(1)}, bf16[8,64,128]{2,1,0:T(8,128)(2,1)S(1)}, bf16[4,64,128]{2,1,0:T(8,128)(2,1)S(1)}) custom-call(bf16[32,64,128]{2,1,0:T(8,128)(2,1)S(1)} %get-tuple-element.19.fxa, bf16[32,64,128]{2,1,0:T(8,128)(2,1)S(1)} %get-tuple-element.20.fxb, ...), custom_call_target="tpu_custom_call" | custom-call | flops 100000000 | bytes 2000000 | tf_op jit(solution)/shard_map/smooth/pallas_call | solution.py:157
  15.5 1.4 %collective-permute-done.3.rest_1_.refs_10_ = s32[1,1]{1,0:T(1,128)} collective-permute-done((s32[1,1]{1,0:T(1,128)}, s32[1,1]{1,0:T(1,128)}, u32[]{:S(2)}, u32[]{:S(2)}) %collective-permute-start.3) | collective-permute-done | bytes 36 | tf_op jit(solution)/shard_map/ppermute | solution.py:320
  17.0 6.3 %collective-permute-done.2.rxc = bf16[2,64,128]{2,1,0:T(8,128)(2,1)S(1)} collective-permute-done((bf16[2,64,128]{2,1,0:T(8,128)(2,1)S(1)}, bf16[2,64,128]{2,1,0:T(8,128)(2,1)S(1)}, u32[]{:S(2)}, u32[]{:S(2)}) %collective-permute-start.2) | collective-permute-done | bytes 32800 | tf_op jit(solution)/shard_map/ppermute | solution.py:313
  23.3 0.0 collective-permute-done.rxa.refs_5_
  23.3 0.7 %pack.1 = (bf16[11,64,128]{2,1,0:T(8,128)(2,1)S(1)}, bf16[11,64,128]{2,1,0:T(8,128)(2,1)S(1)}) custom-call(bf16[8,64,128]{2,1,0:T(8,128)(2,1)S(1)} %get-tuple-element.21.fya, bf16[8,64,128]{2,1,0:T(8,128)(2,1)S(1)} %get-tuple-element.22.fyb, bf16[32,64,128]{2,1,0:T(8,128)(2,1)S(1)} %collective-permute-done.rxa.refs_5_, ...), custom_call_target="tpu_custom_call" | custom-call | flops 100000 | bytes 1000000 | tf_op jit(solution)/shard_map/pack/pallas_call | solution.py:114
  24.0 0.1 collective-permute-start.4
  24.0 5.0 %collective-permute-start.5 = (bf16[11,64,128]{2,1,0:T(8,128)(2,1)S(1)}, bf16[11,64,128]{2,1,0:T(8,128)(2,1)S(1)}, u32[]{:S(2)}, u32[]{:S(2)}) collective-permute-start(bf16[11,64,128]{2,1,0:T(8,128)(2,1)S(1)} %get-tuple-element.30), channel_id=1, source_target_pairs={{1,2},{2,1},{5,6},{6,5},{9,10},{10,9},{13,14},{14,13},{17,18},{18,... | collective-permute-start | bytes 540680 | tf_op jit(solution)/shard_map/ppermute | solution.py:313
  29.1 0.0 copy-done.1
  29.1 0.0 copy-done.3
  29.1 0.0 copy-done.4
  29.1 7.8 %own.1 = f32[64,64]{1,0:T(8,128)} custom-call(s32[1,1]{1,0:T(1,128)S(6)} %copy.8.cnt_any.rest_0_.refs_9_, bf16[64,8,32,128]{3,2,1,0:T(8,128)(2,1)S(1)} %copy-done.1, f32[8,32,128]{2,1,0:T(8,128)S(1)} %copy-done.3, f32[8,32,128]{2,1,0:T(8,128)S(1)} %copy-done.4), custom_call_target="tpu_custom_call" | custom-call | flops 2000000000 | bytes 8000000 | tf_op jit(solution)/shard_map/own/pallas_call | solution.py:233
  36.9 0.0 collective-permute-done.1.refs_6_
  36.9 0.0 collective-permute-done.4.refs_7_
  36.9 0.0 collective-permute-done.5.refs_8_
  36.9 1.9 %couple.1 = (f32[64,256]{1,0:T(8,128)}, f32[64,256]{1,0:T(8,128)}, s32[1,1]{1,0:T(1,128)}) custom-call(bf16[32,64,128]{2,1,0:T(8,128)(2,1)S(1)} %get-tuple-element.23.refs_0_, bf16[32,64,128]{2,1,0:T(8,128)(2,1)S(1)} %get-tuple-element.24.refs_1_, bf16[8,64,128]{2,1,0:T(8,128)(2,1)S(1)} %get-tuple-element.25.refs_2_, ...), custom_call_target="tpu_custom_call" | custom-call | flops 100000000 | bytes 1000000 | tf_op jit(solution)/shard_map/couple/pallas_call | solution.py:301
Async XLA Ops:
  1.3 2.2 %copy-start = (bf16[64,8,32,128]{3,2,1,0:T(8,128)(2,1)S(1)}, bf16[64,8,32,128]{3,2,1,0:T(8,128)(2,1)}, u32[]{:S(2)}) copy-start(bf16[64,8,32,128]{3,2,1,0:T(8,128)(2,1)} %v.3) | copy-start | bytes 12582916
  3.5 0.9 %copy-start.2 = (f32[8,32,128]{2,1,0:T(8,128)S(1)}, f32[8,32,128]{2,1,0:T(8,128)}, u32[]{:S(2)}) copy-start(f32[8,32,128]{2,1,0:T(8,128)} %s.3) | copy-start | bytes 393220
  4.4 24.7 %copy-start.1 = (bf16[64,8,32,128]{3,2,1,0:T(8,128)(2,1)S(1)}, bf16[64,8,32,128]{3,2,1,0:T(8,128)(2,1)}, u32[]{:S(2)}) copy-start(bf16[64,8,32,128]{3,2,1,0:T(8,128)(2,1)} %v.3) | copy-start | bytes 12582916
  4.4 24.7 %copy-start.3 = (f32[8,32,128]{2,1,0:T(8,128)S(1)}, f32[8,32,128]{2,1,0:T(8,128)}, u32[]{:S(2)}) copy-start(f32[8,32,128]{2,1,0:T(8,128)} %s.3) | copy-start | bytes 393220
  4.4 24.7 %copy-start.4 = (f32[8,32,128]{2,1,0:T(8,128)S(1)}, f32[8,32,128]{2,1,0:T(8,128)}, u32[]{:S(2)}) copy-start(f32[8,32,128]{2,1,0:T(8,128)} %d.1) | copy-start | bytes 393220
  5.8 17.5 %collective-permute-start = (bf16[32,64,128]{2,1,0:T(8,128)(2,1)S(1)}, bf16[32,64,128]{2,1,0:T(8,128)(2,1)S(1)}, u32[]{:S(2)}, u32[]{:S(2)}) collective-permute-start(bf16[32,64,128]{2,1,0:T(8,128)(2,1)S(1)} %get-tuple-element.19.fxa), channel_id=1, source_target_pairs={{0,4},{4,0},{8,12},{12,8},{16,20},{20,16},{24,28},{28,24},{1,5},{5... | collective-permute-start | bytes 1572872 | tf_op jit(solution)/shard_map/ppermute | solution.py:313
  5.9 31.0 %collective-permute-start.1 = (bf16[32,64,128]{2,1,0:T(8,128)(2,1)S(1)}, bf16[32,64,128]{2,1,0:T(8,128)(2,1)S(1)}, u32[]{:S(2)}, u32[]{:S(2)}) collective-permute-start(bf16[32,64,128]{2,1,0:T(8,128)(2,1)S(1)} %get-tuple-element.20.fxb), channel_id=1, source_target_pairs={{4,8},{8,4},{12,16},{16,12},{20,24},{24,20},{5,9},{9,5},{13,17},{1... | collective-permute-start | bytes 1572872 | tf_op jit(solution)/shard_map/ppermute | solution.py:313
  9.3 14.0 %collective-permute-start.2 = (bf16[2,64,128]{2,1,0:T(8,128)(2,1)S(1)}, bf16[2,64,128]{2,1,0:T(8,128)(2,1)S(1)}, u32[]{:S(2)}, u32[]{:S(2)}) collective-permute-start(bf16[2,64,128]{2,1,0:T(8,128)(2,1)S(1)} %get-tuple-element.28), channel_id=1, source_target_pairs={{4,8},{8,4},{12,16},{16,12},{20,24},{24,20},{5,9},{9,5},{13,17},{1... | collective-permute-start | bytes 98312 | tf_op jit(solution)/shard_map/ppermute | solution.py:313
  12.3 4.6 %collective-permute-start.3 = (s32[1,1]{1,0:T(1,128)}, s32[1,1]{1,0:T(1,128)}, u32[]{:S(2)}, u32[]{:S(2)}) collective-permute-start(s32[1,1]{1,0:T(1,128)} %param.7), channel_id=1, source_target_pairs={{0,2},{1,3},{2,0},{3,1},{4,6},{5,7},{6,4},{7,5},{8,10},{9,11},{10,... | collective-permute-start | bytes 20 | tf_op jit(solution)/shard_map/ppermute | solution.py:320
  24.0 13.0 %collective-permute-start.4 = (bf16[11,64,128]{2,1,0:T(8,128)(2,1)S(1)}, bf16[11,64,128]{2,1,0:T(8,128)(2,1)S(1)}, u32[]{:S(2)}, u32[]{:S(2)}) collective-permute-start(bf16[11,64,128]{2,1,0:T(8,128)(2,1)S(1)} %get-tuple-element.29), channel_id=1, source_target_pairs={{0,1},{1,0},{2,3},{3,2},{4,5},{5,4},{6,7},{7,6},{8,9},{9,8},{10,11... | collective-permute-start | bytes 540680 | tf_op jit(solution)/shard_map/ppermute | solution.py:313
  24.0 12.9 %collective-permute-start.5 = (bf16[11,64,128]{2,1,0:T(8,128)(2,1)S(1)}, bf16[11,64,128]{2,1,0:T(8,128)(2,1)S(1)}, u32[]{:S(2)}, u32[]{:S(2)}) collective-permute-start(bf16[11,64,128]{2,1,0:T(8,128)(2,1)S(1)} %get-tuple-element.30), channel_id=1, source_target_pairs={{1,2},{2,1},{5,6},{6,5},{9,10},{10,9},{13,14},{14,13},{17,18},{18,... | collective-permute-start | bytes 540680 | tf_op jit(solution)/shard_map/ppermute | solution.py:313

commit v4 on v3

v4 whole, which is shorter than its diff:
```python
import jax
import jax.numpy as jnp
from jax import lax
from jax.experimental import pallas as pl
from jax.experimental.pallas import tpu as pltpu
from jax.sharding import PartitionSpec as P

F32 = jnp.float32
BF = jnp.bfloat16
NT = (((1,), (1,)), ((), ()))
NN = (((1,), (0,)), ((), ()))
PAD = 4
BAND = 8
VM = pl.BlockSpec(memory_space=pltpu.VMEM)
SM = pl.BlockSpec(memory_space=pltpu.SMEM)
ANY = pl.BlockSpec(memory_space=pl.ANY)
HBM = pl.BlockSpec(memory_space=pltpu.HBM)


def cost(flops, bytes_accessed):
    return pl.CostEstimate(flops=flops, bytes_accessed=bytes_accessed, transcendentals=0)


def tri(n, reps, scale):
    size = n * reps
    i = lax.broadcasted_iota(jnp.int32, (size, size), 0)
    j = lax.broadcasted_iota(jnp.int32, (size, size), 1)
    near = ((i // n) == (j // n)) & (jnp.abs(i - j) == 1)
    return (jnp.where(i == j, 1.0, jnp.where(near, 0.5, 0.0)) * scale).astype(BF)


def even(axis):
    return lax.rem(lax.axis_index(axis), 2) == 0


def pairs(count, first):
    steps = []
    for i in range(first, count - 1, 2):
        steps += [(i, i + 1), (i + 1, i)]
    return steps


def edge_kernel(cnt, v, s, fxa, fxb, fxc, fya, fyb, rx, ry):
    rows, nx, ny, nz = v.shape
    stx, sty = ny + PAD, BAND + PAD
    x_even, y_even = even("sx"), even("sy")
    xa = jnp.where(x_even, nx - 1, 0)
    ya = jnp.where(y_even, ny - 1, 0)
    xb, yb = nx - 1 - xa, ny - 1 - ya
    live = lax.broadcasted_iota(jnp.int32, (rows, nz), 0) < jnp.broadcast_to(cnt[...], (rows, nz))

    def scaled(m, stiff):
        return jnp.where(live, m * jnp.broadcast_to(stiff, (rows, nz)), 0.0).astype(BF)

    for x, out in ((xb, fxb), (xa, fxa)):
        for a in range(rows):
            rx[a * stx : a * stx + ny, :] = v[a, x].astype(F32)
        for y in range(ny):
            out[y] = scaled(rx[pl.ds(y, rows, stride=stx), :], s[x, pl.ds(y, 1), :])
    fxc[0] = fxb[ya]
    fxc[1] = fxb[yb]
    for y, out in ((ya, fya), (yb, fyb)):
        band = pl.multiple_of((y // BAND) * BAND, BAND)
        inner = y - band
        for x in range(nx):
            for a in range(rows):
                ry[x, a * sty : a * sty + BAND, :] = v[a, x, pl.ds(band, BAND), :].astype(F32)
            out[x] = scaled(ry[x, pl.ds(inner, rows, stride=sty), :], s[x, pl.ds(y, 1), :])


def edges(counts, vectors, stiff):
    rows, nx, ny, nz = vectors.shape
    face = lambda n: jax.ShapeDtypeStruct((n, rows, nz), BF)
    return pl.pallas_call(
        edge_kernel,
        out_shape=(face(ny), face(ny), face(2), face(nx), face(nx)),
        in_specs=[VM, VM, VM],
        out_specs=(VM,) * 5,
        scratch_shapes=[
            pltpu.VMEM((rows * (ny + PAD), nz), F32),
            pltpu.VMEM((nx, rows * (BAND + PAD), nz), F32),
        ],
        cost_estimate=cost(10**6, 4 * 10**6),
        compiler_params=pltpu.CompilerParams(vmem_limit_bytes=12 * 2**20),
        name="edges",
    )(counts, vectors, stiff)


def pack_kernel(cnt, fya, fyb, rxa, rxc, mya, myb):
    nx, rows, nz = fya.shape
    ny = rxa.shape[0]
    hi = jnp.where(even("sy"), ny - 1, 0)
    count = jnp.broadcast_to(cnt[...].astype(F32), (rows, nz)).astype(BF)
    for i, (src, y, out) in enumerate(((fya, hi, mya), (fyb, ny - 1 - hi, myb))):
        out[0:nx] = src[...]
        out[nx] = rxa[y]
        out[nx + 1] = rxc[i]
        out[nx + 2] = count


def pack(counts, fya, fyb, rxa, rxc):
    nx, rows, nz = fya.shape
    out = jax.ShapeDtypeStruct((nx + 3, rows, nz), BF)
    return pl.pallas_call(
        pack_kernel,
        out_shape=(out, out),
        in_specs=[VM] * 5,
        out_specs=(VM, VM),
        cost_estimate=cost(10**5, 10**6),
        compiler_params=pltpu.CompilerParams(vmem_limit_bytes=8 * 2**20),
        name="pack",
    )(counts, fya, fyb, rxa, rxc)


def along_z(stack, n, stencil):
    rows, nz = stack(0).shape
    wide = jnp.concatenate([jnp.concatenate([stack(2 * c), stack(2 * c + 1)], 1) for c in range(n // 2)], 0)
    z = lax.dot_general(wide, stencil, NN, preferred_element_type=F32)
    return [z[(i // 2) * rows : (i // 2 + 1) * rows, (i % 2) * nz : (i % 2 + 1) * nz] for i in range(n)]


def smooth_kernel(fxa, fxb, fya, fyb, wxa, wxb, wya, wyb, wc):
    ny, _, nz = fxa.shape
    stencil = tri(nz, 2, -0.25)
    for src, out in ((fxa, wxa), (fxb, wxb), (fya, wya), (fyb, wyb)):
        n = src.shape[0]
        zs = along_z(lambda i: src[i], n, stencil)
        for i in range(n):
            t = zs[i] + zs[i]
            if i > 0:
                t = t + zs[i - 1]
            if i < n - 1:
                t = t + zs[i + 1]
            out[i] = t.astype(BF)
    y_even = even("sy")
    rows_y = (jnp.where(y_even, ny - 1, 0), jnp.where(y_even, 0, ny - 1))
    for i, src in enumerate((fxa, fxb)):
        zs = along_z(lambda k: src[rows_y[k]], 2, stencil)
        for k in range(2):
            wc[2 * i + k] = zs[k].astype(BF)


def smooth(fxa, fxb, fya, fyb):
    ny, rows, nz = fxa.shape
    nx = fya.shape[0]
    face = lambda n: jax.ShapeDtypeStruct((n, rows, nz), BF)
    return pl.pallas_call(
        smooth_kernel,
        out_shape=(face(ny), face(ny), face(nx), face(nx), face(4)),
        in_specs=[VM] * 4,
        out_specs=(VM,) * 5,
        cost_estimate=cost(10**8, 2 * 10**6),
        compiler_params=pltpu.CompilerParams(vmem_limit_bytes=12 * 2**20),
        name="smooth",
    )(fxa, fxb, fya, fyb)


def own_kernel(cnt, v, s, d, own, r, er, ubuf, acc, accs):
    rows, nx, ny, nz = v.shape
    st = ny + PAD
    er[...] = d[...] + s[...] * s[...]
    for ref in (ubuf, acc, accs):
        ref[...] = jnp.zeros_like(ref)
    inner = jnp.where(lax.broadcasted_iota(jnp.int32, (rows, nz), 1) == 0, 0.0, 1.0).astype(BF)

    def with_previous(p):
        return p + pltpu.roll(p, 1, 1) * inner

    def dot(left, right, total):
        return total + lax.dot_general(
            jnp.concatenate(left, 1), jnp.concatenate(right, 1), NT, preferred_element_type=F32
        )

    def slab(x, total, stotal):
        if x is not None:
            for a in range(rows):
                r[a * st : a * st + ny, :] = v[a, x].astype(F32)
        last = None
        left, right, ps = [], [], []
        for y in range(ny):
            if x is not None:
                m = r[pl.ds(y, rows, stride=st), :]
                u = (m * jnp.broadcast_to(s[x, pl.ds(y, 1), :], (rows, nz))).astype(BF)
                left.append((m * jnp.broadcast_to(er[x, pl.ds(y, 1), :], (rows, nz))).astype(BF))
                right.append(m.astype(BF))
                both = u + ubuf[y]
                ubuf[y] = u
            else:
                both = ubuf[y]
            ps.append(both if last is None else both + last)
            last = both
            if y % 2:
                if x is not None:
                    total = dot(left, right, total)
                stotal = dot([with_previous(p) for p in ps], ps, stotal)
                left, right, ps = [], [], []
        return total, dot([with_previous(last)], [last], stotal)

    @pl.loop(0, nx)
    def _(x):
        acc[...], accs[...] = slab(x, acc[...], accs[...])

    _, q = slab(None, None, accs[...])
    total = acc[...] - 0.125 * (q + q.T)
    live = jnp.broadcast_to(cnt[...], (rows, rows))
    keep = (lax.broadcasted_iota(jnp.int32, (rows, rows), 0) < live) & (
        lax.broadcasted_iota(jnp.int32, (rows, rows), 1) < live
    )
    own[...] = jnp.where(keep, total, 0.0)


def own(counts, vectors, stiff, diag):
    rows, nx, ny, nz = vectors.shape
    return pl.pallas_call(
        own_kernel,
        out_shape=jax.ShapeDtypeStruct((rows, rows), F32),
        in_specs=[VM] * 4,
        out_specs=VM,
        scratch_shapes=[
            pltpu.VMEM((rows * (ny + PAD), nz), F32),
            pltpu.VMEM((nx, ny, nz), F32),
            pltpu.VMEM((ny, rows, nz), BF),
            pltpu.VMEM((rows, rows), F32),
            pltpu.VMEM((rows, rows), F32),
        ],
        compiler_params=pltpu.CompilerParams(vmem_limit_bytes=16 * 2**20),
        cost_estimate=cost(2 * 10**9, 8 * 10**6),
        name="own",
    )(counts, vectors, stiff, diag)


def gram(left, right, n, total):
    for i in range(0, n, 2):
        total += lax.dot_general(
            jnp.concatenate([left[i], left[i + 1]], 1),
            jnp.concatenate([right[i], right[i + 1]], 1),
            NT,
            preferred_element_type=F32,
        )
    return total


def across_y_kernel(cnt, wya, wyb, wc, rya, ryb, faces, corners, two):
    nx, rows, _ = wya.shape
    x_even, y_even = even("sx"), even("sy")
    zero = jnp.zeros((rows, rows), F32)
    ya, yb = gram(wya, rya, nx, zero), gram(wyb, ryb, nx, zero)
    around = [
        [lax.dot_general(wc[2 * i + k], ry[nx + i], NT, preferred_element_type=F32) for k, ry in enumerate((rya, ryb))]
        for i in range(2)
    ]
    faces[:, 0:rows] = jnp.where(y_even, yb, ya)
    faces[:, rows : 2 * rows] = jnp.where(y_even, ya, yb)
    for ix in range(2):
        for iy in range(2):
            options = [jnp.where(y_even == (iy == 1), around[k][0], around[k][1]) for k in range(2)]
            i = 2 * ix + iy
            corners[:, i * rows : (i + 1) * rows] = jnp.where(x_even == (ix == 1), options[0], options[1])
    lane = lax.broadcasted_iota(jnp.int32, two.shape, 1)
    beside = rya[nx + 2].astype(F32)[0:8].astype(jnp.int32)
    two[...] = jnp.where(lane == 0, jnp.broadcast_to(cnt[...], two.shape), beside)


def across_y(counts, wya, wyb, wc, rya, ryb):
    rows, nz = wya.shape[1:]
    return pl.pallas_call(
        across_y_kernel,
        out_shape=(
            jax.ShapeDtypeStruct((rows, 2 * rows), F32),
            jax.ShapeDtypeStruct((rows, 4 * rows), F32),
            jax.ShapeDtypeStruct((8, nz), jnp.int32),
        ),
        in_specs=[VM] * 6,
        out_specs=(VM,) * 3,
        cost_estimate=cost(10**7, 10**6),
        compiler_params=pltpu.CompilerParams(vmem_limit_bytes=8 * 2**20),
        name="across_y",
    )(counts, wya, wyb, wc, rya, ryb)


def across_x_kernel(fy, wxa, wxb, rxa, rxb, faces):
    n, rows, _ = wxa.shape
    zero = jnp.zeros((rows, rows), F32)
    xa, xb = gram(wxa, rxa, n, zero), gram(wxb, rxb, n, zero)
    x_even = even("sx")
    faces[:, 0:rows] = jnp.where(x_even, xb, xa)
    faces[:, rows : 2 * rows] = jnp.where(x_even, xa, xb)
    faces[:, 2 * rows : 4 * rows] = fy[...]


def across_x(fy, wxa, wxb, rxa, rxb):
    rows = wxa.shape[1]
    return pl.pallas_call(
        across_x_kernel,
        out_shape=jax.ShapeDtypeStruct((rows, 4 * rows), F32),
        in_specs=[VM] * 5,
        out_specs=VM,
        cost_estimate=cost(10**8, 2 * 10**6),
        compiler_params=pltpu.CompilerParams(vmem_limit_bytes=8 * 2**20),
        name="across_x",
    )(fy, wxa, wxb, rxa, rxb)


def offset_kernel(masks, *refs):
    *known, offsets = refs
    me = lax.axis_index("sy")
    lane = lax.broadcasted_iota(jnp.int32, known[0].shape, 1)
    total = jnp.zeros(known[0].shape, F32)
    for one, mask in zip(known, masks):
        source = (me ^ mask) ^ lane
        total += jnp.where((lane < 2) & (source < me), one[...], 0).astype(F32)
    offsets[...] = jnp.sum(total, axis=1, keepdims=True)[0:1].astype(jnp.int32)


def offset_of(masks, known):
    return pl.pallas_call(
        lambda *refs: offset_kernel(masks, *refs),
        out_shape=jax.ShapeDtypeStruct((1, 1), jnp.int32),
        in_specs=[VM] * len(known),
        out_specs=VM,
        cost_estimate=cost(10**3, 10**4),
        compiler_params=pltpu.CompilerParams(vmem_limit_bytes=4 * 2**20),
        name="offset_of",
    )(*known)


def swap(values, axis, first):
    return lax.ppermute(values, axis, pairs(lax.axis_size(axis), first))


def on_device(vectors, root_stiff, diag_coef, counts):
    n_y = lax.axis_size("sy")
    fxa, fxb, fxc, fya, fyb = edges(counts, vectors, root_stiff)
    rxa = swap(fxa, "sx", 0)
    rxc = swap(fxc, "sx", 1)
    rxb = swap(fxb, "sx", 1)
    wxa, wxb, wya, wyb, wc = smooth(fxa, fxb, fya, fyb)
    mya, myb = pack(counts, fya, fyb, rxa, rxc)
    rya = swap(mya, "sy", 0)
    ryb = swap(myb, "sy", 1)
    own_block = own(counts, vectors, root_stiff, diag_coef)
    fy, corners, two = across_y(counts, wya, wyb, wc, rya, ryb)
    known, masks, bit = [two], [0], 2
    while bit < n_y:
        known += [lax.ppermute(one, "sy", [(i, i ^ bit) for i in range(n_y)]) for one in known]
        masks += [m ^ bit for m in masks]
        bit *= 2
    faces = across_x(fy, wxa, wxb, rxa, rxb)
    offsets = offset_of(tuple(masks), known)
    return own_block[None, None], faces[None, None], corners[None, None], offsets


def solution(mesh):
    assert mesh.shape["sy"] & (mesh.shape["sy"] - 1) == 0
    return jax.shard_map(
        on_device,
        mesh=mesh,
        in_specs=(
            P(None, "sx", "sy", None),
            P("sx", "sy", None),
            P("sx", "sy", None),
            P("sx", "sy"),
        ),
        out_specs=(
            P("sx", "sy", None, None),
            P("sx", "sy", None, None),
            P("sx", "sy", None, None),
            P("sx", "sy"),
        ),
        check_vma=False,
    )
```

time: 39 us -> 40.4 us (1.036)
  waiting for transfers between devices: 7.75 us -> 13.7 us
  starting transfers between devices: 14.3 us -> 11.7 us
  Pallas kernels: 12.2 us -> 10.3 us
    ppermute x5, waiting for transfers between devices: 6.34 us -> 10.3 us  [swap(): return lax.ppermute(values, axis, pairs(lax.axis_size(axis), first))]
    ppermute x1, starting transfers between devices: 2.65 us -> 0.01 us  [on_device(): lax.ppermute(one, 'sy', [(i, i ^ bit) for i in range(n_y)])]
    ppermute x1, waiting for transfers between devices: 1.41 us -> 3.39 us  [on_device(): lax.ppermute(one, 'sy', [(i, i ^ bit) for i in range(n_y)])]
    pallas_call x1, Pallas kernels: 7.78 us -> 6.18 us  [own(): pl.pallas_call(own_kernel, out_shape=jax.ShapeDtypeStruct((rows, rows), F...]
    pallas_call x1, Pallas kernels: 1.39 us -> 0.86 us  [edges(): pl.pallas_call(edge_kernel, out_shape=(face(ny), face(ny), face(2), face(...]
    pallas_call x2 -> x4, Pallas kernels: 2.51 us -> 2.74 us  [the longest x1 1.11 us: across_x(): pl.pallas_call(across_x_kernel, out_shape=jax.ShapeDtypeStruct((rows, 4 *...]
    unnamed x10 -> x8, local copies, waits for them, and re-layouts: 3.1 us -> 3.09 us
  transfers between devices with their start and end apart: 6 -> 6, of which waited for: 2 -> 2; matrix products, arithmetic and copies ran while one was open for 0% -> 0% of each run, Pallas kernels for 23% -> 22%
where the time goes in v4:
time: 40.4 us; the launch traced here: 40.2 us
  waiting for transfers between devices  13.7 us (34%)
  starting transfers between devices  11.7 us (29%)
  Pallas kernels  10.3 us (25%)
  local copies, waits for them, and re-layouts  3.09 us (8%)
  between operations  1.36 us (3%)
    ppermute x5, starting transfers between devices, swap(): return lax.ppermute(values, axis, pairs(lax.axis_size(axis), first))  11.7 us
    ppermute x5, waiting for transfers between devices, swap(): return lax.ppermute(values, axis, pairs(lax.axis_size(axis), first))  10.3 us
    pallas_call x1, Pallas kernels, own(): pl.pallas_call(own_kernel, out_shape=jax.ShapeDtypeStruct((rows, rows), F...  6.18 us
    ppermute x1, waiting for transfers between devices, on_device(): lax.ppermute(one, 'sy', [(i, i ^ bit) for i in range(n_y)])  3.39 us
    unnamed x8, local copies, waits for them, and re-layouts  3.09 us
    pallas_call x1, Pallas kernels, across_x(): pl.pallas_call(across_x_kernel, out_shape=jax.ShapeDtypeStruct((rows, 4 *...  1.11 us
    pallas_call x1, Pallas kernels, across_y(): pl.pallas_call(across_y_kernel, out_shape=(jax.ShapeDtypeStruct((rows, 2...  0.96 us
    pallas_call x1, Pallas kernels, edges(): pl.pallas_call(edge_kernel, out_shape=(face(ny), face(ny), face(2), face(...  0.86 us
  transfers between devices with their start and end apart: 6, of which 2 were waited for; matrix products, arithmetic and copies ran while one was open for 0% of the time, Pallas kernels for 22%

profile of v4, /device:TPU:12, one launch (start us, length us, event | category | flops | bytes accessed | tf_op | source)
XLA Modules:
  0.0 40.2 jit_solution(15864874258327888928)
XLA Ops:
  1.3 0.0 copy-start
  1.3 2.2 %copy-done = bf16[64,8,32,128]{3,2,1,0:T(8,128)(2,1)S(1)} copy-done((bf16[64,8,32,128]{3,2,1,0:T(8,128)(2,1)S(1)}, bf16[64,8,32,128]{3,2,1,0:T(8,128)(2,1)}, u32[]{:S(2)}) %copy-start) | copy-done | bytes 4194328
  3.5 0.0 copy-start.2
  3.5 0.9 %copy-done.2 = f32[8,32,128]{2,1,0:T(8,128)S(1)} copy-done((f32[8,32,128]{2,1,0:T(8,128)S(1)}, f32[8,32,128]{2,1,0:T(8,128)}, u32[]{:S(2)}) %copy-start.2) | copy-done | bytes 131096
  4.4 0.0 copy-start.1
  4.4 0.0 copy-start.3
  4.4 0.9 %edges.1 = (bf16[32,64,128]{2,1,0:T(8,128)(2,1)S(1)}, bf16[32,64,128]{2,1,0:T(8,128)(2,1)S(1)}, bf16[2,64,128]{2,1,0:T(8,128)(2,1)S(1)}, bf16[8,64,128]{2,1,0:T(8,128)(2,1)S(1)}, bf16[8,64,128]{2,1,0:T(8,128)(2,1)S(1)}) custom-call(s32[1,1]{1,0:T(1,128)S(6)} %copy.8.cnt, bf16[64,8,32,128]{3,2,1,0:T(8,128)(2,1)S(1)} %copy-done, f32[8,32,128]{2,1,0:T(8,128)S(1)} %copy-done.2), custom_call_target="tpu_custom_call" | custom-call | flops 1000000 | bytes 4000000 | tf_op jit(solution)/shard_map/edges/pallas_call | solution.py:74
  5.2 0.1 collective-permute-start
  5.3 3.4 %collective-permute-start.4 = (bf16[32,64,128]{2,1,0:T(8,128)(2,1)S(1)}, bf16[32,64,128]{2,1,0:T(8,128)(2,1)S(1)}, u32[]{:S(2)}, u32[]{:S(2)}) collective-permute-start(bf16[32,64,128]{2,1,0:T(8,128)(2,1)S(1)} %get-tuple-element.20.fxb), channel_id=1, source_target_pairs={{4,8},{8,4},{12,16},{16,12},{20,24},{24,20},{5,9},{9,5},{13,17},{1... | collective-permute-start | bytes 1572872 | tf_op jit(solution)/shard_map/ppermute | solution.py:328
  8.8 3.2 %collective-permute-start.1 = (bf16[2,64,128]{2,1,0:T(8,128)(2,1)S(1)}, bf16[2,64,128]{2,1,0:T(8,128)(2,1)S(1)}, u32[]{:S(2)}, u32[]{:S(2)}) collective-permute-start(bf16[2,64,128]{2,1,0:T(8,128)(2,1)S(1)} %get-tuple-element.26), channel_id=1, source_target_pairs={{4,8},{8,4},{12,16},{16,12},{20,24},{24,20},{5,9},{9,5},{13,17},{1... | collective-permute-start | bytes 98312 | tf_op jit(solution)/shard_map/ppermute | solution.py:328
  11.9 0.6 %smooth.1 = (bf16[32,64,128]{2,1,0:T(8,128)(2,1)S(1)}, bf16[32,64,128]{2,1,0:T(8,128)(2,1)S(1)}, bf16[8,64,128]{2,1,0:T(8,128)(2,1)S(1)}, bf16[8,64,128]{2,1,0:T(8,128)(2,1)S(1)}, bf16[4,64,128]{2,1,0:T(8,128)(2,1)S(1)}) custom-call(bf16[32,64,128]{2,1,0:T(8,128)(2,1)S(1)} %get-tuple-element.19.fxa, bf16[32,64,128]{2,1,0:T(8,128)(2,1)S(1)} %get-tuple-element.20.fxb, ...), custom_call_target="tpu_custom_call" | custom-call | flops 100000000 | bytes 2000000 | tf_op jit(solution)/shard_map/smooth/pallas_call | solution.py:147
  12.5 10.3 %collective-permute-done.1.rxc = bf16[2,64,128]{2,1,0:T(8,128)(2,1)S(1)} collective-permute-done((bf16[2,64,128]{2,1,0:T(8,128)(2,1)S(1)}, bf16[2,64,128]{2,1,0:T(8,128)(2,1)S(1)}, u32[]{:S(2)}, u32[]{:S(2)}) %collective-permute-start.1) | collective-permute-done | bytes 32800 | tf_op jit(solution)/shard_map/ppermute | solution.py:328
  22.8 0.0 collective-permute-done.rxa
  22.8 0.1 pack.1
  22.8 0.0 collective-permute-start.2
  22.9 5.0 %collective-permute-start.3 = (bf16[11,64,128]{2,1,0:T(8,128)(2,1)S(1)}, bf16[11,64,128]{2,1,0:T(8,128)(2,1)S(1)}, u32[]{:S(2)}, u32[]{:S(2)}) collective-permute-start(bf16[11,64,128]{2,1,0:T(8,128)(2,1)S(1)} %get-tuple-element.28), channel_id=1, source_target_pairs={{1,2},{2,1},{5,6},{6,5},{9,10},{10,9},{13,14},{14,13},{17,18},{18,... | collective-permute-start | bytes 540680 | tf_op jit(solution)/shard_map/ppermute | solution.py:328
  27.9 0.0 copy-done.1
  27.9 0.0 copy-done.3
  27.9 6.2 %own.1 = f32[64,64]{1,0:T(8,128)} custom-call(s32[1,1]{1,0:T(1,128)S(6)} %copy.8.cnt, bf16[64,8,32,128]{3,2,1,0:T(8,128)(2,1)S(1)} %copy-done.1, f32[8,32,128]{2,1,0:T(8,128)S(1)} %copy-done.2, f32[8,32,128]{2,1,0:T(8,128)S(1)} %copy-done.3), custom_call_target="tpu_custom_call" | custom-call | flops 2000000000 | bytes 8000000 | tf_op jit(solution)/shard_map/own/pallas_call | solution.py:214
  34.1 0.0 collective-permute-done.2.rya
  34.1 0.0 collective-permute-done.3.ryb
  34.1 1.0 %across_y.1 = (f32[64,128]{1,0:T(8,128)S(1)}, f32[64,256]{1,0:T(8,128)}, s32[8,128]{1,0:T(8,128)S(1)}) custom-call(s32[1,1]{1,0:T(1,128)S(6)} %copy.8.cnt, bf16[8,64,128]{2,1,0:T(8,128)(2,1)S(1)} %get-tuple-element.23.wya, bf16[8,64,128]{2,1,0:T(8,128)(2,1)S(1)} %get-tuple-element.24.wyb, bf16[4,64,128]{2,1,0:T(8,128)(2,1)S(1)} %get-tuple-element.25.wc, ...), custom_call_target="tpu_custom_call" | custom-call | flops 10000000 | bytes 1000000 | tf_op jit(solution)/shard_map/across_y/pallas_call | solution.py:266
  35.1 0.0 collective-permute-start.5
  35.1 0.0 collective-permute-done.4.rxb
  35.1 1.1 %across_x.1 = f32[64,256]{1,0:T(8,128)} custom-call(f32[64,128]{1,0:T(8,128)S(1)} %get-tuple-element.29.fy, bf16[32,64,128]{2,1,0:T(8,128)(2,1)S(1)} %get-tuple-element.30.wxa, bf16[32,64,128]{2,1,0:T(8,128)(2,1)S(1)} %get-tuple-element.31.wxb, bf16[32,64,128]{2,1,0:T(8,128)(2,1)S(1)} %collective-permute-done.rxa, ...), custom_call_target="tpu_custom_call" | custom-call | flops 100000000 | bytes 2000000 | tf_op jit(solution)/shard_map/across_x/pallas_call | solution.py:293
  36.2 3.4 %collective-permute-done.5.refs_1_ = s32[8,128]{1,0:T(8,128)S(1)} collective-permute-done((s32[8,128]{1,0:T(8,128)S(1)}, s32[8,128]{1,0:T(8,128)S(1)}, u32[]{:S(2)}, u32[]{:S(2)}) %collective-permute-start.5) | collective-permute-done | bytes 4128 | tf_op jit(solution)/shard_map/ppermute | solution.py:345
  39.6 0.6 %offset_of.1 = s32[1,1]{1,0:T(1,128)} custom-call(s32[8,128]{1,0:T(8,128)S(1)} %get-tuple-element.33.refs_0_, s32[8,128]{1,0:T(8,128)S(1)} %collective-permute-done.5.refs_1_), custom_call_target="tpu_custom_call" | custom-call | flops 1000 | bytes 10000 | tf_op jit(solution)/shard_map/offset_of/pallas_call | solution.py:316
Async XLA Ops:
  1.3 2.2 %copy-start = (bf16[64,8,32,128]{3,2,1,0:T(8,128)(2,1)S(1)}, bf16[64,8,32,128]{3,2,1,0:T(8,128)(2,1)}, u32[]{:S(2)}) copy-start(bf16[64,8,32,128]{3,2,1,0:T(8,128)(2,1)} %v.3) | copy-start | bytes 12582916
  3.5 0.9 %copy-start.2 = (f32[8,32,128]{2,1,0:T(8,128)S(1)}, f32[8,32,128]{2,1,0:T(8,128)}, u32[]{:S(2)}) copy-start(f32[8,32,128]{2,1,0:T(8,128)} %s.3) | copy-start | bytes 393220
  4.4 23.5 %copy-start.1 = (bf16[64,8,32,128]{3,2,1,0:T(8,128)(2,1)S(1)}, bf16[64,8,32,128]{3,2,1,0:T(8,128)(2,1)}, u32[]{:S(2)}) copy-start(bf16[64,8,32,128]{3,2,1,0:T(8,128)(2,1)} %v.3) | copy-start | bytes 12582916
  4.4 23.5 %copy-start.3 = (f32[8,32,128]{2,1,0:T(8,128)S(1)}, f32[8,32,128]{2,1,0:T(8,128)}, u32[]{:S(2)}) copy-start(f32[8,32,128]{2,1,0:T(8,128)} %d.1) | copy-start | bytes 393220
  5.2 17.5 %collective-permute-start = (bf16[32,64,128]{2,1,0:T(8,128)(2,1)S(1)}, bf16[32,64,128]{2,1,0:T(8,128)(2,1)S(1)}, u32[]{:S(2)}, u32[]{:S(2)}) collective-permute-start(bf16[32,64,128]{2,1,0:T(8,128)(2,1)S(1)} %get-tuple-element.19.fxa), channel_id=1, source_target_pairs={{0,4},{4,0},{8,12},{12,8},{16,20},{20,16},{24,28},{28,24},{1,5},{5... | collective-permute-start | bytes 1572872 | tf_op jit(solution)/shard_map/ppermute | solution.py:328
  5.3 29.8 %collective-permute-start.4 = (bf16[32,64,128]{2,1,0:T(8,128)(2,1)S(1)}, bf16[32,64,128]{2,1,0:T(8,128)(2,1)S(1)}, u32[]{:S(2)}, u32[]{:S(2)}) collective-permute-start(bf16[32,64,128]{2,1,0:T(8,128)(2,1)S(1)} %get-tuple-element.20.fxb), channel_id=1, source_target_pairs={{4,8},{8,4},{12,16},{16,12},{20,24},{24,20},{5,9},{9,5},{13,17},{1... | collective-permute-start | bytes 1572872 | tf_op jit(solution)/shard_map/ppermute | solution.py:328
  8.8 14.0 %collective-permute-start.1 = (bf16[2,64,128]{2,1,0:T(8,128)(2,1)S(1)}, bf16[2,64,128]{2,1,0:T(8,128)(2,1)S(1)}, u32[]{:S(2)}, u32[]{:S(2)}) collective-permute-start(bf16[2,64,128]{2,1,0:T(8,128)(2,1)S(1)} %get-tuple-element.26), channel_id=1, source_target_pairs={{4,8},{8,4},{12,16},{16,12},{20,24},{24,20},{5,9},{9,5},{13,17},{1... | collective-permute-start | bytes 98312 | tf_op jit(solution)/shard_map/ppermute | solution.py:328
  22.8 11.3 %collective-permute-start.2 = (bf16[11,64,128]{2,1,0:T(8,128)(2,1)S(1)}, bf16[11,64,128]{2,1,0:T(8,128)(2,1)S(1)}, u32[]{:S(2)}, u32[]{:S(2)}) collective-permute-start(bf16[11,64,128]{2,1,0:T(8,128)(2,1)S(1)} %get-tuple-element.27), channel_id=1, source_target_pairs={{0,1},{1,0},{2,3},{3,2},{4,5},{5,4},{6,7},{7,6},{8,9},{9,8},{10,11... | collective-permute-start | bytes 540680 | tf_op jit(solution)/shard_map/ppermute | solution.py:328
  22.9 11.2 %collective-permute-start.3 = (bf16[11,64,128]{2,1,0:T(8,128)(2,1)S(1)}, bf16[11,64,128]{2,1,0:T(8,128)(2,1)S(1)}, u32[]{:S(2)}, u32[]{:S(2)}) collective-permute-start(bf16[11,64,128]{2,1,0:T(8,128)(2,1)S(1)} %get-tuple-element.28), channel_id=1, source_target_pairs={{1,2},{2,1},{5,6},{6,5},{9,10},{10,9},{13,14},{14,13},{17,18},{18,... | collective-permute-start | bytes 540680 | tf_op jit(solution)/shard_map/ppermute | solution.py:328
  35.1 4.5 %collective-permute-start.5 = (s32[8,128]{1,0:T(8,128)S(1)}, s32[8,128]{1,0:T(8,128)S(1)}, u32[]{:S(2)}, u32[]{:S(2)}) collective-permute-start(s32[8,128]{1,0:T(8,128)S(1)} %get-tuple-element.33.refs_0_), channel_id=1, source_target_pairs={{0,2},{1,3},{2,0},{3,1},{4,6},{5,7},{6,4},{7,5},{8,10},{9,11},{10,... | collective-permute-start | bytes 12296 | tf_op jit(solution)/shard_map/ppermute | solution.py:345

commit v5 on v4

--- a/solution.py
+++ b/solution.py
@@ -40,31 +40,48 @@
     return steps
 
 
-def edge_kernel(cnt, v, s, fxa, fxb, fxc, fya, fyb, rx, ry):
+def edge_kernel(cnt, v, s_any, fxa, fxb, fxc, fya, fyb, rx, ry, s, xbuf, ybuf, sem):
     rows, nx, ny, nz = v.shape
     stx, sty = ny + PAD, BAND + PAD
     x_even, y_even = even("sx"), even("sy")
     xa = jnp.where(x_even, nx - 1, 0)
     ya = jnp.where(y_even, ny - 1, 0)
     xb, yb = nx - 1 - xa, ny - 1 - ya
+    bands = [pl.multiple_of((y // BAND) * BAND, BAND) for y in (ya, yb)]
+    copies = [
+        pltpu.make_async_copy(src, dst, sem.at[i])
+        for i, (src, dst) in enumerate(
+            (
+                (s_any, s),
+                (v.at[:, xb], xbuf.at[0]),
+                (v.at[:, xa], xbuf.at[1]),
+                (v.at[:, :, pl.ds(bands[0], BAND)], ybuf.at[0]),
+                (v.at[:, :, pl.ds(bands[1], BAND)], ybuf.at[1]),
+            )
+        )
+    ]
+    for c in copies:
+        c.start()
     live = lax.broadcasted_iota(jnp.int32, (rows, nz), 0) < jnp.broadcast_to(cnt[...], (rows, nz))
 
     def scaled(m, stiff):
         return jnp.where(live, m * jnp.broadcast_to(stiff, (rows, nz)), 0.0).astype(BF)
 
-    for x, out in ((xb, fxb), (xa, fxa)):
+    copies[0].wait()
+    for i, (x, out) in enumerate(((xb, fxb), (xa, fxa))):
+        copies[1 + i].wait()
         for a in range(rows):
-            rx[a * stx : a * stx + ny, :] = v[a, x].astype(F32)
+            rx[a * stx : a * stx + ny, :] = xbuf[i, a].astype(F32)
         for y in range(ny):
             out[y] = scaled(rx[pl.ds(y, rows, stride=stx), :], s[x, pl.ds(y, 1), :])
     fxc[0] = fxb[ya]
     fxc[1] = fxb[yb]
-    for y, out in ((ya, fya), (yb, fyb)):
-        band = pl.multiple_of((y // BAND) * BAND, BAND)
-        inner = y - band
+    for i, (y, out) in enumerate(((ya, fya), (yb, fyb))):
+        copies[3 + i].wait()
+        inner = y - bands[i]
         for x in range(nx):
             for a in range(rows):
-                ry[x, a * sty : a * sty + BAND, :] = v[a, x, pl.ds(band, BAND), :].astype(F32)
+                ry[x, a * sty : a * sty + BAND, :] = ybuf[i, a, x].astype(F32)
             out[x] = scaled(ry[x, pl.ds(inner, rows, stride=sty), :], s[x, pl.ds(y, 1), :])
 
 
@@ -74,14 +91,18 @@
     return pl.pallas_call(
         edge_kernel,
         out_shape=(face(ny), face(ny), face(2), face(nx), face(nx)),
-        in_specs=[VM, VM, VM],
+        in_specs=[VM, HBM, HBM],
         out_specs=(VM,) * 5,
         scratch_shapes=[
             pltpu.VMEM((rows * (ny + PAD), nz), F32),
             pltpu.VMEM((nx, rows * (BAND + PAD), nz), F32),
+            pltpu.VMEM(stiff.shape, F32),
+            pltpu.VMEM((2, rows, ny, nz), BF),
+            pltpu.VMEM((2, rows, nx, BAND, nz), BF),
+            pltpu.SemaphoreType.DMA((5,)),
         ],
         cost_estimate=cost(10**6, 4 * 10**6),
-        compiler_params=pltpu.CompilerParams(vmem_limit_bytes=12 * 2**20),
+        compiler_params=pltpu.CompilerParams(vmem_limit_bytes=52 * 2**20),
         name="edges",
     )(counts, vectors, stiff)
 
@@ -155,12 +176,10 @@
     )(fxa, fxb, fya, fyb)
 
 
-def own_kernel(cnt, v, s, d, own, r, er, ubuf, acc, accs):
-    rows, nx, ny, nz = v.shape
+def own_kernel(first, stop, v, s, d, ubuf, acc, accs, r, er):
+    rows, _, ny, nz = v.shape
     st = ny + PAD
     er[...] = d[...] + s[...] * s[...]
-    for ref in (ubuf, acc, accs):
-        ref[...] = jnp.zeros_like(ref)
     inner = jnp.where(lax.broadcasted_iota(jnp.int32, (rows, nz), 1) == 0, 0.0, 1.0).astype(BF)
 
     def with_previous(p):
@@ -196,10 +215,24 @@
                 left, right, ps = [], [], []
         return total, dot([with_previous(last)], [last], stotal)
 
-    @pl.loop(0, nx)
+    @pl.loop(first, stop)
     def _(x):
         acc[...], accs[...] = slab(x, acc[...], accs[...])
 
+    return slab
+
+
+def own_begin_kernel(stop, v, s, d, ubuf, acc, accs, r, er):
+    for ref in (ubuf, acc, accs):
+        ref[...] = jnp.zeros_like(ref)
+    own_kernel(0, stop, v, s, d, ubuf, acc, accs, r, er)
+
+
+def own_end_kernel(first, cnt, v, s, d, ubuf0, acc0, accs0, own, ubuf, acc, accs, r, er):
+    for src, ref in ((ubuf0, ubuf), (acc0, acc), (accs0, accs)):
+        ref[...] = src[...]
+    rows, nx = v.shape[:2]
+    slab = own_kernel(first, nx, v, s, d, ubuf, acc, accs, r, er)
     _, q = slab(None, None, accs[...])
     total = acc[...] - 0.125 * (q + q.T)
     live = jnp.broadcast_to(cnt[...], (rows, rows))
@@ -209,24 +242,42 @@
     own[...] = jnp.where(keep, total, 0.0)
 
 
-def own(counts, vectors, stiff, diag):
+def own_parts(vectors):
     rows, nx, ny, nz = vectors.shape
-    return pl.pallas_call(
-        own_kernel,
+    state = [((ny, rows, nz), BF), ((rows, rows), F32), ((rows, rows), F32)]
+    work = [pltpu.VMEM((rows * (ny + PAD), nz), F32), pltpu.VMEM((nx, ny, nz), F32)]
+    params = dict(
+        cost_estimate=cost(10**9, 5 * 10**6),
+        compiler_params=pltpu.CompilerParams(vmem_limit_bytes=16 * 2**20),
+    )
+    return state, work, params
+
+
+def own_begin(cut, vectors, stiff, diag):
+    state, work, params = own_parts(vectors)
+    return pl.pallas_call(
+        lambda *refs: own_begin_kernel(cut, *refs),
+        out_shape=tuple(jax.ShapeDtypeStruct(*one) for one in state),
+        in_specs=[VM] * 3,
+        out_specs=(VM,) * 3,
+        scratch_shapes=work,
+        name="own_begin",
+        **params,
+    )(vectors, stiff, diag)
+
+
+def own_end(cut, counts, vectors, stiff, diag, so_far):
+    state, work, params = own_parts(vectors)
+    rows = vectors.shape[0]
+    return pl.pallas_call(
+        lambda *refs: own_end_kernel(cut, *refs),
         out_shape=jax.ShapeDtypeStruct((rows, rows), F32),
-        in_specs=[VM] * 4,
+        in_specs=[VM] * 7,
         out_specs=VM,
-        scratch_shapes=[
-            pltpu.VMEM((rows * (ny + PAD), nz), F32),
-            pltpu.VMEM((nx, ny, nz), F32),
-            pltpu.VMEM((ny, rows, nz), BF),
-            pltpu.VMEM((rows, rows), F32),
-            pltpu.VMEM((rows, rows), F32),
-        ],
-        compiler_params=pltpu.CompilerParams(vmem_limit_bytes=16 * 2**20),
-        cost_estimate=cost(2 * 10**9, 8 * 10**6),
-        name="own",
-    )(counts, vectors, stiff, diag)
+        scratch_shapes=[pltpu.VMEM(*one) for one in state] + work,
+        name="own_end",
+        **params,
+    )(counts, vectors, stiff, diag, *so_far)
 
 
 def gram(left, right, n, total):
@@ -240,7 +291,8 @@
     return total
 
 
-def across_y_kernel(cnt, wya, wyb, wc, rya, ryb, faces, corners, two):
+def across_y_kernel(masks, fx, wya, wyb, wc, rya, ryb, *rest):
+    *known, faces, corners, offsets = rest
     nx, rows, _ = wya.shape
     x_even, y_even = even("sx"), even("sy")
     zero = jnp.zeros((rows, rows), F32)
@@ -249,56 +301,72 @@
         [lax.dot_general(wc[2 * i + k], ry[nx + i], NT, preferred_element_type=F32) for k, ry in enumerate((rya, ryb))]
         for i in range(2)
     ]
-    faces[:, 0:rows] = jnp.where(y_even, yb, ya)
-    faces[:, rows : 2 * rows] = jnp.where(y_even, ya, yb)
+    faces[:, 0 : 2 * rows] = fx[...]
+    faces[:, 2 * rows : 3 * rows] = jnp.where(y_even, yb, ya)
+    faces[:, 3 * rows : 4 * rows] = jnp.where(y_even, ya, yb)
+    offset_kernel(masks, *known, offsets)
     for ix in range(2):
         for iy in range(2):
             options = [jnp.where(y_even == (iy == 1), around[k][0], around[k][1]) for k in range(2)]
             i = 2 * ix + iy
             corners[:, i * rows : (i + 1) * rows] = jnp.where(x_even == (ix == 1), options[0], options[1])
+
+
+def two_kernel(cnt, rya, two):
     lane = lax.broadcasted_iota(jnp.int32, two.shape, 1)
-    beside = rya[nx + 2].astype(F32)[0:8].astype(jnp.int32)
+    beside = rya[rya.shape[0] - 1].astype(F32)[0 : two.shape[0]].astype(jnp.int32)
     two[...] = jnp.where(lane == 0, jnp.broadcast_to(cnt[...], two.shape), beside)
 
 
-def across_y(counts, wya, wyb, wc, rya, ryb):
-    rows, nz = wya.shape[1:]
-    return pl.pallas_call(
-        across_y_kernel,
+def two_counts(counts, rya):
+    return pl.pallas_call(
+        two_kernel,
+        out_shape=jax.ShapeDtypeStruct((8, rya.shape[2]), jnp.int32),
+        in_specs=[VM] * 2,
+        out_specs=VM,
+        cost_estimate=cost(10**4, 10**4),
+        compiler_params=pltpu.CompilerParams(vmem_limit_bytes=8 * 2**20),
+        name="two_counts",
+    )(counts, rya)
+
+
+def across_y(masks, fx, wya, wyb, wc, rya, ryb, known):
+    rows = wya.shape[1]
+    return pl.pallas_call(
+        lambda *refs: across_y_kernel(masks, *refs),
         out_shape=(
-            jax.ShapeDtypeStruct((rows, 2 * rows), F32),
             jax.ShapeDtypeStruct((rows, 4 * rows), F32),
-            jax.ShapeDtypeStruct((8, nz), jnp.int32),
+            jax.ShapeDtypeStruct((rows, 4 * rows), F32),
+            jax.ShapeDtypeStruct((1, 1), jnp.int32),
         ),
-        in_specs=[VM] * 6,
+        in_specs=[VM] * (6 + len(known)),
         out_specs=(VM,) * 3,
         cost_estimate=cost(10**7, 10**6),
         compiler_params=pltpu.CompilerParams(vmem_limit_bytes=8 * 2**20),
         name="across_y",
-    )(counts, wya, wyb, wc, rya, ryb)
-
-
-def across_x_kernel(fy, wxa, wxb, rxa, rxb, faces):
+    )(fx, wya, wyb, wc, rya, ryb, *known)
+
+
+def across_x_kernel(wxa, wxb, rxa, rxb, faces):
     n, rows, _ = wxa.shape
     zero = jnp.zeros((rows, rows), F32)
     xa, xb = gram(wxa, rxa, n, zero), gram(wxb, rxb, n, zero)
     x_even = even("sx")
     faces[:, 0:rows] = jnp.where(x_even, xb, xa)
     faces[:, rows : 2 * rows] = jnp.where(x_even, xa, xb)
-    faces[:, 2 * rows : 4 * rows] = fy[...]
-
-
-def across_x(fy, wxa, wxb, rxa, rxb):
+
+
+def across_x(wxa, wxb, rxa, rxb):
     rows = wxa.shape[1]
     return pl.pallas_call(
         across_x_kernel,
-        out_shape=jax.ShapeDtypeStruct((rows, 4 * rows), F32),
-        in_specs=[VM] * 5,
+        out_shape=jax.ShapeDtypeStruct((rows, 2 * rows), F32),
+        in_specs=[VM] * 4,
         out_specs=VM,
         cost_estimate=cost(10**8, 2 * 10**6),
         compiler_params=pltpu.CompilerParams(vmem_limit_bytes=8 * 2**20),
         name="across_x",
-    )(fy, wxa, wxb, rxa, rxb)
+    )(wxa, wxb, rxa, rxb)
 
 
 def offset_kernel(masks, *refs):
@@ -312,18 +380,6 @@
     offsets[...] = jnp.sum(total, axis=1, keepdims=True)[0:1].astype(jnp.int32)
 
 
-def offset_of(masks, known):
-    return pl.pallas_call(
-        lambda *refs: offset_kernel(masks, *refs),
-        out_shape=jax.ShapeDtypeStruct((1, 1), jnp.int32),
-        in_specs=[VM] * len(known),
-        out_specs=VM,
-        cost_estimate=cost(10**3, 10**4),
-        compiler_params=pltpu.CompilerParams(vmem_limit_bytes=4 * 2**20),
-        name="offset_of",
-    )(*known)
-
-
 def swap(values, axis, first):
     return lax.ppermute(values, axis, pairs(lax.axis_size(axis), first))
 
@@ -331,22 +387,24 @@
 def on_device(vectors, root_stiff, diag_coef, counts):
     n_y = lax.axis_size("sy")
     fxa, fxb, fxc, fya, fyb = edges(counts, vectors, root_stiff)
-    rxa = swap(fxa, "sx", 0)
     rxc = swap(fxc, "sx", 1)
     rxb = swap(fxb, "sx", 1)
+    rxa = swap(fxa, "sx", 0)
     wxa, wxb, wya, wyb, wc = smooth(fxa, fxb, fya, fyb)
     mya, myb = pack(counts, fya, fyb, rxa, rxc)
     rya = swap(mya, "sy", 0)
+    cut = vectors.shape[1] // 2
+    so_far = own_begin(cut, vectors, root_stiff, diag_coef)
     ryb = swap(myb, "sy", 1)
-    own_block = own(counts, vectors, root_stiff, diag_coef)
-    fy, corners, two = across_y(counts, wya, wyb, wc, rya, ryb)
+    two = two_counts(counts, rya)
     known, masks, bit = [two], [0], 2
     while bit < n_y:
         known += [lax.ppermute(one, "sy", [(i, i ^ bit) for i in range(n_y)]) for one in known]
         masks += [m ^ bit for m in masks]
         bit *= 2
-    faces = across_x(fy, wxa, wxb, rxa, rxb)
-    offsets = offset_of(tuple(masks), known)
+    own_block = own_end(cut, counts, vectors, root_stiff, diag_coef, so_far)
+    fx = across_x(wxa, wxb, rxa, rxb)
+    faces, corners, offsets = across_y(tuple(masks), fx, wya, wyb, wc, rya, ryb, known)
     return own_block[None, None], faces[None, None], corners[None, None], offsets
 
 

time: 40.4 us -> 39.5 us (0.978)
  local copies, waits for them, and re-layouts: 3.09 us -> 1.07 us
  waiting for transfers between devices: 13.7 us -> 14.4 us
    unnamed x8 -> x6, local copies, waits for them, and re-layouts: 3.09 us -> 1.07 us
    pallas_call x1, Pallas kernels: 0.86 us -> 2.39 us  [edges(): pl.pallas_call(edge_kernel, out_shape=(face(ny), face(ny), face(2), face(...]
    pallas_call x4 -> x5, Pallas kernels: 8.84 us -> 7.7 us  [the longest x1 3.64 us: own_end(): pl.pallas_call(lambda *refs: own_end_kernel(cut, *refs), out_shape=jax.Sh...]
    ppermute x1, waiting for transfers between devices: 3.39 us -> 4 us  [on_device(): lax.ppermute(one, 'sy', [(i, i ^ bit) for i in range(n_y)])]
  transfers between devices with their start and end apart: 6 -> 6, of which waited for: 2 -> 2; matrix products, arithmetic and copies ran while one was open for 0% -> 0% of each run, Pallas kernels for 22% -> 19%
where the time goes in v5:
time: 39.5 us; the launch traced here: 39.3 us
  waiting for transfers between devices  14.4 us (36%)
  starting transfers between devices  11.6 us (29%)
  Pallas kernels  10.7 us (27%)
  between operations  1.55 us (4%)
  local copies, waits for them, and re-layouts  1.07 us (3%)
    ppermute x5, starting transfers between devices, swap(): return lax.ppermute(values, axis, pairs(lax.axis_size(axis), first))  11.6 us
    ppermute x5, waiting for transfers between devices, swap(): return lax.ppermute(values, axis, pairs(lax.axis_size(axis), first))  10.4 us
    ppermute x1, waiting for transfers between devices, on_device(): lax.ppermute(one, 'sy', [(i, i ^ bit) for i in range(n_y)])  4 us
    pallas_call x1, Pallas kernels, own_end(): pl.pallas_call(lambda *refs: own_end_kernel(cut, *refs), out_shape=jax.Sh...  3.64 us
    pallas_call x1, Pallas kernels, own_begin(): pl.pallas_call(lambda *refs: own_begin_kernel(cut, *refs), out_shape=tupl...  2.52 us
    pallas_call x1, Pallas kernels, edges(): pl.pallas_call(edge_kernel, out_shape=(face(ny), face(ny), face(2), face(...  2.39 us
    unnamed x6, local copies, waits for them, and re-layouts  1.07 us
    pallas_call x1, Pallas kernels, across_y(): pl.pallas_call(lambda *refs: across_y_kernel(masks, *refs), out_shape=(ja...  0.98 us
  transfers between devices with their start and end apart: 6, of which 2 were waited for; matrix products, arithmetic and copies ran while one was open for 0% of the time, Pallas kernels for 19%

profile of v5, /device:TPU:12, one launch (start us, length us, event | category | flops | bytes accessed | tf_op | source)
XLA Modules:
  0.0 39.3 jit_solution(14732501985663045334)
XLA Ops:
  0.6 0.0 copy-start
  1.4 0.0 copy-start.1
  1.4 1.1 %copy-done.1 = f32[8,32,128]{2,1,0:T(8,128)S(1)} copy-done((f32[8,32,128]{2,1,0:T(8,128)S(1)}, f32[8,32,128]{2,1,0:T(8,128)}, u32[]{:S(2)}) %copy-start.1) | copy-done | bytes 131096
  2.5 0.0 copy-start.2
  2.5 2.4 %edges.1 = (bf16[32,64,128]{2,1,0:T(8,128)(2,1)S(1)}, bf16[32,64,128]{2,1,0:T(8,128)(2,1)S(1)}, bf16[2,64,128]{2,1,0:T(8,128)(2,1)S(1)}, bf16[8,64,128]{2,1,0:T(8,128)(2,1)S(1)}, bf16[8,64,128]{2,1,0:T(8,128)(2,1)S(1)}) custom-call(s32[1,1]{1,0:T(1,128)S(6)} %copy.8.refs_0_.cnt, bf16[64,8,32,128]{3,2,1,0:T(8,128)(2,1)} %v.1, f32[8,32,128]{2,1,0:T(8,128)S(1)} %copy-done.1), custom_call_target="tpu_custom_call" | custom-call | flops 1000000 | bytes 4000000 | tf_op jit(solution)/shard_map/edges/pallas_call | solution.py:91
  4.9 0.1 collective-permute-start
  5.0 3.4 %collective-permute-start.1 = (bf16[32,64,128]{2,1,0:T(8,128)(2,1)S(1)}, bf16[32,64,128]{2,1,0:T(8,128)(2,1)S(1)}, u32[]{:S(2)}, u32[]{:S(2)}) collective-permute-start(bf16[32,64,128]{2,1,0:T(8,128)(2,1)S(1)} %get-tuple-element.26.fxb), channel_id=1, source_target_pairs={{4,8},{8,4},{12,16},{16,12},{20,24},{24,20},{5,9},{9,5},{13,17},{1... | collective-permute-start | bytes 1572872 | tf_op jit(solution)/shard_map/ppermute | solution.py:384
  8.4 3.0 %collective-permute-start.2 = (bf16[2,64,128]{2,1,0:T(8,128)(2,1)S(1)}, bf16[2,64,128]{2,1,0:T(8,128)(2,1)S(1)}, u32[]{:S(2)}, u32[]{:S(2)}) collective-permute-start(bf16[2,64,128]{2,1,0:T(8,128)(2,1)S(1)} %get-tuple-element.34), channel_id=1, source_target_pairs={{4,8},{8,4},{12,16},{16,12},{20,24},{24,20},{5,9},{9,5},{13,17},{1... | collective-permute-start | bytes 98312 | tf_op jit(solution)/shard_map/ppermute | solution.py:384
  11.5 0.6 %smooth.1 = (bf16[32,64,128]{2,1,0:T(8,128)(2,1)S(1)}, bf16[32,64,128]{2,1,0:T(8,128)(2,1)S(1)}, bf16[8,64,128]{2,1,0:T(8,128)(2,1)S(1)}, bf16[8,64,128]{2,1,0:T(8,128)(2,1)S(1)}, bf16[4,64,128]{2,1,0:T(8,128)(2,1)S(1)}) custom-call(bf16[32,64,128]{2,1,0:T(8,128)(2,1)S(1)} %get-tuple-element.25.fxa, bf16[32,64,128]{2,1,0:T(8,128)(2,1)S(1)} %get-tuple-element.26.fxb, ...), custom_call_target="tpu_custom_call" | custom-call | flops 100000000 | bytes 2000000 | tf_op jit(solution)/shard_map/smooth/pallas_call | solution.py:168
  12.0 10.4 %collective-permute-done.2.rxc = bf16[2,64,128]{2,1,0:T(8,128)(2,1)S(1)} collective-permute-done((bf16[2,64,128]{2,1,0:T(8,128)(2,1)S(1)}, bf16[2,64,128]{2,1,0:T(8,128)(2,1)S(1)}, u32[]{:S(2)}, u32[]{:S(2)}) %collective-permute-start.2) | collective-permute-done | bytes 32800 | tf_op jit(solution)/shard_map/ppermute | solution.py:384
  22.4 0.0 collective-permute-done.rxa
  22.4 0.1 pack.1
  22.5 0.0 collective-permute-start.3
  22.5 5.0 %collective-permute-start.4 = (bf16[11,64,128]{2,1,0:T(8,128)(2,1)S(1)}, bf16[11,64,128]{2,1,0:T(8,128)(2,1)S(1)}, u32[]{:S(2)}, u32[]{:S(2)}) collective-permute-start(bf16[11,64,128]{2,1,0:T(8,128)(2,1)S(1)} %get-tuple-element.36), channel_id=1, source_target_pairs={{1,2},{2,1},{5,6},{6,5},{9,10},{10,9},{13,14},{14,13},{17,18},{18,... | collective-permute-start | bytes 540680 | tf_op jit(solution)/shard_map/ppermute | solution.py:384
  27.6 0.0 copy-done
  27.6 0.0 copy-done.2
  27.6 2.5 %own_begin.1 = (bf16[32,64,128]{2,1,0:T(8,128)(2,1)S(1)}, f32[64,64]{1,0:T(8,128)S(1)}, f32[64,64]{1,0:T(8,128)S(1)}) custom-call(bf16[64,8,32,128]{3,2,1,0:T(8,128)(2,1)S(1)} %copy-done, f32[8,32,128]{2,1,0:T(8,128)S(1)} %copy-done.1, f32[8,32,128]{2,1,0:T(8,128)S(1)} %copy-done.2), custom_call_target="tpu_custom_call" | custom-call | flops 1000000000 | bytes 5000000 | tf_op jit(solution)/shard_map/own_begin/pallas_call | solution.py:258
  30.1 3.6 %own_end.1 = f32[64,64]{1,0:T(8,128)} custom-call(s32[1,1]{1,0:T(1,128)S(6)} %copy.8.refs_0_.cnt, bf16[64,8,32,128]{3,2,1,0:T(8,128)(2,1)S(1)} %copy-done, f32[8,32,128]{2,1,0:T(8,128)S(1)} %copy-done.1, f32[8,32,128]{2,1,0:T(8,128)S(1)} %copy-done.2, bf16[32,64,128]{2,1,0:T(8,128)(2,1)S(1)} %get-tuple-element.22.refs_4_, ...), custom_call_target="tpu_custom_call" | custom-call | flops 1000000000 | bytes 5000000 | tf_op jit(solution)/shard_map/own_end/pallas_call | solution.py:272
  33.8 0.0 collective-permute-done.3.rya.refs_4_
  33.8 0.1 two_counts.1.refs_6_
  33.8 0.0 collective-permute-start.5
  33.8 0.0 collective-permute-done.1.rxb
  33.9 0.5 %across_x.1.refs_0_ = f32[64,128]{1,0:T(8,128)S(1)} custom-call(bf16[32,64,128]{2,1,0:T(8,128)(2,1)S(1)} %get-tuple-element.29.wxa, bf16[32,64,128]{2,1,0:T(8,128)(2,1)S(1)} %get-tuple-element.30.wxb, bf16[32,64,128]{2,1,0:T(8,128)(2,1)S(1)} %collective-permute-done.rxa, bf16[32,64,128]{2,1,0:T(8,128)(2,1)S(1)} %collective-permute-done.1.rxb), custom_call_target="tpu_custom_call" | custom-call | flops 100000000 | bytes 2000000 | tf_op jit(solution)/shard_map/across_x/pallas_call | solution.py:361
  34.3 0.0 collective-permute-done.4.refs_5_
  34.3 4.0 %collective-permute-done.5.refs_7_ = s32[8,128]{1,0:T(8,128)S(1)} collective-permute-done((s32[8,128]{1,0:T(8,128)S(1)}, s32[8,128]{1,0:T(8,128)S(1)}, u32[]{:S(2)}, u32[]{:S(2)}) %collective-permute-start.5) | collective-permute-done | bytes 4128 | tf_op jit(solution)/shard_map/ppermute | solution.py:402
  38.3 1.0 %across_y.1 = (f32[64,256]{1,0:T(8,128)}, f32[64,256]{1,0:T(8,128)}, s32[1,1]{1,0:T(1,128)}) custom-call(f32[64,128]{1,0:T(8,128)S(1)} %across_x.1.refs_0_, bf16[8,64,128]{2,1,0:T(8,128)(2,1)S(1)} %get-tuple-element.31.refs_1_, bf16[8,64,128]{2,1,0:T(8,128)(2,1)S(1)} %get-tuple-element.32.refs_2_, bf16[4,64,128]{2,1,0:T(8,128)(2,1)S(1)} %get-tuple-element.33.refs_3_, ...), custom_call_target="tpu_custom_call" | custom-call | flops 10000000 | bytes 1000000 | tf_op jit(solution)/shard_map/across_y/pallas_call | solution.py:335
Async XLA Ops:
  0.6 26.9 %copy-start = (bf16[64,8,32,128]{3,2,1,0:T(8,128)(2,1)S(1)}, bf16[64,8,32,128]{3,2,1,0:T(8,128)(2,1)}, u32[]{:S(2)}) copy-start(bf16[64,8,32,128]{3,2,1,0:T(8,128)(2,1)} %v.1) | copy-start | bytes 12582916
  1.4 1.1 %copy-start.1 = (f32[8,32,128]{2,1,0:T(8,128)S(1)}, f32[8,32,128]{2,1,0:T(8,128)}, u32[]{:S(2)}) copy-start(f32[8,32,128]{2,1,0:T(8,128)} %s_any.1) | copy-start | bytes 393220
  2.5 25.1 %copy-start.2 = (f32[8,32,128]{2,1,0:T(8,128)S(1)}, f32[8,32,128]{2,1,0:T(8,128)}, u32[]{:S(2)}) copy-start(f32[8,32,128]{2,1,0:T(8,128)} %refs_3_.1) | copy-start | bytes 393220
  4.9 17.5 %collective-permute-start = (bf16[32,64,128]{2,1,0:T(8,128)(2,1)S(1)}, bf16[32,64,128]{2,1,0:T(8,128)(2,1)S(1)}, u32[]{:S(2)}, u32[]{:S(2)}) collective-permute-start(bf16[32,64,128]{2,1,0:T(8,128)(2,1)S(1)} %get-tuple-element.25.fxa), channel_id=1, source_target_pairs={{0,4},{4,0},{8,12},{12,8},{16,20},{20,16},{24,28},{28,24},{1,5},{5... | collective-permute-start | bytes 1572872 | tf_op jit(solution)/shard_map/ppermute | solution.py:384
  5.0 28.9 %collective-permute-start.1 = (bf16[32,64,128]{2,1,0:T(8,128)(2,1)S(1)}, bf16[32,64,128]{2,1,0:T(8,128)(2,1)S(1)}, u32[]{:S(2)}, u32[]{:S(2)}) collective-permute-start(bf16[32,64,128]{2,1,0:T(8,128)(2,1)S(1)} %get-tuple-element.26.fxb), channel_id=1, source_target_pairs={{4,8},{8,4},{12,16},{16,12},{20,24},{24,20},{5,9},{9,5},{13,17},{1... | collective-permute-start | bytes 1572872 | tf_op jit(solution)/shard_map/ppermute | solution.py:384
  8.4 14.0 %collective-permute-start.2 = (bf16[2,64,128]{2,1,0:T(8,128)(2,1)S(1)}, bf16[2,64,128]{2,1,0:T(8,128)(2,1)S(1)}, u32[]{:S(2)}, u32[]{:S(2)}) collective-permute-start(bf16[2,64,128]{2,1,0:T(8,128)(2,1)S(1)} %get-tuple-element.34), channel_id=1, source_target_pairs={{4,8},{8,4},{12,16},{16,12},{20,24},{24,20},{5,9},{9,5},{13,17},{1... | collective-permute-start | bytes 98312 | tf_op jit(solution)/shard_map/ppermute | solution.py:384
  22.5 11.3 %collective-permute-start.3 = (bf16[11,64,128]{2,1,0:T(8,128)(2,1)S(1)}, bf16[11,64,128]{2,1,0:T(8,128)(2,1)S(1)}, u32[]{:S(2)}, u32[]{:S(2)}) collective-permute-start(bf16[11,64,128]{2,1,0:T(8,128)(2,1)S(1)} %get-tuple-element.35), channel_id=1, source_target_pairs={{0,1},{1,0},{2,3},{3,2},{4,5},{5,4},{6,7},{7,6},{8,9},{9,8},{10,11... | collective-permute-start | bytes 540680 | tf_op jit(solution)/shard_map/ppermute | solution.py:384
  22.5 11.8 %collective-permute-start.4 = (bf16[11,64,128]{2,1,0:T(8,128)(2,1)S(1)}, bf16[11,64,128]{2,1,0:T(8,128)(2,1)S(1)}, u32[]{:S(2)}, u32[]{:S(2)}) collective-permute-start(bf16[11,64,128]{2,1,0:T(8,128)(2,1)S(1)} %get-tuple-element.36), channel_id=1, source_target_pairs={{1,2},{2,1},{5,6},{6,5},{9,10},{10,9},{13,14},{14,13},{17,18},{18,... | collective-permute-start | bytes 540680 | tf_op jit(solution)/shard_map/ppermute | solution.py:384
  33.8 4.5 %collective-permute-start.5 = (s32[8,128]{1,0:T(8,128)S(1)}, s32[8,128]{1,0:T(8,128)S(1)}, u32[]{:S(2)}, u32[]{:S(2)}) collective-permute-start(s32[8,128]{1,0:T(8,128)S(1)} %two_counts.1.refs_6_), channel_id=1, source_target_pairs={{0,2},{1,3},{2,0},{3,1},{4,6},{5,7},{6,4},{7,5},{8,10},{9,11},{10,... | collective-permute-start | bytes 12296 | tf_op jit(solution)/shard_map/ppermute | solution.py:402

commit v6 on v5

--- a/solution.py
+++ b/solution.py
@@ -73,9 +73,13 @@
         for a in range(rows):
             rx[a * stx : a * stx + ny, :] = xbuf[i, a].astype(F32)
         for y in range(ny):
-            out[y] = scaled(rx[pl.ds(y, rows, stride=stx), :], s[x, pl.ds(y, 1), :])
-    fxc[0] = fxb[ya]
-    fxc[1] = fxb[yb]
+            row = scaled(rx[pl.ds(y, rows, stride=stx), :], s[x, pl.ds(y, 1), :])
+            if i == 1:
+                out[y] = row
+            elif 0 < y < ny - 1:
+                out[y - 1] = row
+            else:
+                fxc[jnp.where(ya == y, 0, 1)] = row
     for i, (y, out) in enumerate(((ya, fya), (yb, fyb))):
         copies[3 + i].wait()
         inner = y - bands[i]
@@ -90,7 +94,7 @@
     face = lambda n: jax.ShapeDtypeStruct((n, rows, nz), BF)
     return pl.pallas_call(
         edge_kernel,
-        out_shape=(face(ny), face(ny), face(2), face(nx), face(nx)),
+        out_shape=(face(ny), face(ny - 2), face(2), face(nx), face(nx)),
         in_specs=[VM, HBM, HBM],
         out_specs=(VM,) * 5,
         scratch_shapes=[
@@ -140,40 +144,64 @@
     return [z[(i // 2) * rows : (i // 2 + 1) * rows, (i % 2) * nz : (i % 2 + 1) * nz] for i in range(n)]
 
 
-def smooth_kernel(fxa, fxb, fya, fyb, wxa, wxb, wya, wyb, wc):
+def smooth_kernel(fxa, fxb, fxc, fya, fyb, wxa, wxb, wxe, wya, wyb, wc):
     ny, _, nz = fxa.shape
     stencil = tri(nz, 2, -0.25)
-    for src, out in ((fxa, wxa), (fxb, wxb), (fya, wya), (fyb, wyb)):
-        n = src.shape[0]
-        zs = along_z(lambda i: src[i], n, stencil)
+    y_even = even("sy")
+    first, last = jnp.where(y_even, 1, 0), jnp.where(y_even, 0, 1)
+
+    def put_xb(i, value):
+        if 0 < i < ny - 1:
+            wxb[i - 1] = value
+        else:
+            wxe[first if i == 0 else last] = value
+
+    def get_xb(i):
+        return fxb[i - 1] if 0 < i < ny - 1 else fxc[first if i == 0 else last]
+
+    def getter(ref):
+        return lambda i: ref[i]
+
+    def putter(ref):
+        def put(i, value):
+            ref[i] = value
+
+        return put
+
+    for n, get, put in (
+        (ny, getter(fxa), putter(wxa)),
+        (ny, get_xb, put_xb),
+        (fya.shape[0], getter(fya), putter(wya)),
+        (fyb.shape[0], getter(fyb), putter(wyb)),
+    ):
+        zs = along_z(get, n, stencil)
         for i in range(n):
             t = zs[i] + zs[i]
             if i > 0:
                 t = t + zs[i - 1]
             if i < n - 1:
                 t = t + zs[i + 1]
-            out[i] = t.astype(BF)
-    y_even = even("sy")
+            put(i, t.astype(BF))
     rows_y = (jnp.where(y_even, ny - 1, 0), jnp.where(y_even, 0, ny - 1))
-    for i, src in enumerate((fxa, fxb)):
-        zs = along_z(lambda k: src[rows_y[k]], 2, stencil)
+    for i, get in enumerate((lambda k: fxa[rows_y[k]], lambda k: fxc[k])):
+        zs = along_z(get, 2, stencil)
         for k in range(2):
             wc[2 * i + k] = zs[k].astype(BF)
 
 
-def smooth(fxa, fxb, fya, fyb):
+def smooth(fxa, fxb, fxc, fya, fyb):
     ny, rows, nz = fxa.shape
     nx = fya.shape[0]
     face = lambda n: jax.ShapeDtypeStruct((n, rows, nz), BF)
     return pl.pallas_call(
         smooth_kernel,
-        out_shape=(face(ny), face(ny), face(nx), face(nx), face(4)),
-        in_specs=[VM] * 4,
-        out_specs=(VM,) * 5,
+        out_shape=(face(ny), face(ny - 2), face(2), face(nx), face(nx), face(4)),
+        in_specs=[VM] * 5,
+        out_specs=(VM,) * 6,
         cost_estimate=cost(10**8, 2 * 10**6),
         compiler_params=pltpu.CompilerParams(vmem_limit_bytes=12 * 2**20),
         name="smooth",
-    )(fxa, fxb, fya, fyb)
+    )(fxa, fxb, fxc, fya, fyb)
 
 
 def own_kernel(first, stop, v, s, d, ubuf, acc, accs, r, er):
@@ -347,26 +375,27 @@
     )(fx, wya, wyb, wc, rya, ryb, *known)
 
 
-def across_x_kernel(wxa, wxb, rxa, rxb, faces):
+def across_x_kernel(wxa, wxb, wxe, rxa, rxb, rxc, faces):
     n, rows, _ = wxa.shape
     zero = jnp.zeros((rows, rows), F32)
-    xa, xb = gram(wxa, rxa, n, zero), gram(wxb, rxb, n, zero)
+    xa = gram(wxa, rxa, n, zero)
+    xb = gram(wxb, rxb, n - 2, gram(wxe, rxc, 2, zero))
     x_even = even("sx")
     faces[:, 0:rows] = jnp.where(x_even, xb, xa)
     faces[:, rows : 2 * rows] = jnp.where(x_even, xa, xb)
 
 
-def across_x(wxa, wxb, rxa, rxb):
+def across_x(wxa, wxb, wxe, rxa, rxb, rxc):
     rows = wxa.shape[1]
     return pl.pallas_call(
         across_x_kernel,
         out_shape=jax.ShapeDtypeStruct((rows, 2 * rows), F32),
-        in_specs=[VM] * 4,
+        in_specs=[VM] * 6,
         out_specs=VM,
         cost_estimate=cost(10**8, 2 * 10**6),
         compiler_params=pltpu.CompilerParams(vmem_limit_bytes=8 * 2**20),
         name="across_x",
-    )(wxa, wxb, rxa, rxb)
+    )(wxa, wxb, wxe, rxa, rxb, rxc)
 
 
 def offset_kernel(masks, *refs):
@@ -390,10 +419,10 @@
     rxc = swap(fxc, "sx", 1)
     rxb = swap(fxb, "sx", 1)
     rxa = swap(fxa, "sx", 0)
-    wxa, wxb, wya, wyb, wc = smooth(fxa, fxb, fya, fyb)
+    wxa, wxb, wxe, wya, wyb, wc = smooth(fxa, fxb, fxc, fya, fyb)
     mya, myb = pack(counts, fya, fyb, rxa, rxc)
     rya = swap(mya, "sy", 0)
-    cut = vectors.shape[1] // 2
+    cut = vectors.shape[1] * 5 // 8
     so_far = own_begin(cut, vectors, root_stiff, diag_coef)
     ryb = swap(myb, "sy", 1)
     two = two_counts(counts, rya)
@@ -403,7 +432,7 @@
         masks += [m ^ bit for m in masks]
         bit *= 2
     own_block = own_end(cut, counts, vectors, root_stiff, diag_coef, so_far)
-    fx = across_x(wxa, wxb, rxa, rxb)
+    fx = across_x(wxa, wxb, wxe, rxa, rxb, rxc)
     faces, corners, offsets = across_y(tuple(masks), fx, wya, wyb, wc, rya, ryb, known)
     return own_block[None, None], faces[None, None], corners[None, None], offsets
 

time: 39.5 us -> 38.8 us (0.982)
  waiting for transfers between devices: 14.4 us -> 13.7 us
    ppermute x5, waiting for transfers between devices: 10.4 us -> 9.7 us  [swap(): return lax.ppermute(values, axis, pairs(lax.axis_size(axis), first))]
    pallas_call x1, Pallas kernels: 3.64 us -> 2.98 us  [own_end(): pl.pallas_call(lambda *refs: own_end_kernel(cut, *refs), out_shape=jax.Sh...]
    pallas_call x1, Pallas kernels: 2.52 us -> 3.14 us  [own_begin(): pl.pallas_call(lambda *refs: own_begin_kernel(cut, *refs), out_shape=tupl...]
where the time goes in v6:
time: 38.8 us; the launch traced here: 38.6 us
  waiting for transfers between devices  13.7 us (35%)
  starting transfers between devices  11.6 us (30%)
  Pallas kernels  10.7 us (28%)
  between operations  1.55 us (4%)
  local copies, waits for them, and re-layouts  1.07 us (3%)
    ppermute x5, starting transfers between devices, swap(): return lax.ppermute(values, axis, pairs(lax.axis_size(axis), first))  11.6 us
    ppermute x5, waiting for transfers between devices, swap(): return lax.ppermute(values, axis, pairs(lax.axis_size(axis), first))  9.7 us
    ppermute x1, waiting for transfers between devices, on_device(): lax.ppermute(one, 'sy', [(i, i ^ bit) for i in range(n_y)])  3.99 us
    pallas_call x1, Pallas kernels, own_begin(): pl.pallas_call(lambda *refs: own_begin_kernel(cut, *refs), out_shape=tupl...  3.14 us
    pallas_call x1, Pallas kernels, own_end(): pl.pallas_call(lambda *refs: own_end_kernel(cut, *refs), out_shape=jax.Sh...  2.98 us
    pallas_call x1, Pallas kernels, edges(): pl.pallas_call(edge_kernel, out_shape=(face(ny), face(ny - 2), face(2), f...  2.39 us
    unnamed x6, local copies, waits for them, and re-layouts  1.07 us
    pallas_call x1, Pallas kernels, across_y(): pl.pallas_call(lambda *refs: across_y_kernel(masks, *refs), out_shape=(ja...  0.99 us
  transfers between devices with their start and end apart: 6, of which 2 were waited for; matrix products, arithmetic and copies ran while one was open for 0% of the time, Pallas kernels for 19%

profile of v6, /device:TPU:12, one launch (start us, length us, event | category | flops | bytes accessed | tf_op | source)
XLA Modules:
  0.0 38.6 jit_solution(11424739405944534413)
XLA Ops:
  0.6 0.0 copy-start
  1.4 0.0 copy-start.1
  1.4 1.1 %copy-done.1 = f32[8,32,128]{2,1,0:T(8,128)S(1)} copy-done((f32[8,32,128]{2,1,0:T(8,128)S(1)}, f32[8,32,128]{2,1,0:T(8,128)}, u32[]{:S(2)}) %copy-start.1) | copy-done | bytes 131096
  2.5 0.0 copy-start.2
  2.5 2.4 %edges.1 = (bf16[32,64,128]{2,1,0:T(8,128)(2,1)S(1)}, bf16[30,64,128]{2,1,0:T(8,128)(2,1)S(1)}, bf16[2,64,128]{2,1,0:T(8,128)(2,1)S(1)}, bf16[8,64,128]{2,1,0:T(8,128)(2,1)S(1)}, bf16[8,64,128]{2,1,0:T(8,128)(2,1)S(1)}) custom-call(s32[1,1]{1,0:T(1,128)S(6)} %copy.8.refs_0_.cnt, bf16[64,8,32,128]{3,2,1,0:T(8,128)(2,1)} %v.1, f32[8,32,128]{2,1,0:T(8,128)S(1)} %copy-done.1), custom_call_target="tpu_custom_call" | custom-call | flops 1000000 | bytes 4000000 | tf_op jit(solution)/shard_map/edges/pallas_call | solution.py:95
  4.9 0.1 collective-permute-start
  5.0 3.4 %collective-permute-start.1 = (bf16[30,64,128]{2,1,0:T(8,128)(2,1)S(1)}, bf16[30,64,128]{2,1,0:T(8,128)(2,1)S(1)}, u32[]{:S(2)}, u32[]{:S(2)}) collective-permute-start(bf16[30,64,128]{2,1,0:T(8,128)(2,1)S(1)} %get-tuple-element.27.fxb), channel_id=1, source_target_pairs={{4,8},{8,4},{12,16},{16,12},{20,24},{24,20},{5,9},{9,5},{13,17},{1... | collective-permute-start | bytes 1474568 | tf_op jit(solution)/shard_map/ppermute | solution.py:413
  8.4 3.0 %collective-permute-start.2 = (bf16[2,64,128]{2,1,0:T(8,128)(2,1)S(1)}, bf16[2,64,128]{2,1,0:T(8,128)(2,1)S(1)}, u32[]{:S(2)}, u32[]{:S(2)}) collective-permute-start(bf16[2,64,128]{2,1,0:T(8,128)(2,1)S(1)} %get-tuple-element.28.fxc), channel_id=1, source_target_pairs={{4,8},{8,4},{12,16},{16,12},{20,24},{24,20},{5,9},{9,5},{13,17},{1... | collective-permute-start | bytes 98312 | tf_op jit(solution)/shard_map/ppermute | solution.py:413
  11.5 0.6 %smooth.1 = (bf16[32,64,128]{2,1,0:T(8,128)(2,1)S(1)}, bf16[30,64,128]{2,1,0:T(8,128)(2,1)S(1)}, bf16[2,64,128]{2,1,0:T(8,128)(2,1)S(1)}, bf16[8,64,128]{2,1,0:T...) custom-call(bf16[32,64,128]{2,1,0:T(8,128)(2,1)S(1)} %get-tuple-element.26.fxa, ...), custom_call_target="tpu_custom_call" | custom-call | flops 100000000 | bytes 2000000 | tf_op jit(solution)/shard_map/smooth/pallas_call | solution.py:196
  12.0 9.7 %collective-permute-done.2.rxc = bf16[2,64,128]{2,1,0:T(8,128)(2,1)S(1)} collective-permute-done((bf16[2,64,128]{2,1,0:T(8,128)(2,1)S(1)}, bf16[2,64,128]{2,1,0:T(8,128)(2,1)S(1)}, u32[]{:S(2)}, u32[]{:S(2)}) %collective-permute-start.2) | collective-permute-done | bytes 32800 | tf_op jit(solution)/shard_map/ppermute | solution.py:413
  21.7 0.0 collective-permute-done.rxa
  21.7 0.1 pack.1
  21.8 0.0 collective-permute-start.3
  21.8 5.0 %collective-permute-start.4 = (bf16[11,64,128]{2,1,0:T(8,128)(2,1)S(1)}, bf16[11,64,128]{2,1,0:T(8,128)(2,1)S(1)}, u32[]{:S(2)}, u32[]{:S(2)}) collective-permute-start(bf16[11,64,128]{2,1,0:T(8,128)(2,1)S(1)} %get-tuple-element.38), channel_id=1, source_target_pairs={{1,2},{2,1},{5,6},{6,5},{9,10},{10,9},{13,14},{14,13},{17,18},{18,... | collective-permute-start | bytes 540680 | tf_op jit(solution)/shard_map/ppermute | solution.py:413
  26.9 0.0 copy-done
  26.9 0.0 copy-done.2
  26.9 3.1 %own_begin.1 = (bf16[32,64,128]{2,1,0:T(8,128)(2,1)S(1)}, f32[64,64]{1,0:T(8,128)S(1)}, f32[64,64]{1,0:T(8,128)S(1)}) custom-call(bf16[64,8,32,128]{3,2,1,0:T(8,128)(2,1)S(1)} %copy-done, f32[8,32,128]{2,1,0:T(8,128)S(1)} %copy-done.1, f32[8,32,128]{2,1,0:T(8,128)S(1)} %copy-done.2), custom_call_target="tpu_custom_call" | custom-call | flops 1000000000 | bytes 5000000 | tf_op jit(solution)/shard_map/own_begin/pallas_call | solution.py:286
  30.0 3.0 %own_end.1 = f32[64,64]{1,0:T(8,128)} custom-call(s32[1,1]{1,0:T(1,128)S(6)} %copy.8.refs_0_.cnt, bf16[64,8,32,128]{3,2,1,0:T(8,128)(2,1)S(1)} %copy-done, f32[8,32,128]{2,1,0:T(8,128)S(1)} %copy-done.1, f32[8,32,128]{2,1,0:T(8,128)S(1)} %copy-done.2, bf16[32,64,128]{2,1,0:T(8,128)(2,1)S(1)} %get-tuple-element.23.refs_4_, ...), custom_call_target="tpu_custom_call" | custom-call | flops 1000000000 | bytes 5000000 | tf_op jit(solution)/shard_map/own_end/pallas_call | solution.py:300
  33.0 0.0 collective-permute-done.3.rya.refs_4_
  33.0 0.1 two_counts.1.refs_6_
  33.1 0.0 collective-permute-start.5
  33.1 0.0 collective-permute-done.1.rxb
  33.1 0.5 %across_x.1.refs_0_ = f32[64,128]{1,0:T(8,128)S(1)} custom-call(bf16[32,64,128]{2,1,0:T(8,128)(2,1)S(1)} %get-tuple-element.31.wxa, bf16[30,64,128]{2,1,0:T(8,128)(2,1)S(1)} %get-tuple-element.32.wxb, bf16[2,64,128]{2,1,0:T(8,128)(2,1)S(1)} %get-tuple-element.33.wxe, bf16[32,64,128]{2,1,0:T(8,128)(2,1)S(1)} %collective-permute-done.rxa, ...), custom_call_target="tpu_custom_call" | custom-call | flops 100000000 | bytes 2000000 | tf_op jit(solution)/shard_map/across_x/pallas_call | solution.py:390
  33.6 0.0 collective-permute-done.4.refs_5_
  33.6 4.0 %collective-permute-done.5.refs_7_ = s32[8,128]{1,0:T(8,128)S(1)} collective-permute-done((s32[8,128]{1,0:T(8,128)S(1)}, s32[8,128]{1,0:T(8,128)S(1)}, u32[]{:S(2)}, u32[]{:S(2)}) %collective-permute-start.5) | collective-permute-done | bytes 4128 | tf_op jit(solution)/shard_map/ppermute | solution.py:431
  37.6 1.0 %across_y.1 = (f32[64,256]{1,0:T(8,128)}, f32[64,256]{1,0:T(8,128)}, s32[1,1]{1,0:T(1,128)}) custom-call(f32[64,128]{1,0:T(8,128)S(1)} %across_x.1.refs_0_, bf16[8,64,128]{2,1,0:T(8,128)(2,1)S(1)} %get-tuple-element.34.refs_1_, bf16[8,64,128]{2,1,0:T(8,128)(2,1)S(1)} %get-tuple-element.35.refs_2_, bf16[4,64,128]{2,1,0:T(8,128)(2,1)S(1)} %get-tuple-element.36.refs_3_, ...), custom_call_target="tpu_custom_call" | custom-call | flops 10000000 | bytes 1000000 | tf_op jit(solution)/shard_map/across_y/pallas_call | solution.py:363
Async XLA Ops:
  0.6 26.2 %copy-start = (bf16[64,8,32,128]{3,2,1,0:T(8,128)(2,1)S(1)}, bf16[64,8,32,128]{3,2,1,0:T(8,128)(2,1)}, u32[]{:S(2)}) copy-start(bf16[64,8,32,128]{3,2,1,0:T(8,128)(2,1)} %v.1) | copy-start | bytes 12582916
  1.4 1.1 %copy-start.1 = (f32[8,32,128]{2,1,0:T(8,128)S(1)}, f32[8,32,128]{2,1,0:T(8,128)}, u32[]{:S(2)}) copy-start(f32[8,32,128]{2,1,0:T(8,128)} %s_any.1) | copy-start | bytes 393220
  2.5 24.4 %copy-start.2 = (f32[8,32,128]{2,1,0:T(8,128)S(1)}, f32[8,32,128]{2,1,0:T(8,128)}, u32[]{:S(2)}) copy-start(f32[8,32,128]{2,1,0:T(8,128)} %refs_3_.1) | copy-start | bytes 393220
  4.9 16.8 %collective-permute-start = (bf16[32,64,128]{2,1,0:T(8,128)(2,1)S(1)}, bf16[32,64,128]{2,1,0:T(8,128)(2,1)S(1)}, u32[]{:S(2)}, u32[]{:S(2)}) collective-permute-start(bf16[32,64,128]{2,1,0:T(8,128)(2,1)S(1)} %get-tuple-element.26.fxa), channel_id=1, source_target_pairs={{0,4},{4,0},{8,12},{12,8},{16,20},{20,16},{24,28},{28,24},{1,5},{5... | collective-permute-start | bytes 1572872 | tf_op jit(solution)/shard_map/ppermute | solution.py:413
  5.0 28.1 %collective-permute-start.1 = (bf16[30,64,128]{2,1,0:T(8,128)(2,1)S(1)}, bf16[30,64,128]{2,1,0:T(8,128)(2,1)S(1)}, u32[]{:S(2)}, u32[]{:S(2)}) collective-permute-start(bf16[30,64,128]{2,1,0:T(8,128)(2,1)S(1)} %get-tuple-element.27.fxb), channel_id=1, source_target_pairs={{4,8},{8,4},{12,16},{16,12},{20,24},{24,20},{5,9},{9,5},{13,17},{1... | collective-permute-start | bytes 1474568 | tf_op jit(solution)/shard_map/ppermute | solution.py:413
  8.4 13.3 %collective-permute-start.2 = (bf16[2,64,128]{2,1,0:T(8,128)(2,1)S(1)}, bf16[2,64,128]{2,1,0:T(8,128)(2,1)S(1)}, u32[]{:S(2)}, u32[]{:S(2)}) collective-permute-start(bf16[2,64,128]{2,1,0:T(8,128)(2,1)S(1)} %get-tuple-element.28.fxc), channel_id=1, source_target_pairs={{4,8},{8,4},{12,16},{16,12},{20,24},{24,20},{5,9},{9,5},{13,17},{1... | collective-permute-start | bytes 98312 | tf_op jit(solution)/shard_map/ppermute | solution.py:413
  21.8 11.2 %collective-permute-start.3 = (bf16[11,64,128]{2,1,0:T(8,128)(2,1)S(1)}, bf16[11,64,128]{2,1,0:T(8,128)(2,1)S(1)}, u32[]{:S(2)}, u32[]{:S(2)}) collective-permute-start(bf16[11,64,128]{2,1,0:T(8,128)(2,1)S(1)} %get-tuple-element.37), channel_id=1, source_target_pairs={{0,1},{1,0},{2,3},{3,2},{4,5},{5,4},{6,7},{7,6},{8,9},{9,8},{10,11... | collective-permute-start | bytes 540680 | tf_op jit(solution)/shard_map/ppermute | solution.py:413
  21.8 11.8 %collective-permute-start.4 = (bf16[11,64,128]{2,1,0:T(8,128)(2,1)S(1)}, bf16[11,64,128]{2,1,0:T(8,128)(2,1)S(1)}, u32[]{:S(2)}, u32[]{:S(2)}) collective-permute-start(bf16[11,64,128]{2,1,0:T(8,128)(2,1)S(1)} %get-tuple-element.38), channel_id=1, source_target_pairs={{1,2},{2,1},{5,6},{6,5},{9,10},{10,9},{13,14},{14,13},{17,18},{18,... | collective-permute-start | bytes 540680 | tf_op jit(solution)/shard_map/ppermute | solution.py:413
  33.1 4.5 %collective-permute-start.5 = (s32[8,128]{1,0:T(8,128)S(1)}, s32[8,128]{1,0:T(8,128)S(1)}, u32[]{:S(2)}, u32[]{:S(2)}) collective-permute-start(s32[8,128]{1,0:T(8,128)S(1)} %two_counts.1.refs_6_), channel_id=1, source_target_pairs={{0,2},{1,3},{2,0},{3,1},{4,6},{5,7},{6,4},{7,5},{8,10},{9,11},{10,... | collective-permute-start | bytes 12296 | tf_op jit(solution)/shard_map/ppermute | solution.py:431
